TPU v7x, 32 devices: a whole 2x2x4 slice. The times are simulated.
32 devices in a mesh: tm: 8 (over y, x, core), space: 4 (over z).
Axes of the slice: x: 2, y: 2, z: 4, core: 2. Of those that a mesh axis runs over, the one named last changes fastest.
Arguments:
- initial_state: float32 [1024, 1024], P('space'), may hold values from -6 to 6
- guess_coarse: float32 [8, 1024, 1024], P('tm', 'space'), may hold values from -6 to 6
- force_fine: float32 [8, 1024, 1024], P('tm', 'space'), may hold values from -6 to 6
- force_coarse: float32 [8, 1024, 1024], P('tm', 'space'), may hold values from -6 to 6
- eigen_basis: float32 [1024, 1024], replicated, may hold values from -1 to 1, as said below
- eigen_rates: float32 [1024], replicated, may hold values from 0.02 to 4
- carried_correction: float32 [1024, 1024], replicated, may hold values from -6 to 6
Outputs:
- fine_states: float32 [8, 1024, 1024], P('tm', 'space')
- coarse_states: float32 [8, 1024, 1024], P('tm', 'space')
Inputs may be any that keep to these rules, and one draw needn't show every extreme that they name: `eigen_basis`: an orthogonal matrix: its transpose is its inverse up to float32 rounding.
All inputs are finite; a program needn't handle non-finite values.
Results may differ from a plain program's by a relative error of at most 0.00013.
Values sent between devices are 32-bit elements; how exact they have to be, the bound alone decides.
No kernel may reach another device: no remote copies, remote signals or barrier semaphores. Data moves between devices by JAX's collectives and lax.ppermute only.
A program may use at most 128 MiB of HBM per device.

v0:
```python
import jax
import jax.numpy as jnp
from jax import lax
from jax.experimental import pallas as pl
from jax.sharding import PartitionSpec as P


both = ("tm", "space")


class Plan:
    def __init__(self, groups, blocks):
        self.groups, self.blocks, self.rounds = groups, blocks, blocks // 2
        self.low = blocks // 2 - 1

    def flat(self, t, s):
        return t * self.blocks + s

    def home(self, g, h):
        return self.flat(2 * (g // 2) + h, self.low + g % 2)

    def inward(self, r, shift):
        return [
            (self.flat(g, b), self.home(g - shift, b // self.rounds))
            for g in range(shift, self.groups)
            for b in range(self.blocks)
            if b % self.rounds == r
        ]

    def outward(self, r, shift, chains):
        return [
            (self.home(g, h), self.flat(g + shift, h * self.rounds + r))
            for g in chains
            for h in range(2)
        ]

    def partners(self):
        return [(t, t ^ 1) for t in range(self.groups)]

    def rings(self):
        used = [[self.home(g, h) for g in range(self.groups)] for h in range(2)]
        idle = [s for s in range(self.blocks) if s not in (self.low, self.low + 1)]
        return used + [[self.flat(t, s) for t in range(self.groups)] for s in idle]


def parts(x):
    high = lax.reduce_precision(x, 8, 7)
    return high, lax.reduce_precision(x - high, 8, 7)


def operand(x, axis):
    high, low = parts(x)
    return jnp.concatenate([high, low, high], axis).astype(jnp.bfloat16)


def weight(x, axis):
    high, low = parts(x)
    return jnp.concatenate([high, high, low], axis).astype(jnp.bfloat16)


def dot(left, right):
    return jnp.dot(left, right, preferred_element_type=jnp.float32)


def reaction(field):
    return field + 0.5 * jnp.tanh(field)


def scan_kernel(terms, decay, carried, out):
    state = decay[...] * carried[...]
    out[0] = state
    for k in range(1, out.shape[0]):
        state = decay[...] * state + terms[k - 1]
        out[k] = state


def scan_along(terms, decay, carried):
    chains, rows, columns = terms.shape
    step = min(rows, 32)
    deep = pl.BlockSpec((chains, step, columns), lambda i: (0, i, 0))
    flat = pl.BlockSpec((step, columns), lambda i: (i, 0))
    return pl.pallas_call(
        scan_kernel,
        grid=(rows // step,),
        in_specs=[deep, flat, flat],
        out_specs=deep,
        out_shape=jax.ShapeDtypeStruct(terms.shape, terms.dtype),
        name="scan_along",
    )(terms, decay, carried)


def on_device(
    initial_state,
    guess_coarse,
    force_fine,
    force_coarse,
    eigen_basis,
    eigen_rates,
    carried_correction,
):
    groups, blocks = lax.axis_size("tm"), lax.axis_size("space")
    plan = Plan(groups, blocks)
    t, s = lax.axis_index("tm"), lax.axis_index("space")
    grid = eigen_basis.shape[0]
    half = grid // 2
    part = grid // groups
    block = initial_state.shape[0]
    h = t % 2
    chain = 2 * (t // 2) + jnp.clip(s - plan.low, 0, 1)
    mine, other = h * half, (1 - h) * half

    rows_mine = lax.dynamic_slice_in_dim(eigen_basis, mine, half, 0)
    rows_other = lax.dynamic_slice_in_dim(eigen_basis, other, half, 0)
    cols_mine = lax.dynamic_slice_in_dim(eigen_basis, mine, half, 1)
    cols_other = lax.dynamic_slice_in_dim(eigen_basis, other, half, 1)
    right_mine, right_other = weight(cols_mine, 0), weight(cols_other, 0)
    down_mine, down_other = weight(rows_mine.T, 1), weight(rows_other.T, 1)
    up_mine, up_other = weight(rows_mine, 1), weight(rows_other, 1)
    back_mine, back_other = weight(cols_mine.T, 0), weight(cols_other.T, 0)
    rates_mine = lax.dynamic_slice_in_dim(eigen_rates, mine, half, 0)
    sums = eigen_rates[:, None] + rates_mine[None, :]
    fine_decay = 1.0 / (1.0 + sums)
    coarse_decay = 1.0 / (1.0 + 2.0 * sums)
    own_part = chain * part
    rates_part = lax.dynamic_slice_in_dim(eigen_rates, own_part, part, 0)
    part_decay = 1.0 / (1.0 + 2.0 * (rates_part[:, None] + rates_mine[None, :]))
    carried_mine = lax.dynamic_slice_in_dim(carried_correction, mine, half, 1)
    carried_part = lax.dynamic_slice_in_dim(carried_mine, own_part, part, 0)

    def swap(x):
        return lax.ppermute(x, "tm", plan.partners())

    def inward(pieces, shift):
        out = []
        for r in range(plan.rounds):
            out += [lax.ppermute(x, both, plan.inward(r, shift)) for x in pieces]
        return out

    def outward(pieces, shift, chains):
        pieces = [
            lax.ppermute(x, both, plan.outward(r, shift, chains))
            for r, x in enumerate(pieces)
        ]
        out = pieces[0]
        for r in range(1, plan.rounds):
            out = jnp.where(s % plan.rounds == r, pieces[r], out)
        return out

    def to_eigen(pieces):
        field = operand(jnp.concatenate(pieces, 0), 1)
        arrived = swap(dot(field, right_other))
        kept = dot(down_mine, operand(dot(field, right_mine), 0))
        return kept + dot(down_other, operand(arrived, 0))

    def from_eigen(coeffs):
        coeffs = operand(coeffs, 0)
        arrived = operand(swap(dot(up_other, coeffs)), 1)
        kept = operand(dot(up_mine, coeffs), 1)
        return [
            dot(kept[i : i + block], back_mine) + dot(arrived[i : i + block], back_other)
            for i in range(0, half, block)
        ]

    def forced(fields, forces):
        return [reaction(x) + f for x, f in zip(fields, forces)]

    source_fine, source_coarse = force_fine[0], force_coarse[0]
    cut = block // 2
    started = []
    for c in range(2):
        rows = slice(c * cut, (c + 1) * cut)
        along = [(g, g + 1) for g in range(groups - 1)]
        before = lax.ppermute(guess_coarse[0, rows], "tm", along)
        if started:
            before, started[-1] = lax.optimization_barrier((before, started[-1]))
        before = jnp.where(t == 0, initial_state[rows], before)
        started.append(reaction(before) + source_fine[rows])
    entered = [inward([x], 0) for x in started]
    start = [x for pair in zip(*entered) for x in pair]
    coarse_now = inward([source_coarse], 0)
    fine_next = inward([source_fine], 1)
    coarse_next = inward([source_coarse], 1)

    relaxed_fine = from_eigen(fine_decay * to_eigen(start))
    coeffs = fine_decay * to_eigen(forced(relaxed_fine, coarse_now))
    relaxed_coarse = from_eigen(coeffs)
    second = to_eigen(forced(relaxed_coarse, fine_next))
    second = from_eigen(fine_decay * second)
    ahead = fine_decay * to_eigen(forced(second, coarse_next))
    term = jnp.where(chain == 0, ahead, ahead - coarse_decay * coeffs)

    rings = plan.rings()
    spread = lax.all_to_all(term, both, 0, 0, axis_index_groups=rings, tiled=True)
    states = scan_along(spread.reshape(groups, part, half), part_decay, carried_part)
    states = states.reshape(grid, half)
    states = lax.all_to_all(states, both, 0, 0, axis_index_groups=rings, tiled=True)
    total = jnp.where(chain == 0, coarse_decay * carried_mine + coeffs, states)

    coarse_new = from_eigen(total)
    coarse_out = outward(coarse_new, 0, range(groups))
    fine_new = to_eigen(forced(coarse_new, fine_next))
    fine_new = from_eigen(fine_decay * fine_new)
    fine_out = outward(fine_new, 1, range(groups - 1))
    first_out = outward(relaxed_fine, 0, range(1))
    fine_out = jnp.where(t == 0, first_out, fine_out)
    return (fine_out[None], coarse_out[None])


def solution(mesh):
    placed = (
        P("space", None),
        P("tm", "space", None),
        P("tm", "space", None),
        P("tm", "space", None),
        P(),
        P(),
        P(),
    )
    return jax.shard_map(
        on_device,
        mesh=mesh,
        in_specs=placed,
        out_specs=(P("tm", "space", None), P("tm", "space", None)),
        check_vma=False,
    )
```

profile of v0, /device:TPU:25, one launch (start us, length us, event | category | flops | bytes accessed | tf_op | source)
XLA Modules:
  0.0 367.4 jit_solution(3217369319813351181)
XLA Ops:
  0.6 1.3 slice_bitcast_fusion
  1.9 3.7 %collective-permute-start.1 = (f32[128,1024]{1,0:T(8,128)S(1)}, f32[128,1024]{1,0:T(8,128)S(1)}, u32[]{:S(2)}, u32[]{:S(2)}) collective-permute-start(f32[128,1024]{1,0:T(8,128)S(1)} %get-tuple-element.82), channel_id=1, source_target_pairs={{0,4},{4,8},{8,12},{12,16},{16,20},{20,24},{24,28},{1,5},{5,9},{9,... | collective-permute-start | bytes 1572872 | tf_op jit(solution)/shard_map/ppermute | solution.py:173
  5.6 1.9 collective-permute-start
  7.5 1.7 collective-permute-start.10
  9.2 3.0 reduce-precision_convert_fusion.12
  12.5 4.8 %collective-permute-done = f32[128,1024]{1,0:T(8,128)S(1)} collective-permute-done((f32[128,1024]{1,0:T(8,128)S(1)}, f32[128,1024]{1,0:T(8,128)S(1)}, u32[]{:S(2)}, u32[]{:S(2)}) %collective-permute-start) | collective-permute-done | bytes 524320 | tf_op jit(solution)/shard_map/ppermute | solution.py:173
  18.0 5.5 %collective-permute-start.4 = (f32[128,1024]{1,0:T(8,128)S(1)}, f32[128,1024]{1,0:T(8,128)S(1)}, u32[]{:S(2)}, u32[]{:S(2)}) collective-permute-start(f32[128,1024]{1,0:T(8,128)S(1)} %bitcast_add_fusion.1), channel_id=1, source_target_pairs={{1,1},{3,5},{5,2},{7,6},{9,9},{11,13},{13,10},{15,14},{17,17},{19,... | collective-permute-start | bytes 1572872 | tf_op jit(solution)/shard_map/ppermute | solution.py:136
  25.4 1.7 collective-permute-start.5
  28.1 1.8 collective-permute-start.11
  30.0 5.2 %collective-permute-done.4 = f32[128,1024]{1,0:T(8,128)S(1)} collective-permute-done((f32[128,1024]{1,0:T(8,128)S(1)}, f32[128,1024]{1,0:T(8,128)S(1)}, u32[]{:S(2)}, u32[]{:S(2)}) %collective-permute-start.4) | collective-permute-done | bytes 524320 | tf_op jit(solution)/shard_map/ppermute | solution.py:136
  35.2 11.2 %collective-permute-done.5 = f32[128,1024]{1,0:T(8,128)S(1)} collective-permute-done((f32[128,1024]{1,0:T(8,128)S(1)}, f32[128,1024]{1,0:T(8,128)S(1)}, u32[]{:S(2)}, u32[]{:S(2)}) %collective-permute-start.5) | collective-permute-done | bytes 524320 | tf_op jit(solution)/shard_map/ppermute | solution.py:136
  46.9 1.8 fusion.57
  49.7 1.8 fusion.130
  51.5 1.8 fusion.59
  53.5 2.1 fusion.16
  55.6 1.8 fusion.55
  57.9 1.8 fusion.134
  62.3 3.3 add_add_fusion.8
  66.6 2.1 add_add_fusion.7
  69.1 1.8 fusion.53
  71.7 13.4 %collective-permute-start.15 = (f32[256,1024]{1,0:T(8,128)S(1)}, f32[256,1024]{1,0:T(8,128)S(1)}, u32[]{:S(2)}, u32[]{:S(2)}) collective-permute-start(f32[256,1024]{1,0:T(8,128)S(1)} %bitcast.32), channel_id=1, source_target_pairs={{5,1},{7,5},{9,2},{11,6},{13,9},{15,13},{17,10},{19,14},{21,17},{2... | collective-permute-start | bytes 3145736 | tf_op jit(solution)/shard_map/ppermute | solution.py:136
  85.2 1.8 fusion.138
  87.0 1.8 fusion.71
  89.0 2.1 fusion.26
  91.1 1.8 fusion.142
  93.0 1.8 fusion.51
  100.4 2.2 fusion.49
  103.5 13.6 %collective-permute-start.19 = (f32[256,1024]{1,0:T(8,128)S(1)}, f32[256,1024]{1,0:T(8,128)S(1)}, u32[]{:S(2)}, u32[]{:S(2)}) collective-permute-start(f32[256,1024]{1,0:T(8,128)S(1)} %bitcast.36), channel_id=1, source_target_pairs={{5,1},{7,5},{9,2},{11,6},{13,9},{15,13},{17,10},{19,14},{21,17},{2... | collective-permute-start | bytes 3145736 | tf_op jit(solution)/shard_map/ppermute | solution.py:136
  117.2 1.8 fusion.146
  119.0 1.8 fusion.83
  121.0 2.1 fusion.30
  123.1 1.8 fusion.150
  125.0 1.8 fusion.47
  132.5 3.0 fusion.45
  135.6 4.4 %fusion.154 = (bf16[512,512]{1,0:T(8,128)(2,1)S(1)}, bf16[512,512]{1,0:T(8,128)(2,1)S(1)}) fusion(bf16[1024,512]{1,0:T(8,128)(2,1)S(1)} %get-tuple-element.21, bf16[1024,512]{1,0:T(8,128)(2,1)} %copy-done.6, bf16[512,1024]{1,0:T(8,128)(2,1)} %copy-done.41, bf16[512,1024]{1,0:T(8,128)(2,1)} %copy-done.40), kind=kOutput, calls=%fused_computation.270 | convolution fusion | flops 1630797824 | bytes 5242880 | tf_op jit(solution)/shard_map/dot_general | solution.py:62
  140.1 1.8 fusion.95
  141.9 1.4 fusion.156
  143.3 3.7 subtract_select_fusion
  147.0 39.5 %all-to-all-start = ((f32[8,128,512]{2,1,0:T(8,128)}), f32[8,128,512]{2,1,0:T(8,128)S(1)}, u32[]{:S(2)}, u32[]{:S(2)}) async-start(f32[8,128,512]{2,1,0:T(8,128)} %bitcast.30), calls=%async_computation | async-start | bytes 4194304 | tf_op jit(solution)/shard_map/all_to_all | solution.py:193
  186.5 1.8 dynamic_slice.31.carried
  189.1 20.5 %all-to-all-done.terms = f32[8,128,512]{2,1,0:T(8,128)S(1)} async-done(((f32[8,128,512]{2,1,0:T(8,128)}), f32[8,128,512]{2,1,0:T(8,128)S(1)}, u32[]{:S(2)}, u32[]{:S(2)}) %all-to-all-start) | async-done | bytes 2097184 | tf_op jit(solution)/shard_map/all_to_all | solution.py:193
  209.6 1.4 copy-done.1
  211.0 3.8 %scan_along.1 = f32[8,128,512]{2,1,0:T(8,128)} custom-call(f32[8,128,512]{2,1,0:T(8,128)} %copy-done.1, f32[128,512]{1,0:T(8,128)} %add_divide_fusion.decay, f32[128,512]{1,0:T(8,128)} %dynamic_slice.31.carried), custom_call_target="tpu_custom_call" | custom-call | tf_op jit(solution)/shard_map/scan_along/pallas_call | solution.py:82
  214.8 32.4 %all_to_all.18 = f32[8,128,512]{2,1,0:T(8,128)S(1)} all-to-all(f32[8,128,512]{2,1,0:T(8,128)} %scan_along.1), channel_id=1, replica_groups={{1,2,9,10,17,18,25,26},{5,6,13,14,21,22,29,30},{0,4,8,12,16,20,24,28},{..., dimensions={0} | all-to-all | bytes 4194304 | tf_op jit(solution)/shard_map/all_to_all | solution.py:196
  247.2 2.6 fusion.34
  251.4 1.8 fusion.158
  253.2 1.8 fusion.43
  255.0 1.3 collective-permute-start.21
  261.6 2.1 add_add_fusion.1
  265.3 1.8 fusion.41
  267.1 1.6 collective-permute-start.9
  268.8 1.7 collective-permute-start.8
  271.2 1.6 collective-permute-start.26
  272.9 1.8 fusion.162
  274.7 1.8 fusion.107
  276.7 2.1 fusion.38
  278.8 1.9 fusion.166
  280.7 1.8 fusion.39
  285.5 2.0 convolution_add_fusion
  288.2 2.0 convolution_add_fusion.1
  290.3 1.3 collective-permute-start.24
  291.6 29.5 %collective-permute-done.26 = f32[256,1024]{1,0:T(8,128)S(1)} collective-permute-done((f32[256,1024]{1,0:T(8,128)}, f32[256,1024]{1,0:T(8,128)S(1)}, u32[]{:S(2)}, u32[]{:S(2)}) %collective-permute-start.26) | collective-permute-done | bytes 1048608 | tf_op jit(solution)/shard_map/ppermute | solution.py:141
  322.2 42.0 %collective-permute-done.24 = f32[256,1024]{1,0:T(8,128)} collective-permute-done((f32[256,1024]{1,0:T(8,128)}, f32[256,1024]{1,0:T(8,128)}, u32[]{:S(2)}, u32[]{:S(2)}) %collective-permute-start.24) | collective-permute-done | bytes 1048608 | tf_op jit(solution)/shard_map/ppermute | solution.py:141
  364.2 2.9 select_bitcast_fusion.1
  (186 shorter events, 38.1 us)
Async XLA Ops:
  1.9 10.4 %collective-permute-start.1 = (f32[128,1024]{1,0:T(8,128)S(1)}, f32[128,1024]{1,0:T(8,128)S(1)}, u32[]{:S(2)}, u32[]{:S(2)}) collective-permute-start(f32[128,1024]{1,0:T(8,128)S(1)} %get-tuple-element.82), channel_id=1, source_target_pairs={{0,4},{4,8},{8,12},{12,16},{16,20},{20,24},{24,28},{1,5},{5,9},{9,... | collective-permute-start | bytes 1572872 | tf_op jit(solution)/shard_map/ppermute | solution.py:173
  5.6 11.7 %collective-permute-start = (f32[128,1024]{1,0:T(8,128)S(1)}, f32[128,1024]{1,0:T(8,128)S(1)}, u32[]{:S(2)}, u32[]{:S(2)}) collective-permute-start(f32[128,1024]{1,0:T(8,128)S(1)} %get-tuple-element.83), channel_id=1, source_target_pairs={{0,4},{4,8},{8,12},{12,16},{16,20},{20,24},{24,28},{1,5},{5,9},{9,... | collective-permute-start | bytes 1572872 | tf_op jit(solution)/shard_map/ppermute | solution.py:173
  7.5 54.7 %collective-permute-start.10 = (f32[256,1024]{1,0:T(8,128)}, f32[256,1024]{1,0:T(8,128)}, u32[]{:S(2)}, u32[]{:S(2)}) collective-permute-start(f32[256,1024]{1,0:T(8,128)} %bitcast.33), channel_id=1, source_target_pairs={{0,1},{2,5},{4,2},{6,6},{8,9},{10,13},{12,10},{14,14},{16,17},{18,... | collective-permute-start | bytes 3145736 | tf_op jit(solution)/shard_map/ppermute | solution.py:136
  9.2 3.1 copy-start.4
  9.2 3.1 copy-start.5
  12.2 104.9 %copy-start.6 = (bf16[1024,512]{1,0:T(8,128)(2,1)}, bf16[1024,512]{1,0:T(8,128)(2,1)S(1)}, u32[]{:S(2)}) copy-start(bf16[1024,512]{1,0:T(8,128)(2,1)S(1)} %get-tuple-element.23) | copy-start | bytes 3145732
  12.2 120.2 %copy-start.32 = (bf16[1024,512]{1,0:T(8,128)(2,1)}, bf16[1024,512]{1,0:T(8,128)(2,1)S(1)}, u32[]{:S(2)}) copy-start(bf16[1024,512]{1,0:T(8,128)(2,1)S(1)} %get-tuple-element.20) | copy-start | bytes 3145732
  12.3 120.2 %copy-start.34 = (bf16[1024,512]{1,0:T(8,128)(2,1)}, bf16[1024,512]{1,0:T(8,128)(2,1)S(1)}, u32[]{:S(2)}) copy-start(bf16[1024,512]{1,0:T(8,128)(2,1)S(1)} %get-tuple-element.22) | copy-start | bytes 3145732
  12.3 12.1 %copy-start = (f32[1024,1024]{1,0:T(8,128)S(1)}, f32[1024,1024]{1,0:T(8,128)}, u32[]{:S(2)}) copy-start(f32[1024,1024]{1,0:T(8,128)} %param.11) | copy-start | bytes 12582916
  17.3 10.7 %collective-permute-start.2 = (f32[128,1024]{1,0:T(8,128)S(1)}, f32[128,1024]{1,0:T(8,128)S(1)}, u32[]{:S(2)}, u32[]{:S(2)}) collective-permute-start(f32[128,1024]{1,0:T(8,128)S(1)} %bitcast_add_fusion.1), channel_id=1, source_target_pairs={{0,1},{2,5},{4,2},{6,6},{8,9},{10,13},{12,10},{14,14},{16,17},{18,... | collective-permute-start | bytes 1572872 | tf_op jit(solution)/shard_map/ppermute | solution.py:136
  18.0 17.2 %collective-permute-start.4 = (f32[128,1024]{1,0:T(8,128)S(1)}, f32[128,1024]{1,0:T(8,128)S(1)}, u32[]{:S(2)}, u32[]{:S(2)}) collective-permute-start(f32[128,1024]{1,0:T(8,128)S(1)} %bitcast_add_fusion.1), channel_id=1, source_target_pairs={{1,1},{3,5},{5,2},{7,6},{9,9},{11,13},{13,10},{15,14},{17,17},{19,... | collective-permute-start | bytes 1572872 | tf_op jit(solution)/shard_map/ppermute | solution.py:136
  23.7 6.3 %collective-permute-start.3 = (f32[128,1024]{1,0:T(8,128)S(1)}, f32[128,1024]{1,0:T(8,128)S(1)}, u32[]{:S(2)}, u32[]{:S(2)}) collective-permute-start(f32[128,1024]{1,0:T(8,128)S(1)} %bitcast_add_fusion), channel_id=1, source_target_pairs={{0,1},{2,5},{4,2},{6,6},{8,9},{10,13},{12,10},{14,14},{16,17},{18,... | collective-permute-start | bytes 1572872 | tf_op jit(solution)/shard_map/ppermute | solution.py:136
  25.3 93.7 %copy-start.26 = (bf16[1024,512]{0,1:T(8,128)(2,1)}, bf16[1024,512]{0,1:T(8,128)(2,1)S(1)}, u32[]{:S(2)}) copy-start(bf16[1024,512]{0,1:T(8,128)(2,1)S(1)} %get-tuple-element.17) | copy-start | bytes 3145732
  25.3 93.7 %copy-start.29 = (bf16[1024,512]{0,1:T(8,128)(2,1)}, bf16[1024,512]{0,1:T(8,128)(2,1)S(1)}, u32[]{:S(2)}) copy-start(bf16[1024,512]{0,1:T(8,128)(2,1)S(1)} %get-tuple-element.18) | copy-start | bytes 3145732
  25.3 95.7 %copy-start.16 = (bf16[1024,512]{0,1:T(8,128)(2,1)}, bf16[1024,512]{0,1:T(8,128)(2,1)S(1)}, u32[]{:S(2)}) copy-start(bf16[1024,512]{0,1:T(8,128)(2,1)S(1)} %get-tuple-element.16) | copy-start | bytes 3145732
  25.3 95.7 %copy-start.19 = (bf16[1024,512]{0,1:T(8,128)(2,1)}, bf16[1024,512]{0,1:T(8,128)(2,1)S(1)}, u32[]{:S(2)}) copy-start(bf16[1024,512]{0,1:T(8,128)(2,1)S(1)} %get-tuple-element.19) | copy-start | bytes 3145732
  25.4 2.7 copy-start.43
  25.4 21.1 %collective-permute-start.5 = (f32[128,1024]{1,0:T(8,128)S(1)}, f32[128,1024]{1,0:T(8,128)S(1)}, u32[]{:S(2)}, u32[]{:S(2)}) collective-permute-start(f32[128,1024]{1,0:T(8,128)S(1)} %bitcast_add_fusion), channel_id=1, source_target_pairs={{1,1},{3,5},{5,2},{7,6},{9,9},{11,13},{13,10},{15,14},{17,17},{19,... | collective-permute-start | bytes 1572872 | tf_op jit(solution)/shard_map/ppermute | solution.py:136
  28.0 95.1 %copy-start.12 = (bf16[512,1024]{1,0:T(8,128)(2,1)}, bf16[512,1024]{1,0:T(8,128)(2,1)S(1)}, u32[]{:S(2)}) copy-start(bf16[512,1024]{1,0:T(8,128)(2,1)S(1)} %get-tuple-element.13) | copy-start | bytes 3145732
  28.0 95.1 %copy-start.14 = (bf16[512,1024]{1,0:T(8,128)(2,1)}, bf16[512,1024]{1,0:T(8,128)(2,1)S(1)}, u32[]{:S(2)}) copy-start(bf16[512,1024]{1,0:T(8,128)(2,1)S(1)} %get-tuple-element.15) | copy-start | bytes 3145732
  28.0 97.0 %copy-start.8 = (bf16[512,1024]{1,0:T(8,128)(2,1)}, bf16[512,1024]{1,0:T(8,128)(2,1)S(1)}, u32[]{:S(2)}) copy-start(bf16[512,1024]{1,0:T(8,128)(2,1)S(1)} %get-tuple-element.12) | copy-start | bytes 3145732
  28.0 97.0 %copy-start.10 = (bf16[512,1024]{1,0:T(8,128)(2,1)}, bf16[512,1024]{1,0:T(8,128)(2,1)S(1)}, u32[]{:S(2)}) copy-start(bf16[512,1024]{1,0:T(8,128)(2,1)S(1)} %get-tuple-element.14) | copy-start | bytes 3145732
  28.1 38.6 %collective-permute-start.11 = (f32[256,1024]{1,0:T(8,128)S(1)}, f32[256,1024]{1,0:T(8,128)S(1)}, u32[]{:S(2)}, u32[]{:S(2)}) collective-permute-start(f32[256,1024]{1,0:T(8,128)S(1)} %bitcast.34), channel_id=1, source_target_pairs={{1,1},{3,5},{5,2},{7,6},{9,9},{11,13},{13,10},{15,14},{17,17},{19,... | collective-permute-start | bytes 3145736 | tf_op jit(solution)/shard_map/ppermute | solution.py:136
  48.7 4.6 %collective-permute-start.6 = (f32[512,512]{1,0:T(8,128)S(1)}, f32[512,512]{1,0:T(8,128)S(1)}, u32[]{:S(2)}, u32[]{:S(2)}) collective-permute-start(f32[512,512]{1,0:T(8,128)S(1)} %fusion.57), channel_id=1, source_target_pairs={{0,4},{4,0},{8,12},{12,8},{16,20},{20,16},{24,28},{28,24},{1,5},{5... | collective-permute-start | bytes 3145736 | tf_op jit(solution)/shard_map/ppermute | solution.py:131
  49.6 78.5 %copy-start.36 = (bf16[512,1024]{0,1:T(8,128)(2,1)}, bf16[512,1024]{0,1:T(8,128)(2,1)S(1)}, u32[]{:S(2)}) copy-start(bf16[512,1024]{0,1:T(8,128)(2,1)S(1)} %get-tuple-element.9) | copy-start | bytes 3145732
  49.6 78.5 %copy-start.38 = (bf16[512,1024]{0,1:T(8,128)(2,1)}, bf16[512,1024]{0,1:T(8,128)(2,1)S(1)}, u32[]{:S(2)}) copy-start(bf16[512,1024]{0,1:T(8,128)(2,1)S(1)} %get-tuple-element.10) | copy-start | bytes 3145732
  49.6 81.3 %copy-start.22 = (bf16[512,1024]{0,1:T(8,128)(2,1)}, bf16[512,1024]{0,1:T(8,128)(2,1)S(1)}, u32[]{:S(2)}) copy-start(bf16[512,1024]{0,1:T(8,128)(2,1)S(1)} %get-tuple-element.8) | copy-start | bytes 3145732
  49.6 81.3 %copy-start.24 = (bf16[512,1024]{0,1:T(8,128)(2,1)}, bf16[512,1024]{0,1:T(8,128)(2,1)S(1)}, u32[]{:S(2)}) copy-start(bf16[512,1024]{0,1:T(8,128)(2,1)S(1)} %get-tuple-element.11) | copy-start | bytes 3145732
  57.4 4.6 %collective-permute-start.7 = (f32[512,512]{1,0:T(8,128)S(1)}, f32[512,512]{1,0:T(8,128)S(1)}, u32[]{:S(2)}, u32[]{:S(2)}) collective-permute-start(f32[512,512]{1,0:T(8,128)S(1)} %fusion.55), channel_id=1, source_target_pairs={{0,4},{4,0},{8,12},{12,8},{16,20},{20,16},{24,28},{28,24},{1,5},{5... | collective-permute-start | bytes 3145736 | tf_op jit(solution)/shard_map/ppermute | solution.py:131
  70.9 17.9 %collective-permute-start.12 = (f32[512,512]{1,0:T(8,128)S(1)}, f32[512,512]{1,0:T(8,128)S(1)}, u32[]{:S(2)}, u32[]{:S(2)}) collective-permute-start(f32[512,512]{1,0:T(8,128)S(1)} %fusion.53), channel_id=1, source_target_pairs={{0,4},{4,0},{8,12},{12,8},{16,20},{20,16},{24,28},{28,24},{1,5},{5... | collective-permute-start | bytes 3145736 | tf_op jit(solution)/shard_map/ppermute | solution.py:131
  71.0 26.8 %collective-permute-start.14 = (f32[256,1024]{1,0:T(8,128)S(1)}, f32[256,1024]{1,0:T(8,128)S(1)}, u32[]{:S(2)}, u32[]{:S(2)}) collective-permute-start(f32[256,1024]{1,0:T(8,128)S(1)} %bitcast.31), channel_id=1, source_target_pairs={{4,1},{6,5},{8,2},{10,6},{12,9},{14,13},{16,10},{18,14},{20,17},{2... | collective-permute-start | bytes 3145736 | tf_op jit(solution)/shard_map/ppermute | solution.py:136
  71.7 27.2 %collective-permute-start.15 = (f32[256,1024]{1,0:T(8,128)S(1)}, f32[256,1024]{1,0:T(8,128)S(1)}, u32[]{:S(2)}, u32[]{:S(2)}) collective-permute-start(f32[256,1024]{1,0:T(8,128)S(1)} %bitcast.32), channel_id=1, source_target_pairs={{5,1},{7,5},{9,2},{11,6},{13,9},{15,13},{17,10},{19,14},{21,17},{2... | collective-permute-start | bytes 3145736 | tf_op jit(solution)/shard_map/ppermute | solution.py:136
  91.1 52.2 %copy-start.2 = (f32[1024,512]{1,0:T(8,128)}, f32[1024,512]{1,0:T(8,128)S(1)}, u32[]{:S(2)}) copy-start(f32[1024,512]{1,0:T(8,128)S(1)} %get-tuple-element.88) | copy-start | bytes 6291460
  94.7 2.7 collective-permute-start.13
  102.6 18.2 %collective-permute-start.16 = (f32[512,512]{1,0:T(8,128)S(1)}, f32[512,512]{1,0:T(8,128)S(1)}, u32[]{:S(2)}, u32[]{:S(2)}) collective-permute-start(f32[512,512]{1,0:T(8,128)S(1)} %fusion.49), channel_id=1, source_target_pairs={{0,4},{4,0},{8,12},{12,8},{16,20},{20,16},{24,28},{28,24},{1,5},{5... | collective-permute-start | bytes 3145736 | tf_op jit(solution)/shard_map/ppermute | solution.py:131
  102.8 27.0 %collective-permute-start.18 = (f32[256,1024]{1,0:T(8,128)S(1)}, f32[256,1024]{1,0:T(8,128)S(1)}, u32[]{:S(2)}, u32[]{:S(2)}) collective-permute-start(f32[256,1024]{1,0:T(8,128)S(1)} %bitcast.35), channel_id=1, source_target_pairs={{4,1},{6,5},{8,2},{10,6},{12,9},{14,13},{16,10},{18,14},{20,17},{2... | collective-permute-start | bytes 3145736 | tf_op jit(solution)/shard_map/ppermute | solution.py:136
  103.5 27.3 %collective-permute-start.19 = (f32[256,1024]{1,0:T(8,128)S(1)}, f32[256,1024]{1,0:T(8,128)S(1)}, u32[]{:S(2)}, u32[]{:S(2)}) collective-permute-start(f32[256,1024]{1,0:T(8,128)S(1)} %bitcast.36), channel_id=1, source_target_pairs={{5,1},{7,5},{9,2},{11,6},{13,9},{15,13},{17,10},{19,14},{21,17},{2... | collective-permute-start | bytes 3145736 | tf_op jit(solution)/shard_map/ppermute | solution.py:136
  126.8 2.7 collective-permute-start.17
  132.4 3.0 copy-start.40
  132.5 3.0 copy-start.41
  135.4 6.4 %collective-permute-start.20 = (f32[512,512]{1,0:T(8,128)}, f32[512,512]{1,0:T(8,128)}, u32[]{:S(2)}, u32[]{:S(2)}) collective-permute-start(f32[512,512]{1,0:T(8,128)} %fusion.45), channel_id=1, source_target_pairs={{0,4},{4,0},{8,12},{12,8},{16,20},{20,16},{24,28},{28,24},{1,5},{5... | collective-permute-start | bytes 3145736 | tf_op jit(solution)/shard_map/ppermute | solution.py:131
  135.6 4.4 %copy-start.27 = (bf16[1024,512]{0,1:T(8,128)(2,1)S(1)}, bf16[1024,512]{0,1:T(8,128)(2,1)}, u32[]{:S(2)}) copy-start(bf16[1024,512]{0,1:T(8,128)(2,1)} %copy-done.26) | copy-start | bytes 3145732
  135.6 4.4 %copy-start.30 = (bf16[1024,512]{0,1:T(8,128)(2,1)S(1)}, bf16[1024,512]{0,1:T(8,128)(2,1)}, u32[]{:S(2)}) copy-start(bf16[1024,512]{0,1:T(8,128)(2,1)} %copy-done.29) | copy-start | bytes 3145732
  140.0 3.3 copy-start.17
  140.0 3.3 copy-start.20
  147.0 62.7 %all-to-all-start = ((f32[8,128,512]{2,1,0:T(8,128)}), f32[8,128,512]{2,1,0:T(8,128)S(1)}, u32[]{:S(2)}, u32[]{:S(2)}) async-start(f32[8,128,512]{2,1,0:T(8,128)} %bitcast.30), calls=%async_computation | async-start | bytes 4194304 | tf_op jit(solution)/shard_map/all_to_all | solution.py:193
  214.8 32.4 %copy-start.3 = (f32[1024,512]{1,0:T(8,128)S(1)}, f32[1024,512]{1,0:T(8,128)}, u32[]{:S(2)}) copy-start(f32[1024,512]{1,0:T(8,128)} %copy-done.2) | copy-start | bytes 6291460
  251.4 1.9 copy-start.11
  253.2 3.2 copy-start.37
  253.2 3.2 copy-start.39
  255.0 3.6 collective-permute-start.21
  265.3 7.6 %copy-start.7 = (bf16[1024,512]{1,0:T(8,128)(2,1)S(1)}, bf16[1024,512]{1,0:T(8,128)(2,1)}, u32[]{:S(2)}) copy-start(bf16[1024,512]{1,0:T(8,128)(2,1)} %copy-done.6) | copy-start | bytes 3145732
  267.1 9.5 %collective-permute-start.22 = (f32[512,512]{1,0:T(8,128)S(1)}, f32[512,512]{1,0:T(8,128)S(1)}, u32[]{:S(2)}, u32[]{:S(2)}) collective-permute-start(f32[512,512]{1,0:T(8,128)S(1)} %fusion.41), channel_id=1, source_target_pairs={{0,4},{4,0},{8,12},{12,8},{16,20},{20,16},{24,28},{28,24},{1,5},{5... | collective-permute-start | bytes 3145736 | tf_op jit(solution)/shard_map/ppermute | solution.py:131
  267.1 55.1 %collective-permute-start.9 = (f32[256,1024]{1,0:T(8,128)}, f32[256,1024]{1,0:T(8,128)}, u32[]{:S(2)}, u32[]{:S(2)}) collective-permute-start(f32[256,1024]{1,0:T(8,128)} %get-tuple-element.87), channel_id=1, source_target_pairs={{1,0},{5,2}} | collective-permute-start | bytes 3145736 | tf_op jit(solution)/shard_map/ppermute | solution.py:141
  268.8 53.4 %collective-permute-start.8 = (f32[256,1024]{1,0:T(8,128)}, f32[256,1024]{1,0:T(8,128)}, u32[]{:S(2)}, u32[]{:S(2)}) collective-permute-start(f32[256,1024]{1,0:T(8,128)} %get-tuple-element.85), channel_id=1, source_target_pairs={{1,1},{5,3}} | collective-permute-start | bytes 3145736 | tf_op jit(solution)/shard_map/ppermute | solution.py:141
  270.5 19.8 %collective-permute-start.27 = (f32[256,1024]{1,0:T(8,128)S(1)}, f32[256,1024]{1,0:T(8,128)S(1)}, u32[]{:S(2)}, u32[]{:S(2)}) collective-permute-start(f32[256,1024]{1,0:T(8,128)S(1)} %get-tuple-element.92), channel_id=1, source_target_pairs={{1,0},{5,2},{2,4},{6,6},{9,8},{13,10},{10,12},{14,14},{17,16},{21,... | collective-permute-start | bytes 3145736 | tf_op jit(solution)/shard_map/ppermute | solution.py:141
  271.2 3.5 copy-start.28
  271.2 3.5 copy-start.31
  271.2 49.9 %collective-permute-start.26 = (f32[256,1024]{1,0:T(8,128)}, f32[256,1024]{1,0:T(8,128)S(1)}, u32[]{:S(2)}, u32[]{:S(2)}) collective-permute-start(f32[256,1024]{1,0:T(8,128)} %get-tuple-element.90), channel_id=1, source_target_pairs={{1,1},{5,3},{2,5},{6,7},{9,9},{13,11},{10,13},{14,15},{17,17},{21,... | collective-permute-start | bytes 3145736 | tf_op jit(solution)/shard_map/ppermute | solution.py:141
  274.7 2.0 copy-start.18
  274.7 2.0 copy-start.21
  282.5 2.7 collective-permute-start.23
  287.5 34.7 %collective-permute-start.25 = (f32[256,1024]{1,0:T(8,128)}, f32[256,1024]{1,0:T(8,128)S(1)}, u32[]{:S(2)}, u32[]{:S(2)}) collective-permute-start(f32[256,1024]{1,0:T(8,128)} %convolution_add_fusion), channel_id=1, source_target_pairs={{1,4},{5,6},{2,8},{6,10},{9,12},{13,14},{10,16},{14,18},{17,20},{2... | collective-permute-start | bytes 3145736 | tf_op jit(solution)/shard_map/ppermute | solution.py:141
  290.3 73.9 %collective-permute-start.24 = (f32[256,1024]{1,0:T(8,128)}, f32[256,1024]{1,0:T(8,128)}, u32[]{:S(2)}, u32[]{:S(2)}) collective-permute-start(f32[256,1024]{1,0:T(8,128)} %convolution_add_fusion.1), channel_id=1, source_target_pairs={{1,5},{5,7},{2,9},{6,11},{9,13},{13,15},{10,17},{14,19},{17,21},{2... | collective-permute-start | bytes 3145736 | tf_op jit(solution)/shard_map/ppermute | solution.py:141
  (13 other events, 17.6 us)
where the time goes:
time: 372 us; the launch traced here: 367 us
  waiting for transfers between devices  116 us (31%)
  starting transfers between devices  96 us (26%)
  matrix products  88.5 us (24%)
  blocking collectives  32.4 us (9%)
  other arithmetic  19.7 us (5%)
  local copies, waits for them, and re-layouts  9.1 us (2%)
  Pallas kernels  3.84 us (1%)
    dot_general x50, matrix products, dot(): return jnp.dot(left, right, preferred_element_type=jnp.float32)  88.5 us
    ppermute x6, waiting for transfers between devices, outward(): lax.ppermute(x, both, plan.outward(r, shift, chains))  71.5 us
    ppermute x10, starting transfers between devices, inward(): out += [lax.ppermute(x, both, plan.inward(r, shift)) for x in pieces]  40.5 us
    all_to_all x1, starting transfers between devices, on_device(): lax.all_to_all(term, both, 0, 0, axis_index_groups=rings, tiled=True)  39.5 us
    all_to_all x1, blocking collectives, on_device(): lax.all_to_all(states, both, 0, 0, axis_index_groups=rings, tiled=True)  32.4 us
    all_to_all x1, waiting for transfers between devices, on_device(): lax.all_to_all(term, both, 0, 0, axis_index_groups=rings, tiled=True)  20.5 us
    ppermute x10, waiting for transfers between devices, inward(): out += [lax.ppermute(x, both, plan.inward(r, shift)) for x in pieces]  17.4 us
    another operation x21, other arithmetic  13.4 us
  transfers between devices with their start and end apart: 29, of which 10 were waited for; matrix products, arithmetic and copies ran while one was open for 21% of the time, Pallas kernels for 0%

commit v1 on v0

--- a/solution.py
+++ b/solution.py
@@ -19,17 +19,19 @@
     def home(self, g, h):
         return self.flat(2 * (g // 2) + h, self.low + g % 2)
 
-    def inward(self, r, shift):
+    def block(self, h, r):
+        return r if h == 0 else self.blocks - 1 - r
+
+    def inward(self, r):
         return [
-            (self.flat(g, b), self.home(g - shift, b // self.rounds))
-            for g in range(shift, self.groups)
-            for b in range(self.blocks)
-            if b % self.rounds == r
+            (self.flat(g, self.block(h, r)), self.home(g, h))
+            for g in range(self.groups)
+            for h in range(2)
         ]
 
     def outward(self, r, shift, chains):
         return [
-            (self.home(g, h), self.flat(g + shift, h * self.rounds + r))
+            (self.home(g, h), self.flat(g + shift, self.block(h, r)))
             for g in chains
             for h in range(2)
         ]
@@ -109,8 +111,30 @@
     chain = 2 * (t // 2) + jnp.clip(s - plan.low, 0, 1)
     mine, other = h * half, (1 - h) * half
 
-    rows_mine = lax.dynamic_slice_in_dim(eigen_basis, mine, half, 0)
-    rows_other = lax.dynamic_slice_in_dim(eigen_basis, other, half, 0)
+    def rows_of(basis, which):
+        pieces = []
+        for r in range(plan.rounds):
+            place = jnp.where(which == 0, plan.block(0, r), plan.block(1, r)) * block
+            pieces.append(lax.dynamic_slice_in_dim(basis, place, block, 0))
+        return jnp.concatenate(pieces, 0)
+
+    source_fine, source_coarse = force_fine[0], force_coarse[0]
+    cut = block // 2
+    along = [(g, g + 1) for g in range(groups - 1)]
+    shifted = []
+    for c in range(2):
+        piece = guess_coarse[0, c * cut : (c + 1) * cut]
+        shifted.append(lax.ppermute(piece, "tm", along))
+    started = []
+    for c, before in enumerate(shifted):
+        rows = slice(c * cut, (c + 1) * cut)
+        if started:
+            before, _ = lax.optimization_barrier((before, started[-1]))
+        before = jnp.where(t == 0, initial_state[rows], before)
+        started.append(reaction(before) + source_fine[rows])
+    eigen_basis, _ = lax.optimization_barrier((eigen_basis, started[0]))
+    rows_mine = rows_of(eigen_basis, h)
+    rows_other = rows_of(eigen_basis, 1 - h)
     cols_mine = lax.dynamic_slice_in_dim(eigen_basis, mine, half, 1)
     cols_other = lax.dynamic_slice_in_dim(eigen_basis, other, half, 1)
     right_mine, right_other = weight(cols_mine, 0), weight(cols_other, 0)
@@ -130,11 +154,8 @@
     def swap(x):
         return lax.ppermute(x, "tm", plan.partners())
 
-    def inward(pieces, shift):
-        out = []
-        for r in range(plan.rounds):
-            out += [lax.ppermute(x, both, plan.inward(r, shift)) for x in pieces]
-        return out
+    def inward(x, r):
+        return lax.ppermute(x, both, plan.inward(r))
 
     def outward(pieces, shift, chains):
         pieces = [
@@ -143,7 +164,7 @@
         ]
         out = pieces[0]
         for r in range(1, plan.rounds):
-            out = jnp.where(s % plan.rounds == r, pieces[r], out)
+            out = jnp.where(jnp.minimum(s, blocks - 1 - s) == r, pieces[r], out)
         return out
 
     def to_eigen(pieces):
@@ -164,22 +185,15 @@
     def forced(fields, forces):
         return [reaction(x) + f for x, f in zip(fields, forces)]
 
-    source_fine, source_coarse = force_fine[0], force_coarse[0]
-    cut = block // 2
-    started = []
-    for c in range(2):
-        rows = slice(c * cut, (c + 1) * cut)
-        along = [(g, g + 1) for g in range(groups - 1)]
-        before = lax.ppermute(guess_coarse[0, rows], "tm", along)
-        if started:
-            before, started[-1] = lax.optimization_barrier((before, started[-1]))
-        before = jnp.where(t == 0, initial_state[rows], before)
-        started.append(reaction(before) + source_fine[rows])
-    entered = [inward([x], 0) for x in started]
-    start = [x for pair in zip(*entered) for x in pair]
-    coarse_now = inward([source_coarse], 0)
-    fine_next = inward([source_fine], 1)
-    coarse_next = inward([source_coarse], 1)
+    later_fine = lax.ppermute(source_fine, "tm", [(g + 1, g) for g in range(groups - 1)])
+    later_coarse = lax.ppermute(
+        source_coarse, "tm", [(g + 1, g) for g in range(groups - 1)]
+    )
+    rounds = range(plan.rounds)
+    start = [inward(x, r) for r in rounds for x in started]
+    coarse_now = [inward(source_coarse, r) for r in rounds]
+    fine_next = [inward(later_fine, r) for r in rounds]
+    coarse_next = [inward(later_coarse, r) for r in rounds]
 
     relaxed_fine = from_eigen(fine_decay * to_eigen(start))
     coeffs = fine_decay * to_eigen(forced(relaxed_fine, coarse_now))

time: 372 us -> 332 us (0.89)
  the two profiles are of different devices: /device:TPU:25 before, /device:TPU:17 now
where the time goes in v1:
time: 332 us; the launch traced here: 326 us
  waiting for transfers between devices  116 us (35%)
  matrix products  92.2 us (28%)
  starting transfers between devices  51.1 us (15%)
  blocking collectives  30.6 us (9%)
  other arithmetic  18.4 us (6%)
  local copies, waits for them, and re-layouts  12.1 us (4%)
  Pallas kernels  3.84 us (1%)
    dot_general x50, matrix products, dot(): return jnp.dot(left, right, preferred_element_type=jnp.float32)  92.2 us
    ppermute x10, waiting for transfers between devices, inward(): return lax.ppermute(x, both, plan.inward(r))  47.3 us
    ppermute x6, waiting for transfers between devices, outward(): lax.ppermute(x, both, plan.outward(r, shift, chains))  39.4 us
    all_to_all x1, blocking collectives, on_device(): lax.all_to_all(states, both, 0, 0, axis_index_groups=rings, tiled=True)  30.6 us
    all_to_all x1, waiting for transfers between devices, on_device(): lax.all_to_all(term, both, 0, 0, axis_index_groups=rings, tiled=True)  24.3 us
    ppermute x10, starting transfers between devices, swap(): return lax.ppermute(x, 'tm', plan.partners())  12.6 us
    ppermute x6, starting transfers between devices, outward(): lax.ppermute(x, both, plan.outward(r, shift, chains))  11 us
    another operation x22, other arithmetic  10.9 us
  transfers between devices with their start and end apart: 31, of which 12 were waited for; matrix products, arithmetic and copies ran while one was open for 28% of the time, Pallas kernels for 0%

profile of v1, /device:TPU:17, one launch (start us, length us, event | category | flops | bytes accessed | tf_op | source)
XLA Modules:
  0.0 326.4 jit_solution(8270935634722156928)
XLA Ops:
  0.7 2.4 slice_bitcast_fusion
  3.1 3.7 %collective-permute-start = (f32[128,1024]{1,0:T(8,128)}, f32[128,1024]{1,0:T(8,128)S(1)}, u32[]{:S(2)}, u32[]{:S(2)}) collective-permute-start(f32[128,1024]{1,0:T(8,128)} %get-tuple-element.87), channel_id=1, source_target_pairs={{0,4},{4,8},{8,12},{12,16},{16,20},{20,24},{24,28},{1,5},{5,9},{9,... | collective-permute-start | bytes 1572872 | tf_op jit(solution)/shard_map/ppermute | solution.py:127
  6.8 1.9 collective-permute-start.2
  11.0 2.2 collective-permute-done
  16.5 2.3 collective-permute-done.2
  24.2 22.5 %collective-permute-done.1 = f32[128,1024]{1,0:T(8,128)S(1)} collective-permute-done((f32[128,1024]{1,0:T(8,128)S(1)}, f32[128,1024]{1,0:T(8,128)S(1)}, u32[]{:S(2)}, u32[]{:S(2)}) %collective-permute-start.1) | collective-permute-done | bytes 524320 | tf_op jit(solution)/shard_map/ppermute | solution.py:158
  47.5 10.5 %collective-permute-done.3 = f32[128,1024]{1,0:T(8,128)S(1)} collective-permute-done((f32[128,1024]{1,0:T(8,128)S(1)}, f32[128,1024]{1,0:T(8,128)S(1)}, u32[]{:S(2)}, u32[]{:S(2)}) %collective-permute-start.3) | collective-permute-done | bytes 524320 | tf_op jit(solution)/shard_map/ppermute | solution.py:158
  58.0 4.2 %collective-permute-start.14 = (f32[256,1024]{1,0:T(8,128)S(1)}, f32[256,1024]{1,0:T(8,128)S(1)}, u32[]{:S(2)}, u32[]{:S(2)}) collective-permute-start(f32[256,1024]{1,0:T(8,128)S(1)} %bitcast.31), channel_id=1, source_target_pairs={{4,0},{8,4},{12,8},{16,12},{20,16},{24,20},{28,24},{5,1},{9,5},{13... | collective-permute-start | bytes 3145736 | tf_op jit(solution)/shard_map/ppermute | solution.py:188
  62.8 1.8 fusion.57
  65.1 1.8 fusion.130
  66.9 1.8 fusion.59
  68.9 2.1 fusion.16
  71.0 1.8 fusion.55
  73.4 1.8 fusion.134
  77.7 3.1 add_add_fusion.8
  80.9 2.0 add_add_fusion.7
  83.3 1.8 fusion.53
  85.2 2.4 collective-permute-start.19
  89.8 1.8 fusion.138
  91.6 1.8 fusion.71
  93.6 3.1 fusion.26
  97.7 3.5 %fusion.142 = (bf16[512,512]{0,1:T(8,128)(2,1)S(1)}, bf16[512,512]{0,1:T(8,128)(2,1)S(1)}) fusion(bf16[1024,512]{1,0:T(8,128)(2,1)} %get-tuple-element.31, bf16[1024,512]{1,0:T(8,128)(2,1)S(1)} %get-tuple-element.30, bf16[512,1024]{1,0:T(8,128)(2,1)S(1)} %get-tuple-element.97, bf16[512,1024]{1,0:T(8,128)(2,1)S(1)} %get-tuple-element.98), kind=kOutput, calls=%fused_computation.260 | convolution fusion | flops 1630797824 | bytes 5242880 | tf_op jit(solution)/shard_map/dot_general | solution.py:64
  101.2 3.0 fusion.51
  108.2 6.5 %collective-permute-done.15 = f32[256,1024]{1,0:T(8,128)S(1)} collective-permute-done((f32[256,1024]{1,0:T(8,128)S(1)}, f32[256,1024]{1,0:T(8,128)S(1)}, u32[]{:S(2)}, u32[]{:S(2)}) %collective-permute-start.15) | collective-permute-done | bytes 1048608 | tf_op jit(solution)/shard_map/ppermute | solution.py:158
  117.3 2.2 fusion.49
  121.6 1.8 fusion.146
  123.4 1.8 fusion.83
  125.5 2.1 fusion.30
  127.6 1.8 fusion.150
  129.4 1.8 fusion.47
  131.2 2.7 collective-permute-start.18
  137.5 7.8 %collective-permute-done.20 = f32[256,1024]{1,0:T(8,128)S(1)} collective-permute-done((f32[256,1024]{1,0:T(8,128)S(1)}, f32[256,1024]{1,0:T(8,128)S(1)}, u32[]{:S(2)}, u32[]{:S(2)}) %collective-permute-start.20) | collective-permute-done | bytes 1048608 | tf_op jit(solution)/shard_map/ppermute | solution.py:158
  147.2 3.0 fusion.45
  150.2 2.6 collective-permute-start.22
  152.7 4.7 %fusion.154 = (bf16[512,512]{1,0:T(8,128)(2,1)S(1)}, bf16[512,512]{1,0:T(8,128)(2,1)S(1)}) fusion(bf16[1024,512]{1,0:T(8,128)(2,1)} %copy-done.12, bf16[1024,512]{1,0:T(8,128)(2,1)} %copy-done.14, bf16[512,1024]{1,0:T(8,128)(2,1)} %copy-done.33, bf16[512,1024]{1,0:T(8,128)(2,1)} %copy-done.32), kind=kOutput, calls=%fused_computation.272 | convolution fusion | flops 1630797824 | bytes 5242880 | tf_op jit(solution)/shard_map/dot_general | solution.py:64
  157.5 1.8 fusion.95
  160.8 3.6 %subtract_select_fusion = f32[1024,512]{1,0:T(8,128)} fusion(f32[1024,512]{1,0:T(8,128)S(1)} %get-tuple-element.92, f32[1024,512]{1,0:T(8,128)S(1)} %fusion.95, bf16[512,512]{1,0:T(8,128)(2,1)S(1)} %get-tuple-element.59, bf16[512,512]{1,0:T(8,128)(2,1)S(1)} %get-tuple-element.58, f32[512]{0:T(512)S(1)} %dynamic_slice.32, f32[1024]{0:T(1024)S(1)} %copy-done.42, ...), kind=kOutput, calls=%fused_computation.18 | convolution fusion | flops 1630535680 | bytes 9443329 | tf_op jit(solution)/shard_map/dot_general | solution.py:64
  164.4 5.1 %all-to-all-start = ((f32[8,128,512]{2,1,0:T(8,128)}), f32[8,128,512]{2,1,0:T(8,128)S(1)}, u32[]{:S(2)}, u32[]{:S(2)}) async-start(f32[8,128,512]{2,1,0:T(8,128)} %bitcast.30), calls=%async_computation | async-start | bytes 4194304 | tf_op jit(solution)/shard_map/all_to_all | solution.py:207
  169.6 1.8 dynamic_slice.39.carried
  172.2 24.3 %all-to-all-done.terms = f32[8,128,512]{2,1,0:T(8,128)S(1)} async-done(((f32[8,128,512]{2,1,0:T(8,128)}), f32[8,128,512]{2,1,0:T(8,128)S(1)}, u32[]{:S(2)}, u32[]{:S(2)}) %all-to-all-start) | async-done | bytes 2097184 | tf_op jit(solution)/shard_map/all_to_all | solution.py:207
  197.8 3.8 %scan_along.1 = f32[8,128,512]{2,1,0:T(8,128)} custom-call(f32[8,128,512]{2,1,0:T(8,128)} %copy-done.1, f32[128,512]{1,0:T(8,128)} %add_divide_fusion.decay, f32[128,512]{1,0:T(8,128)} %dynamic_slice.39.carried), custom_call_target="tpu_custom_call" | custom-call | tf_op jit(solution)/shard_map/scan_along/pallas_call | solution.py:84
  201.6 30.6 %all_to_all.18 = f32[8,128,512]{2,1,0:T(8,128)S(1)} all-to-all(f32[8,128,512]{2,1,0:T(8,128)} %scan_along.1), channel_id=1, replica_groups={{1,2,9,10,17,18,25,26},{5,6,13,14,21,22,29,30},{0,4,8,12,16,20,24,28},{..., dimensions={0} | all-to-all | bytes 4194304 | tf_op jit(solution)/shard_map/all_to_all | solution.py:210
  232.3 2.6 fusion.34
  236.4 1.8 fusion.158
  238.3 1.8 fusion.43
  240.1 1.5 collective-permute-start.23
  246.6 2.0 add_add_fusion.1
  250.2 1.8 fusion.41
  252.1 1.6 collective-permute-start.9
  253.7 1.6 collective-permute-start.8
  256.7 2.2 collective-permute-start.28
  258.9 1.8 fusion.162
  260.8 1.8 fusion.107
  262.8 2.1 fusion.38
  264.9 1.8 fusion.166
  266.7 1.8 fusion.39
  268.5 3.6 %collective-permute-start.25 = (f32[512,512]{1,0:T(8,128)S(1)}, f32[512,512]{1,0:T(8,128)S(1)}, u32[]{:S(2)}, u32[]{:S(2)}) collective-permute-start(f32[512,512]{1,0:T(8,128)S(1)} %fusion.39), channel_id=1, source_target_pairs={{0,4},{4,0},{8,12},{12,8},{16,20},{20,16},{24,28},{28,24},{1,5},{5... | collective-permute-start | bytes 3145736 | tf_op jit(solution)/shard_map/ppermute | solution.py:155
  274.7 2.0 convolution_add_fusion
  276.7 2.3 collective-permute-start.27
  279.0 2.0 convolution_add_fusion.1
  281.0 1.9 collective-permute-start.26
  284.0 16.3 %collective-permute-done.27 = f32[256,1024]{1,0:T(8,128)} collective-permute-done((f32[256,1024]{1,0:T(8,128)}, f32[256,1024]{1,0:T(8,128)}, u32[]{:S(2)}, u32[]{:S(2)}) %collective-permute-start.27) | collective-permute-done | bytes 1048608 | tf_op jit(solution)/shard_map/ppermute | solution.py:162
  300.3 23.1 %collective-permute-done.26 = f32[256,1024]{1,0:T(8,128)S(1)} collective-permute-done((f32[256,1024]{1,0:T(8,128)}, f32[256,1024]{1,0:T(8,128)S(1)}, u32[]{:S(2)}, u32[]{:S(2)}) %collective-permute-start.26) | collective-permute-done | bytes 1048608 | tf_op jit(solution)/shard_map/ppermute | solution.py:162
  323.4 2.7 select_bitcast_fusion.1
  (198 shorter events, 50.7 us)
Async XLA Ops:
  0.6 18.2 %copy-start.4 = (f32[256,1024]{1,0:T(8,128)S(1)}, f32[256,1024]{1,0:T(8,128)}, u32[]{:S(2)}) copy-start(f32[256,1024]{1,0:T(8,128)} %param.7) | copy-start | bytes 3145732
  0.6 18.2 %copy-start.5 = (f32[1,256,1024]{2,1,0:T(8,128)S(1)}, f32[1,256,1024]{2,1,0:T(8,128)}, u32[]{:S(2)}) copy-start(f32[1,256,1024]{2,1,0:T(8,128)} %param.9) | copy-start | bytes 3145732
  3.1 10.1 %collective-permute-start = (f32[128,1024]{1,0:T(8,128)}, f32[128,1024]{1,0:T(8,128)S(1)}, u32[]{:S(2)}, u32[]{:S(2)}) collective-permute-start(f32[128,1024]{1,0:T(8,128)} %get-tuple-element.87), channel_id=1, source_target_pairs={{0,4},{4,8},{8,12},{12,16},{16,20},{20,24},{24,28},{1,5},{5,9},{9,... | collective-permute-start | bytes 1572872 | tf_op jit(solution)/shard_map/ppermute | solution.py:127
  6.8 12.0 %collective-permute-start.2 = (f32[128,1024]{1,0:T(8,128)}, f32[128,1024]{1,0:T(8,128)S(1)}, u32[]{:S(2)}, u32[]{:S(2)}) collective-permute-start(f32[128,1024]{1,0:T(8,128)} %get-tuple-element.86), channel_id=1, source_target_pairs={{0,4},{4,8},{8,12},{12,16},{16,20},{20,24},{24,28},{1,5},{5,9},{9,... | collective-permute-start | bytes 1572872 | tf_op jit(solution)/shard_map/ppermute | solution.py:127
  8.7 69.0 %collective-permute-start.10 = (f32[256,1024]{1,0:T(8,128)}, f32[256,1024]{1,0:T(8,128)}, u32[]{:S(2)}, u32[]{:S(2)}) collective-permute-start(f32[256,1024]{1,0:T(8,128)} %bitcast.32), channel_id=1, source_target_pairs={{0,1},{3,5},{4,2},{7,6},{8,9},{11,13},{12,10},{15,14},{16,17},{19,... | collective-permute-start | bytes 3145736 | tf_op jit(solution)/shard_map/ppermute | solution.py:158
  10.0 10.9 %copy-start = (f32[1024,1024]{1,0:T(8,128)S(1)}, f32[1024,1024]{1,0:T(8,128)}, u32[]{:S(2)}) copy-start(f32[1024,1024]{1,0:T(8,128)} %param.11) | copy-start | bytes 12582916
  14.5 32.3 %collective-permute-start.1 = (f32[128,1024]{1,0:T(8,128)S(1)}, f32[128,1024]{1,0:T(8,128)S(1)}, u32[]{:S(2)}, u32[]{:S(2)}) collective-permute-start(f32[128,1024]{1,0:T(8,128)S(1)} %bitcast_add_fusion.1), channel_id=1, source_target_pairs={{0,1},{3,5},{4,2},{7,6},{8,9},{11,13},{12,10},{15,14},{16,17},{19,... | collective-permute-start | bytes 1572872 | tf_op jit(solution)/shard_map/ppermute | solution.py:158
  15.8 46.4 %collective-permute-start.4 = (f32[128,1024]{1,0:T(8,128)S(1)}, f32[128,1024]{1,0:T(8,128)S(1)}, u32[]{:S(2)}, u32[]{:S(2)}) collective-permute-start(f32[128,1024]{1,0:T(8,128)S(1)} %bitcast_add_fusion.1), channel_id=1, source_target_pairs={{1,1},{2,5},{5,2},{6,6},{9,9},{10,13},{13,10},{14,14},{17,17},{18,... | collective-permute-start | bytes 1572872 | tf_op jit(solution)/shard_map/ppermute | solution.py:158
  18.9 39.1 %collective-permute-start.3 = (f32[128,1024]{1,0:T(8,128)S(1)}, f32[128,1024]{1,0:T(8,128)S(1)}, u32[]{:S(2)}, u32[]{:S(2)}) collective-permute-start(f32[128,1024]{1,0:T(8,128)S(1)} %bitcast_add_fusion), channel_id=1, source_target_pairs={{0,1},{3,5},{4,2},{7,6},{8,9},{11,13},{12,10},{15,14},{16,17},{19,... | collective-permute-start | bytes 1572872 | tf_op jit(solution)/shard_map/ppermute | solution.py:158
  20.2 42.1 %collective-permute-start.5 = (f32[128,1024]{1,0:T(8,128)S(1)}, f32[128,1024]{1,0:T(8,128)S(1)}, u32[]{:S(2)}, u32[]{:S(2)}) collective-permute-start(f32[128,1024]{1,0:T(8,128)S(1)} %bitcast_add_fusion), channel_id=1, source_target_pairs={{1,1},{2,5},{5,2},{6,6},{9,9},{10,13},{13,10},{14,14},{17,17},{18,... | collective-permute-start | bytes 1572872 | tf_op jit(solution)/shard_map/ppermute | solution.py:158
  21.6 100.0 %copy-start.12 = (bf16[1024,512]{1,0:T(8,128)(2,1)}, bf16[1024,512]{1,0:T(8,128)(2,1)S(1)}, u32[]{:S(2)}) copy-start(bf16[1024,512]{1,0:T(8,128)(2,1)S(1)} %get-tuple-element.17) | copy-start | bytes 3145732
  21.6 100.0 %copy-start.14 = (bf16[1024,512]{1,0:T(8,128)(2,1)}, bf16[1024,512]{1,0:T(8,128)(2,1)S(1)}, u32[]{:S(2)}) copy-start(bf16[1024,512]{1,0:T(8,128)(2,1)S(1)} %get-tuple-element.19) | copy-start | bytes 3145732
  21.7 125.5 %copy-start.16 = (bf16[1024,512]{1,0:T(8,128)(2,1)}, bf16[1024,512]{1,0:T(8,128)(2,1)S(1)}, u32[]{:S(2)}) copy-start(bf16[1024,512]{1,0:T(8,128)(2,1)S(1)} %get-tuple-element.16) | copy-start | bytes 3145732
  21.7 125.5 %copy-start.18 = (bf16[1024,512]{1,0:T(8,128)(2,1)}, bf16[1024,512]{1,0:T(8,128)(2,1)S(1)}, u32[]{:S(2)}) copy-start(bf16[1024,512]{1,0:T(8,128)(2,1)S(1)} %get-tuple-element.18) | copy-start | bytes 3145732
  22.4 112.7 %copy-start.8 = (bf16[512,1024]{0,1:T(8,128)(2,1)}, bf16[512,1024]{0,1:T(8,128)(2,1)S(1)}, u32[]{:S(2)}) copy-start(bf16[512,1024]{0,1:T(8,128)(2,1)S(1)} %get-tuple-element.9) | copy-start | bytes 3145732
  22.4 112.7 %copy-start.10 = (bf16[512,1024]{0,1:T(8,128)(2,1)}, bf16[512,1024]{0,1:T(8,128)(2,1)S(1)}, u32[]{:S(2)}) copy-start(bf16[512,1024]{0,1:T(8,128)(2,1)S(1)} %get-tuple-element.10) | copy-start | bytes 3145732
  22.4 123.1 %copy-start.6 = (bf16[512,1024]{0,1:T(8,128)(2,1)}, bf16[512,1024]{0,1:T(8,128)(2,1)S(1)}, u32[]{:S(2)}) copy-start(bf16[512,1024]{0,1:T(8,128)(2,1)S(1)} %get-tuple-element.11) | copy-start | bytes 3145732
  23.7 103.9 %copy-start.38 = (bf16[512,1024]{1,0:T(8,128)(2,1)}, bf16[512,1024]{1,0:T(8,128)(2,1)S(1)}, u32[]{:S(2)}) copy-start(bf16[512,1024]{1,0:T(8,128)(2,1)S(1)} %get-tuple-element.97) | copy-start | bytes 3145732
  23.7 103.9 %copy-start.40 = (bf16[512,1024]{1,0:T(8,128)(2,1)}, bf16[512,1024]{1,0:T(8,128)(2,1)S(1)}, u32[]{:S(2)}) copy-start(bf16[512,1024]{1,0:T(8,128)(2,1)S(1)} %get-tuple-element.98) | copy-start | bytes 3145732
  23.7 105.7 %copy-start.34 = (bf16[512,1024]{1,0:T(8,128)(2,1)}, bf16[512,1024]{1,0:T(8,128)(2,1)S(1)}, u32[]{:S(2)}) copy-start(bf16[512,1024]{1,0:T(8,128)(2,1)S(1)} %get-tuple-element.34) | copy-start | bytes 3145732
  23.7 105.7 %copy-start.36 = (bf16[512,1024]{1,0:T(8,128)(2,1)}, bf16[512,1024]{1,0:T(8,128)(2,1)S(1)}, u32[]{:S(2)}) copy-start(bf16[512,1024]{1,0:T(8,128)(2,1)S(1)} %get-tuple-element.35) | copy-start | bytes 3145732
  23.7 23.0 %copy-start.43 = (f32[1,256,1024]{2,1,0:T(8,128)S(1)}, f32[1,256,1024]{2,1,0:T(8,128)}, u32[]{:S(2)}) copy-start(f32[1,256,1024]{2,1,0:T(8,128)} %param.10) | copy-start | bytes 3145732
  24.2 99.2 %copy-start.20 = (bf16[1024,512]{0,1:T(8,128)(2,1)}, bf16[1024,512]{0,1:T(8,128)(2,1)S(1)}, u32[]{:S(2)}) copy-start(bf16[1024,512]{0,1:T(8,128)(2,1)S(1)} %get-tuple-element.42) | copy-start | bytes 3145732
  24.2 99.2 %copy-start.23 = (bf16[1024,512]{0,1:T(8,128)(2,1)}, bf16[1024,512]{0,1:T(8,128)(2,1)S(1)}, u32[]{:S(2)}) copy-start(bf16[1024,512]{0,1:T(8,128)(2,1)S(1)} %get-tuple-element.43) | copy-start | bytes 3145732
  46.7 34.1 %collective-permute-start.11 = (f32[256,1024]{1,0:T(8,128)S(1)}, f32[256,1024]{1,0:T(8,128)S(1)}, u32[]{:S(2)}, u32[]{:S(2)}) collective-permute-start(f32[256,1024]{1,0:T(8,128)S(1)} %bitcast.33), channel_id=1, source_target_pairs={{1,1},{2,5},{5,2},{6,6},{9,9},{10,13},{13,10},{14,14},{17,17},{18,... | collective-permute-start | bytes 3145736 | tf_op jit(solution)/shard_map/ppermute | solution.py:158
  58.0 29.6 %collective-permute-start.14 = (f32[256,1024]{1,0:T(8,128)S(1)}, f32[256,1024]{1,0:T(8,128)S(1)}, u32[]{:S(2)}, u32[]{:S(2)}) collective-permute-start(f32[256,1024]{1,0:T(8,128)S(1)} %bitcast.31), channel_id=1, source_target_pairs={{4,0},{8,4},{12,8},{16,12},{20,16},{24,20},{28,24},{5,1},{9,5},{13... | collective-permute-start | bytes 3145736 | tf_op jit(solution)/shard_map/ppermute | solution.py:188
  64.6 4.2 %collective-permute-start.6 = (f32[512,512]{1,0:T(8,128)S(1)}, f32[512,512]{1,0:T(8,128)S(1)}, u32[]{:S(2)}, u32[]{:S(2)}) collective-permute-start(f32[512,512]{1,0:T(8,128)S(1)} %fusion.57), channel_id=1, source_target_pairs={{0,4},{4,0},{8,12},{12,8},{16,20},{20,16},{24,28},{28,24},{1,5},{5... | collective-permute-start | bytes 3145736 | tf_op jit(solution)/shard_map/ppermute | solution.py:155
  65.1 60.4 %copy-start.26 = (bf16[1024,512]{0,1:T(8,128)(2,1)}, bf16[1024,512]{0,1:T(8,128)(2,1)S(1)}, u32[]{:S(2)}) copy-start(bf16[1024,512]{0,1:T(8,128)(2,1)S(1)} %get-tuple-element.40) | copy-start | bytes 3145732
  65.1 60.4 %copy-start.29 = (bf16[1024,512]{0,1:T(8,128)(2,1)}, bf16[1024,512]{0,1:T(8,128)(2,1)S(1)}, u32[]{:S(2)}) copy-start(bf16[1024,512]{0,1:T(8,128)(2,1)S(1)} %get-tuple-element.41) | copy-start | bytes 3145732
  72.8 4.6 %collective-permute-start.7 = (f32[512,512]{1,0:T(8,128)S(1)}, f32[512,512]{1,0:T(8,128)S(1)}, u32[]{:S(2)}, u32[]{:S(2)}) collective-permute-start(f32[512,512]{1,0:T(8,128)S(1)} %fusion.55), channel_id=1, source_target_pairs={{0,4},{4,0},{8,12},{12,8},{16,20},{20,16},{24,28},{28,24},{1,5},{5... | collective-permute-start | bytes 3145736 | tf_op jit(solution)/shard_map/ppermute | solution.py:155
  85.1 8.3 %collective-permute-start.12 = (f32[512,512]{1,0:T(8,128)S(1)}, f32[512,512]{1,0:T(8,128)S(1)}, u32[]{:S(2)}, u32[]{:S(2)}) collective-permute-start(f32[512,512]{1,0:T(8,128)S(1)} %fusion.53), channel_id=1, source_target_pairs={{0,4},{4,0},{8,12},{12,8},{16,20},{20,16},{24,28},{28,24},{1,5},{5... | collective-permute-start | bytes 3145736 | tf_op jit(solution)/shard_map/ppermute | solution.py:155
  85.2 34.3 %collective-permute-start.19 = (f32[256,1024]{1,0:T(8,128)S(1)}, f32[256,1024]{1,0:T(8,128)S(1)}, u32[]{:S(2)}, u32[]{:S(2)}) collective-permute-start(f32[256,1024]{1,0:T(8,128)S(1)} %bitcast.34), channel_id=1, source_target_pairs={{4,0},{8,4},{12,8},{16,12},{20,16},{24,20},{28,24},{5,1},{9,5},{13... | collective-permute-start | bytes 3145736 | tf_op jit(solution)/shard_map/ppermute | solution.py:189
  87.6 27.0 %collective-permute-start.15 = (f32[256,1024]{1,0:T(8,128)S(1)}, f32[256,1024]{1,0:T(8,128)S(1)}, u32[]{:S(2)}, u32[]{:S(2)}) collective-permute-start(f32[256,1024]{1,0:T(8,128)S(1)} %collective-permute-done.14), channel_id=1, source_target_pairs={{0,1},{3,5},{4,2},{7,6},{8,9},{11,13},{12,10},{15,14},{16,17},{19,... | collective-permute-start | bytes 3145736 | tf_op jit(solution)/shard_map/ppermute | solution.py:158
  88.9 26.8 %collective-permute-start.16 = (f32[256,1024]{1,0:T(8,128)S(1)}, f32[256,1024]{1,0:T(8,128)S(1)}, u32[]{:S(2)}, u32[]{:S(2)}) collective-permute-start(f32[256,1024]{1,0:T(8,128)S(1)} %collective-permute-done.14), channel_id=1, source_target_pairs={{1,1},{2,5},{5,2},{6,6},{9,9},{10,13},{13,10},{14,14},{17,17},{18,... | collective-permute-start | bytes 3145736 | tf_op jit(solution)/shard_map/ppermute | solution.py:158
  96.7 64.0 %copy-start.2 = (f32[1024,512]{1,0:T(8,128)}, f32[1024,512]{1,0:T(8,128)S(1)}, u32[]{:S(2)}) copy-start(f32[1024,512]{1,0:T(8,128)S(1)} %get-tuple-element.92) | copy-start | bytes 6291460
  97.7 3.5 %copy-start.49 = (bf16[1024,512]{1,0:T(8,128)(2,1)S(1)}, bf16[1024,512]{1,0:T(8,128)(2,1)}, u32[]{:S(2)}) copy-start(bf16[1024,512]{1,0:T(8,128)(2,1)} %get-tuple-element.31) | copy-start | bytes 3145732
  104.2 3.7 %collective-permute-start.13 = (f32[512,512]{1,0:T(8,128)S(1)}, f32[512,512]{1,0:T(8,128)S(1)}, u32[]{:S(2)}, u32[]{:S(2)}) collective-permute-start(f32[512,512]{1,0:T(8,128)S(1)} %fusion.51), channel_id=1, source_target_pairs={{0,4},{4,0},{8,12},{12,8},{16,20},{20,16},{24,28},{28,24},{1,5},{5... | collective-permute-start | bytes 3145736 | tf_op jit(solution)/shard_map/ppermute | solution.py:155
  119.5 5.8 %collective-permute-start.17 = (f32[512,512]{1,0:T(8,128)S(1)}, f32[512,512]{1,0:T(8,128)S(1)}, u32[]{:S(2)}, u32[]{:S(2)}) collective-permute-start(f32[512,512]{1,0:T(8,128)S(1)} %fusion.49), channel_id=1, source_target_pairs={{0,4},{4,0},{8,12},{12,8},{16,20},{20,16},{24,28},{28,24},{1,5},{5... | collective-permute-start | bytes 3145736 | tf_op jit(solution)/shard_map/ppermute | solution.py:155
  119.6 25.8 %collective-permute-start.20 = (f32[256,1024]{1,0:T(8,128)S(1)}, f32[256,1024]{1,0:T(8,128)S(1)}, u32[]{:S(2)}, u32[]{:S(2)}) collective-permute-start(f32[256,1024]{1,0:T(8,128)S(1)} %collective-permute-done.19), channel_id=1, source_target_pairs={{0,1},{3,5},{4,2},{7,6},{8,9},{11,13},{12,10},{15,14},{16,17},{19,... | collective-permute-start | bytes 3145736 | tf_op jit(solution)/shard_map/ppermute | solution.py:158
  120.9 25.7 %collective-permute-start.21 = (f32[256,1024]{1,0:T(8,128)S(1)}, f32[256,1024]{1,0:T(8,128)S(1)}, u32[]{:S(2)}, u32[]{:S(2)}) collective-permute-start(f32[256,1024]{1,0:T(8,128)S(1)} %collective-permute-done.19), channel_id=1, source_target_pairs={{1,1},{2,5},{5,2},{6,6},{9,9},{10,13},{13,10},{14,14},{17,17},{18,... | collective-permute-start | bytes 3145736 | tf_op jit(solution)/shard_map/ppermute | solution.py:158
  131.2 5.0 %collective-permute-start.18 = (f32[512,512]{1,0:T(8,128)S(1)}, f32[512,512]{1,0:T(8,128)S(1)}, u32[]{:S(2)}, u32[]{:S(2)}) collective-permute-start(f32[512,512]{1,0:T(8,128)S(1)} %fusion.47), channel_id=1, source_target_pairs={{0,4},{4,0},{8,12},{12,8},{16,20},{20,16},{24,28},{28,24},{1,5},{5... | collective-permute-start | bytes 3145736 | tf_op jit(solution)/shard_map/ppermute | solution.py:155
  147.2 3.0 copy-start.32
  150.2 9.2 %collective-permute-start.22 = (f32[512,512]{1,0:T(8,128)}, f32[512,512]{1,0:T(8,128)}, u32[]{:S(2)}, u32[]{:S(2)}) collective-permute-start(f32[512,512]{1,0:T(8,128)} %fusion.45), channel_id=1, source_target_pairs={{0,4},{4,0},{8,12},{12,8},{16,20},{20,16},{24,28},{28,24},{1,5},{5... | collective-permute-start | bytes 3145736 | tf_op jit(solution)/shard_map/ppermute | solution.py:155
  152.7 4.8 %copy-start.21 = (bf16[1024,512]{0,1:T(8,128)(2,1)S(1)}, bf16[1024,512]{0,1:T(8,128)(2,1)}, u32[]{:S(2)}) copy-start(bf16[1024,512]{0,1:T(8,128)(2,1)} %copy-done.20) | copy-start | bytes 3145732
  152.7 4.8 %copy-start.24 = (bf16[1024,512]{0,1:T(8,128)(2,1)S(1)}, bf16[1024,512]{0,1:T(8,128)(2,1)}, u32[]{:S(2)}) copy-start(bf16[1024,512]{0,1:T(8,128)(2,1)} %copy-done.23) | copy-start | bytes 3145732
  157.5 3.3 copy-start.27
  157.5 3.3 copy-start.30
  164.4 32.0 %all-to-all-start = ((f32[8,128,512]{2,1,0:T(8,128)}), f32[8,128,512]{2,1,0:T(8,128)S(1)}, u32[]{:S(2)}, u32[]{:S(2)}) async-start(f32[8,128,512]{2,1,0:T(8,128)} %bitcast.30), calls=%async_computation | async-start | bytes 4194304 | tf_op jit(solution)/shard_map/all_to_all | solution.py:207
  201.6 30.6 %copy-start.3 = (f32[1024,512]{1,0:T(8,128)S(1)}, f32[1024,512]{1,0:T(8,128)}, u32[]{:S(2)}) copy-start(f32[1024,512]{1,0:T(8,128)} %copy-done.2) | copy-start | bytes 6291460
  238.3 3.5 %copy-start.9 = (bf16[512,1024]{0,1:T(8,128)(2,1)S(1)}, bf16[512,1024]{0,1:T(8,128)(2,1)}, u32[]{:S(2)}) copy-start(bf16[512,1024]{0,1:T(8,128)(2,1)} %copy-done.8) | copy-start | bytes 3145732
  238.3 3.5 %copy-start.11 = (bf16[512,1024]{0,1:T(8,128)(2,1)S(1)}, bf16[512,1024]{0,1:T(8,128)(2,1)}, u32[]{:S(2)}) copy-start(bf16[512,1024]{0,1:T(8,128)(2,1)} %copy-done.10) | copy-start | bytes 3145732
  240.1 3.8 %collective-permute-start.23 = (f32[512,512]{1,0:T(8,128)S(1)}, f32[512,512]{1,0:T(8,128)S(1)}, u32[]{:S(2)}, u32[]{:S(2)}) collective-permute-start(f32[512,512]{1,0:T(8,128)S(1)} %fusion.43), channel_id=1, source_target_pairs={{0,4},{4,0},{8,12},{12,8},{16,20},{20,16},{24,28},{28,24},{1,5},{5... | collective-permute-start | bytes 3145736 | tf_op jit(solution)/shard_map/ppermute | solution.py:155
  250.2 8.7 %copy-start.13 = (bf16[1024,512]{1,0:T(8,128)(2,1)S(1)}, bf16[1024,512]{1,0:T(8,128)(2,1)}, u32[]{:S(2)}) copy-start(bf16[1024,512]{1,0:T(8,128)(2,1)} %copy-done.12) | copy-start | bytes 3145732
  250.2 8.7 %copy-start.15 = (bf16[1024,512]{1,0:T(8,128)(2,1)S(1)}, bf16[1024,512]{1,0:T(8,128)(2,1)}, u32[]{:S(2)}) copy-start(bf16[1024,512]{1,0:T(8,128)(2,1)} %copy-done.14) | copy-start | bytes 3145732
  252.0 10.6 %collective-permute-start.24 = (f32[512,512]{1,0:T(8,128)S(1)}, f32[512,512]{1,0:T(8,128)S(1)}, u32[]{:S(2)}, u32[]{:S(2)}) collective-permute-start(f32[512,512]{1,0:T(8,128)S(1)} %fusion.41), channel_id=1, source_target_pairs={{0,4},{4,0},{8,12},{12,8},{16,20},{20,16},{24,28},{28,24},{1,5},{5... | collective-permute-start | bytes 3145736 | tf_op jit(solution)/shard_map/ppermute | solution.py:155
  252.1 31.9 %collective-permute-start.9 = (f32[256,1024]{1,0:T(8,128)}, f32[256,1024]{1,0:T(8,128)}, u32[]{:S(2)}, u32[]{:S(2)}) collective-permute-start(f32[256,1024]{1,0:T(8,128)} %get-tuple-element.91), channel_id=1, source_target_pairs={{1,0},{5,3}} | collective-permute-start | bytes 3145736 | tf_op jit(solution)/shard_map/ppermute | solution.py:162
  253.7 30.3 %collective-permute-start.8 = (f32[256,1024]{1,0:T(8,128)}, f32[256,1024]{1,0:T(8,128)}, u32[]{:S(2)}, u32[]{:S(2)}) collective-permute-start(f32[256,1024]{1,0:T(8,128)} %get-tuple-element.89), channel_id=1, source_target_pairs={{1,1},{5,2}} | collective-permute-start | bytes 3145736 | tf_op jit(solution)/shard_map/ppermute | solution.py:162
  255.3 25.6 %collective-permute-start.29 = (f32[256,1024]{1,0:T(8,128)S(1)}, f32[256,1024]{1,0:T(8,128)S(1)}, u32[]{:S(2)}, u32[]{:S(2)}) collective-permute-start(f32[256,1024]{1,0:T(8,128)S(1)} %get-tuple-element.96), channel_id=1, source_target_pairs={{1,0},{5,3},{2,4},{6,7},{9,8},{13,11},{10,12},{14,15},{17,16},{21,... | collective-permute-start | bytes 3145736 | tf_op jit(solution)/shard_map/ppermute | solution.py:162
  256.7 4.0 %copy-start.22 = (bf16[1024,512]{0,1:T(8,128)(2,1)S(1)}, bf16[1024,512]{0,1:T(8,128)(2,1)}, u32[]{:S(2)}) copy-start(bf16[1024,512]{0,1:T(8,128)(2,1)} %copy-done.20) | copy-start | bytes 3145732
  256.7 4.0 %copy-start.25 = (bf16[1024,512]{0,1:T(8,128)(2,1)S(1)}, bf16[1024,512]{0,1:T(8,128)(2,1)}, u32[]{:S(2)}) copy-start(bf16[1024,512]{0,1:T(8,128)(2,1)} %copy-done.23) | copy-start | bytes 3145732
  256.7 26.2 %collective-permute-start.28 = (f32[256,1024]{1,0:T(8,128)}, f32[256,1024]{1,0:T(8,128)S(1)}, u32[]{:S(2)}, u32[]{:S(2)}) collective-permute-start(f32[256,1024]{1,0:T(8,128)} %get-tuple-element.94), channel_id=1, source_target_pairs={{1,1},{5,2},{2,5},{6,6},{9,9},{13,10},{10,13},{14,14},{17,17},{21,... | collective-permute-start | bytes 3145736 | tf_op jit(solution)/shard_map/ppermute | solution.py:162
  268.5 5.9 %collective-permute-start.25 = (f32[512,512]{1,0:T(8,128)S(1)}, f32[512,512]{1,0:T(8,128)S(1)}, u32[]{:S(2)}, u32[]{:S(2)}) collective-permute-start(f32[512,512]{1,0:T(8,128)S(1)} %fusion.39), channel_id=1, source_target_pairs={{0,4},{4,0},{8,12},{12,8},{16,20},{20,16},{24,28},{28,24},{1,5},{5... | collective-permute-start | bytes 3145736 | tf_op jit(solution)/shard_map/ppermute | solution.py:155
  276.7 23.6 %collective-permute-start.27 = (f32[256,1024]{1,0:T(8,128)}, f32[256,1024]{1,0:T(8,128)}, u32[]{:S(2)}, u32[]{:S(2)}) collective-permute-start(f32[256,1024]{1,0:T(8,128)} %convolution_add_fusion), channel_id=1, source_target_pairs={{1,4},{5,7},{2,8},{6,11},{9,12},{13,15},{10,16},{14,19},{17,20},{2... | collective-permute-start | bytes 3145736 | tf_op jit(solution)/shard_map/ppermute | solution.py:162
  281.0 42.5 %collective-permute-start.26 = (f32[256,1024]{1,0:T(8,128)}, f32[256,1024]{1,0:T(8,128)S(1)}, u32[]{:S(2)}, u32[]{:S(2)}) collective-permute-start(f32[256,1024]{1,0:T(8,128)} %convolution_add_fusion.1), channel_id=1, source_target_pairs={{1,5},{5,6},{2,9},{6,10},{9,13},{13,14},{10,17},{14,18},{17,21},{2... | collective-permute-start | bytes 3145736 | tf_op jit(solution)/shard_map/ppermute | solution.py:162
  (17 other events, 26.8 us)

commit v2 on v1

--- a/solution.py
+++ b/solution.py
@@ -148,23 +148,35 @@
     own_part = chain * part
     rates_part = lax.dynamic_slice_in_dim(eigen_rates, own_part, part, 0)
     part_decay = 1.0 / (1.0 + 2.0 * (rates_part[:, None] + rates_mine[None, :]))
-    carried_mine = lax.dynamic_slice_in_dim(carried_correction, mine, half, 1)
-    carried_part = lax.dynamic_slice_in_dim(carried_mine, own_part, part, 0)
+    carried_part = lax.dynamic_slice(carried_correction, (own_part, mine), (part, half))
 
     def swap(x):
         return lax.ppermute(x, "tm", plan.partners())
 
+    def sent(x, pairs):
+        return lax.ppermute(x, both, [(a, b) for a, b in pairs if a != b])
+
+    def with_kept(x, out, pairs):
+        stays = False
+        for a, b in pairs:
+            if a == b:
+                stays = stays | (t * blocks + s == a)
+        return out if stays is False else jnp.where(stays, x, out)
+
     def inward(x, r):
-        return lax.ppermute(x, both, plan.inward(r))
+        return with_kept(x, sent(x, plan.inward(r)), plan.inward(r))
 
     def outward(pieces, shift, chains):
-        pieces = [
-            lax.ppermute(x, both, plan.outward(r, shift, chains))
-            for r, x in enumerate(pieces)
-        ]
-        out = pieces[0]
-        for r in range(1, plan.rounds):
-            out = jnp.where(jnp.minimum(s, blocks - 1 - s) == r, pieces[r], out)
+        out = []
+        for r, x in enumerate(pieces):
+            out.append(sent(x, plan.outward(r, shift, chains)))
+        return out
+
+    def settled(pieces, arrived, shift, chains):
+        out = None
+        for r, x in enumerate(pieces):
+            here = with_kept(x, arrived[r], plan.outward(r, shift, chains))
+            out = here if r == 0 else jnp.where(jnp.minimum(s, blocks - 1 - s) == r, here, out)
         return out
 
     def to_eigen(pieces):
@@ -177,10 +189,12 @@
         coeffs = operand(coeffs, 0)
         arrived = operand(swap(dot(up_other, coeffs)), 1)
         kept = operand(dot(up_mine, coeffs), 1)
-        return [
-            dot(kept[i : i + block], back_mine) + dot(arrived[i : i + block], back_other)
-            for i in range(0, half, block)
-        ]
+        out = []
+        for r in range(plan.rounds):
+            rows = slice(r * block, (r + 1) * block)
+            early = dot(kept[rows], back_mine)
+            out.append(early + dot(arrived[rows], back_other))
+        return out
 
     def forced(fields, forces):
         return [reaction(x) + f for x, f in zip(fields, forces)]
@@ -198,24 +212,32 @@
     relaxed_fine = from_eigen(fine_decay * to_eigen(start))
     coeffs = fine_decay * to_eigen(forced(relaxed_fine, coarse_now))
     relaxed_coarse = from_eigen(coeffs)
+    first = chain == 0
     second = to_eigen(forced(relaxed_coarse, fine_next))
     second = from_eigen(fine_decay * second)
     ahead = fine_decay * to_eigen(forced(second, coarse_next))
-    term = jnp.where(chain == 0, ahead, ahead - coarse_decay * coeffs)
+    term = jnp.where(first, ahead, ahead - coarse_decay * coeffs)
 
     rings = plan.rings()
     spread = lax.all_to_all(term, both, 0, 0, axis_index_groups=rings, tiled=True)
     states = scan_along(spread.reshape(groups, part, half), part_decay, carried_part)
     states = states.reshape(grid, half)
     states = lax.all_to_all(states, both, 0, 0, axis_index_groups=rings, tiled=True)
-    total = jnp.where(chain == 0, coarse_decay * carried_mine + coeffs, states)
+    total = states + jnp.where(first, coeffs, 0.0)
 
     coarse_new = from_eigen(total)
-    coarse_out = outward(coarse_new, 0, range(groups))
+    coarse_sent = outward(coarse_new, 0, range(groups))
     fine_new = to_eigen(forced(coarse_new, fine_next))
     fine_new = from_eigen(fine_decay * fine_new)
-    fine_out = outward(fine_new, 1, range(groups - 1))
-    first_out = outward(relaxed_fine, 0, range(1))
+    fine_sent = outward(fine_new, 1, range(groups - 1))
+    first_sent = outward(relaxed_fine, 0, range(1))
+    coarse_new, relaxed_fine, fine_new = lax.optimization_barrier(
+        (coarse_new, relaxed_fine, fine_new)
+    )
+    first_out = settled(relaxed_fine, first_sent, 0, range(1))
+    coarse_out = settled(coarse_new, coarse_sent, 0, range(groups))
+    coarse_out, first_out = lax.optimization_barrier((coarse_out, first_out))
+    fine_out = settled(fine_new, fine_sent, 1, range(groups - 1))
     fine_out = jnp.where(t == 0, first_out, fine_out)
     return (fine_out[None], coarse_out[None])
 

time: 332 us -> 335 us (level)
  the two profiles are of different devices: /device:TPU:17 before, /device:TPU:25 now
where the time goes in v2:
time: 335 us; the launch traced here: 330 us
  matrix products  93.6 us (28%)
  starting transfers between devices  86 us (26%)
  waiting for transfers between devices  79.4 us (24%)
  blocking collectives  32.4 us (10%)
  other arithmetic  20.1 us (6%)
  local copies, waits for them, and re-layouts  12.5 us (4%)
  Pallas kernels  3.83 us (1%)
    dot_general x50, matrix products, dot(): return jnp.dot(left, right, preferred_element_type=jnp.float32)  93.6 us
    ppermute x16, waiting for transfers between devices, sent(): return lax.ppermute(x, both, [(a, b) for a, b in pairs if a != b])  55.9 us
    ppermute x1, starting transfers between devices, on_device(): lax.ppermute(source_fine, 'tm', [(g + 1, g) for g in range(groups - 1)])  32.6 us
    all_to_all x1, blocking collectives, on_device(): lax.all_to_all(states, both, 0, 0, axis_index_groups=rings, tiled=True)  32.4 us
    ppermute x16, starting transfers between devices, sent(): return lax.ppermute(x, both, [(a, b) for a, b in pairs if a != b])  31.3 us
    all_to_all x1, waiting for transfers between devices, on_device(): lax.all_to_all(term, both, 0, 0, axis_index_groups=rings, tiled=True)  20.6 us
    ppermute x10, starting transfers between devices, swap(): return lax.ppermute(x, 'tm', plan.partners())  10.1 us
    another operation x21, other arithmetic  8.71 us
  transfers between devices with their start and end apart: 31, of which 9 were waited for; matrix products, arithmetic and copies ran while one was open for 29% of the time, Pallas kernels for 0%

profile of v2, /device:TPU:25, one launch (start us, length us, event | category | flops | bytes accessed | tf_op | source)
XLA Modules:
  0.0 330.0 jit_solution(2512993941148033016)
XLA Ops:
  0.7 2.4 slice_bitcast_fusion.1
  3.1 3.7 %collective-permute-start = (f32[128,1024]{1,0:T(8,128)}, f32[128,1024]{1,0:T(8,128)S(1)}, u32[]{:S(2)}, u32[]{:S(2)}) collective-permute-start(f32[128,1024]{1,0:T(8,128)} %get-tuple-element.94), channel_id=1, source_target_pairs={{0,4},{4,8},{8,12},{12,16},{16,20},{20,24},{24,28},{1,5},{5,9},{9,... | collective-permute-start | bytes 1572872 | tf_op jit(solution)/shard_map/ppermute | solution.py:127
  6.8 1.9 collective-permute-start.2
  8.7 3.1 collective-permute-start.8
  11.8 1.6 collective-permute-start.9
  16.5 2.3 collective-permute-done.2
  19.6 2.1 collective-permute-start.3
  26.4 32.6 %collective-permute-start.12 = (f32[256,1024]{1,0:T(8,128)S(1)}, f32[256,1024]{1,0:T(8,128)S(1)}, u32[]{:S(2)}, u32[]{:S(2)}) collective-permute-start(f32[256,1024]{1,0:T(8,128)S(1)} %bitcast.34), channel_id=1, source_target_pairs={{4,0},{8,4},{12,8},{16,12},{20,16},{24,20},{28,24},{5,1},{9,5},{13... | collective-permute-start | bytes 3145736 | tf_op jit(solution)/shard_map/ppermute | solution.py:202
  59.5 1.8 fusion.58
  61.3 4.2 %collective-permute-start.6 = (f32[512,512]{1,0:T(8,128)S(1)}, f32[512,512]{1,0:T(8,128)S(1)}, u32[]{:S(2)}, u32[]{:S(2)}) collective-permute-start(f32[512,512]{1,0:T(8,128)S(1)} %fusion.58), channel_id=1, source_target_pairs={{0,4},{4,0},{8,12},{12,8},{16,20},{20,16},{24,28},{28,24},{1,5},{5... | collective-permute-start | bytes 3145736 | tf_op jit(solution)/shard_map/ppermute | solution.py:154
  65.9 1.8 fusion.129
  67.7 1.8 fusion.60
  69.8 2.1 fusion.17
  71.9 1.8 fusion.56
  73.8 1.9 fusion.133
  79.0 3.2 select_add_fusion.1
  82.2 3.1 add_add_fusion.6
  85.7 1.8 fusion.54
  88.1 1.9 collective-permute-start.17
  90.1 5.0 %collective-permute-start.13 = (f32[256,1024]{1,0:T(8,128)S(1)}, f32[256,1024]{1,0:T(8,128)S(1)}, u32[]{:S(2)}, u32[]{:S(2)}) collective-permute-start(f32[256,1024]{1,0:T(8,128)S(1)} %collective-permute-done.12), channel_id=1, source_target_pairs={{0,1},{3,5},{4,2},{7,6},{8,9},{11,13},{12,10},{15,14},{16,17},{19,... | collective-permute-start | bytes 3145736 | tf_op jit(solution)/shard_map/ppermute | solution.py:157
  96.0 1.8 fusion.137
  97.8 1.8 fusion.72
  99.8 3.1 fusion.27
  103.9 3.5 %fusion.141 = (bf16[512,512]{0,1:T(8,128)(2,1)S(1)}, bf16[512,512]{0,1:T(8,128)(2,1)S(1)}) fusion(bf16[1024,512]{1,0:T(8,128)(2,1)} %get-tuple-element.39, bf16[1024,512]{1,0:T(8,128)(2,1)S(1)} %get-tuple-element.38, bf16[512,1024]{1,0:T(8,128)(2,1)S(1)} %get-tuple-element.105, bf16[512,1024]{1,0:T(8,128)(2,1)S(1)} %get-tuple-element.106), kind=kOutput, calls=%fused_computation.262 | convolution fusion | flops 1630797824 | bytes 5242880 | tf_op jit(solution)/shard_map/dot_general | solution.py:64
  107.4 3.0 fusion.52
  114.6 3.0 collective-permute-done.13
  119.1 2.2 fusion.50
  122.2 5.7 %collective-permute-start.18 = (f32[256,1024]{1,0:T(8,128)S(1)}, f32[256,1024]{1,0:T(8,128)S(1)}, u32[]{:S(2)}, u32[]{:S(2)}) collective-permute-start(f32[256,1024]{1,0:T(8,128)S(1)} %collective-permute-done.17), channel_id=1, source_target_pairs={{0,1},{3,5},{4,2},{7,6},{8,9},{11,13},{12,10},{15,14},{16,17},{19,... | collective-permute-start | bytes 3145736 | tf_op jit(solution)/shard_map/ppermute | solution.py:157
  128.6 1.8 fusion.145
  130.4 1.8 fusion.84
  132.5 2.1 fusion.31
  134.6 1.8 fusion.149
  136.4 1.8 fusion.48
  142.8 6.9 %collective-permute-done.18 = f32[256,1024]{1,0:T(8,128)S(1)} collective-permute-done((f32[256,1024]{1,0:T(8,128)S(1)}, f32[256,1024]{1,0:T(8,128)S(1)}, u32[]{:S(2)}, u32[]{:S(2)}) %collective-permute-start.18) | collective-permute-done | bytes 1048608 | tf_op jit(solution)/shard_map/ppermute | solution.py:157
  151.7 3.0 fusion.46
  156.2 4.9 %fusion.153 = (bf16[512,512]{1,0:T(8,128)(2,1)S(1)}, bf16[512,512]{1,0:T(8,128)(2,1)S(1)}) fusion(bf16[1024,512]{1,0:T(8,128)(2,1)} %copy-done.12, bf16[1024,512]{1,0:T(8,128)(2,1)} %copy-done.14, bf16[512,1024]{1,0:T(8,128)(2,1)} %copy-done.34, bf16[512,1024]{1,0:T(8,128)(2,1)} %copy-done.33), kind=kOutput, calls=%fused_computation.274 | convolution fusion | flops 1630797824 | bytes 5242880 | tf_op jit(solution)/shard_map/dot_general | solution.py:64
  161.1 1.8 fusion.96
  164.4 3.6 %subtract_select_fusion = f32[1024,512]{1,0:T(8,128)} fusion(f32[1024,512]{1,0:T(8,128)S(1)} %get-tuple-element.100, f32[1024,512]{1,0:T(8,128)S(1)} %fusion.96, f32[512]{0:T(512)S(1)} %dynamic_slice.29, f32[1024]{0:T(1024)S(1)} %copy-done.43, pred[]{:T(512)S(6)} %eq.39, bf16[512,512]{1,0:T(8,128)(2,1)S(1)} %get-tuple-element.67, ...), kind=kOutput, calls=%fused_computation.18 | convolution fusion | flops 1630535680 | bytes 9443329 | tf_op jit(solution)/shard_map/dot_general | solution.py:64
  168.0 4.4 %all-to-all-start = ((f32[8,128,512]{2,1,0:T(8,128)}), f32[8,128,512]{2,1,0:T(8,128)S(1)}, u32[]{:S(2)}, u32[]{:S(2)}) async-start(f32[8,128,512]{2,1,0:T(8,128)} %bitcast.33), calls=%async_computation | async-start | bytes 4194304 | tf_op jit(solution)/shard_map/all_to_all | solution.py:222
  172.5 1.7 dynamic_slice.35.carried
  175.0 20.6 %all-to-all-done.terms = f32[8,128,512]{2,1,0:T(8,128)S(1)} async-done(((f32[8,128,512]{2,1,0:T(8,128)}), f32[8,128,512]{2,1,0:T(8,128)S(1)}, u32[]{:S(2)}, u32[]{:S(2)}) %all-to-all-start) | async-done | bytes 2097184 | tf_op jit(solution)/shard_map/all_to_all | solution.py:222
  196.9 3.8 %scan_along.1 = f32[8,128,512]{2,1,0:T(8,128)} custom-call(f32[8,128,512]{2,1,0:T(8,128)} %copy-done.1, f32[128,512]{1,0:T(8,128)} %add_divide_fusion.decay, f32[128,512]{1,0:T(8,128)} %dynamic_slice.35.carried), custom_call_target="tpu_custom_call" | custom-call | tf_op jit(solution)/shard_map/scan_along/pallas_call | solution.py:84
  200.8 32.4 %all_to_all.18 = f32[8,128,512]{2,1,0:T(8,128)S(1)} all-to-all(f32[8,128,512]{2,1,0:T(8,128)} %scan_along.1), channel_id=1, replica_groups={{1,2,9,10,17,18,25,26},{5,6,13,14,21,22,29,30},{0,4,8,12,16,20,24,28},{..., dimensions={0} | all-to-all | bytes 4194304 | tf_op jit(solution)/shard_map/all_to_all | solution.py:225
  234.7 1.8 fusion.157
  236.6 1.8 fusion.44
  245.0 2.1 add_add_fusion.2
  248.6 1.8 fusion.42
  250.5 1.6 collective-permute-start.27
  252.2 1.6 collective-permute-start.26
  253.8 1.6 collective-permute-start.24
  255.4 1.6 collective-permute-start.25
  257.1 1.8 fusion.161
  258.9 1.8 fusion.108
  260.9 2.1 fusion.39
  263.0 1.8 fusion.165
  264.9 1.8 fusion.40
  269.7 2.0 convolution_add_fusion
  271.7 1.7 collective-permute-start.28
  273.3 2.0 convolution_add_fusion.1
  276.6 1.8 select_select_fusion
  278.5 3.7 %collective-permute-done.25 = f32[256,1024]{1,0:T(8,128)} collective-permute-done((f32[256,1024]{1,0:T(8,128)}, f32[256,1024]{1,0:T(8,128)}, u32[]{:S(2)}, u32[]{:S(2)}) %collective-permute-start.25) | collective-permute-done | bytes 1048608 | tf_op jit(solution)/shard_map/ppermute | solution.py:157
  282.2 2.8 select_select_fusion.1
  285.0 42.2 %collective-permute-done.29 = f32[256,1024]{1,0:T(8,128)} collective-permute-done((f32[256,1024]{1,0:T(8,128)}, f32[256,1024]{1,0:T(8,128)}, u32[]{:S(2)}, u32[]{:S(2)}) %collective-permute-start.29) | collective-permute-done | bytes 1048608 | tf_op jit(solution)/shard_map/ppermute | solution.py:157
  327.2 2.5 select_bitcast_fusion
  (204 shorter events, 49.2 us)
Async XLA Ops:
  0.6 18.2 %copy-start.4 = (f32[256,1024]{1,0:T(8,128)S(1)}, f32[256,1024]{1,0:T(8,128)}, u32[]{:S(2)}) copy-start(f32[256,1024]{1,0:T(8,128)} %param.7) | copy-start | bytes 3145732
  0.6 18.2 %copy-start.5 = (f32[1,256,1024]{2,1,0:T(8,128)S(1)}, f32[1,256,1024]{2,1,0:T(8,128)}, u32[]{:S(2)}) copy-start(f32[1,256,1024]{2,1,0:T(8,128)} %param.9) | copy-start | bytes 3145732
  3.1 11.2 %collective-permute-start = (f32[128,1024]{1,0:T(8,128)}, f32[128,1024]{1,0:T(8,128)S(1)}, u32[]{:S(2)}, u32[]{:S(2)}) collective-permute-start(f32[128,1024]{1,0:T(8,128)} %get-tuple-element.94), channel_id=1, source_target_pairs={{0,4},{4,8},{8,12},{12,16},{16,20},{20,24},{24,28},{1,5},{5,9},{9,... | collective-permute-start | bytes 1572872 | tf_op jit(solution)/shard_map/ppermute | solution.py:127
  6.8 12.0 %collective-permute-start.2 = (f32[128,1024]{1,0:T(8,128)}, f32[128,1024]{1,0:T(8,128)S(1)}, u32[]{:S(2)}, u32[]{:S(2)}) collective-permute-start(f32[128,1024]{1,0:T(8,128)} %get-tuple-element.95), channel_id=1, source_target_pairs={{0,4},{4,8},{8,12},{12,16},{16,20},{20,24},{24,28},{1,5},{5,9},{9,... | collective-permute-start | bytes 1572872 | tf_op jit(solution)/shard_map/ppermute | solution.py:127
  8.7 73.5 %collective-permute-start.8 = (f32[256,1024]{1,0:T(8,128)}, f32[256,1024]{1,0:T(8,128)}, u32[]{:S(2)}, u32[]{:S(2)}) collective-permute-start(f32[256,1024]{1,0:T(8,128)} %bitcast.36), channel_id=1, source_target_pairs={{0,1},{3,5},{4,2},{7,6},{8,9},{11,13},{12,10},{15,14},{16,17},{19,... | collective-permute-start | bytes 3145736 | tf_op jit(solution)/shard_map/ppermute | solution.py:157
  11.8 66.4 %collective-permute-start.9 = (f32[256,1024]{1,0:T(8,128)}, f32[256,1024]{1,0:T(8,128)}, u32[]{:S(2)}, u32[]{:S(2)}) collective-permute-start(f32[256,1024]{1,0:T(8,128)} %bitcast.37), channel_id=1, source_target_pairs={{2,5},{5,2},{10,13},{13,10},{18,21},{21,18},{26,29},{29,26}} | collective-permute-start | bytes 3145736 | tf_op jit(solution)/shard_map/ppermute | solution.py:157
  13.4 8.3 %copy-start = (f32[1024,1024]{1,0:T(8,128)S(1)}, f32[1024,1024]{1,0:T(8,128)}, u32[]{:S(2)}) copy-start(f32[1024,1024]{1,0:T(8,128)} %param.11) | copy-start | bytes 12582916
  15.8 10.6 %collective-permute-start.4 = (f32[128,1024]{1,0:T(8,128)S(1)}, f32[128,1024]{1,0:T(8,128)S(1)}, u32[]{:S(2)}, u32[]{:S(2)}) collective-permute-start(f32[128,1024]{1,0:T(8,128)S(1)} %bitcast_add_fusion.2), channel_id=1, source_target_pairs={{2,5},{5,2},{10,13},{13,10},{18,21},{21,18},{26,29},{29,26}} | collective-permute-start | bytes 1572872 | tf_op jit(solution)/shard_map/ppermute | solution.py:157
  18.9 6.1 %collective-permute-start.5 = (f32[128,1024]{1,0:T(8,128)S(1)}, f32[128,1024]{1,0:T(8,128)S(1)}, u32[]{:S(2)}, u32[]{:S(2)}) collective-permute-start(f32[128,1024]{1,0:T(8,128)S(1)} %bitcast_add_fusion.1), channel_id=1, source_target_pairs={{2,5},{5,2},{10,13},{13,10},{18,21},{21,18},{26,29},{29,26}} | collective-permute-start | bytes 1572872 | tf_op jit(solution)/shard_map/ppermute | solution.py:157
  19.6 39.5 %collective-permute-start.3 = (f32[128,1024]{1,0:T(8,128)S(1)}, f32[128,1024]{1,0:T(8,128)S(1)}, u32[]{:S(2)}, u32[]{:S(2)}) collective-permute-start(f32[128,1024]{1,0:T(8,128)S(1)} %bitcast_add_fusion.1), channel_id=1, source_target_pairs={{0,1},{3,5},{4,2},{7,6},{8,9},{11,13},{12,10},{15,14},{16,17},{19,... | collective-permute-start | bytes 1572872 | tf_op jit(solution)/shard_map/ppermute | solution.py:157
  22.4 106.2 %copy-start.12 = (bf16[1024,512]{1,0:T(8,128)(2,1)}, bf16[1024,512]{1,0:T(8,128)(2,1)S(1)}, u32[]{:S(2)}) copy-start(bf16[1024,512]{1,0:T(8,128)(2,1)S(1)} %get-tuple-element.25) | copy-start | bytes 3145732
  22.5 106.2 %copy-start.14 = (bf16[1024,512]{1,0:T(8,128)(2,1)}, bf16[1024,512]{1,0:T(8,128)(2,1)S(1)}, u32[]{:S(2)}) copy-start(bf16[1024,512]{1,0:T(8,128)(2,1)S(1)} %get-tuple-element.27) | copy-start | bytes 3145732
  22.5 129.2 %copy-start.16 = (bf16[1024,512]{1,0:T(8,128)(2,1)}, bf16[1024,512]{1,0:T(8,128)(2,1)S(1)}, u32[]{:S(2)}) copy-start(bf16[1024,512]{1,0:T(8,128)(2,1)S(1)} %get-tuple-element.24) | copy-start | bytes 3145732
  22.5 129.2 %copy-start.18 = (bf16[1024,512]{1,0:T(8,128)(2,1)}, bf16[1024,512]{1,0:T(8,128)(2,1)S(1)}, u32[]{:S(2)}) copy-start(bf16[1024,512]{1,0:T(8,128)(2,1)S(1)} %get-tuple-element.26) | copy-start | bytes 3145732
  23.2 117.2 %copy-start.8 = (bf16[512,1024]{0,1:T(8,128)(2,1)}, bf16[512,1024]{0,1:T(8,128)(2,1)S(1)}, u32[]{:S(2)}) copy-start(bf16[512,1024]{0,1:T(8,128)(2,1)S(1)} %get-tuple-element.17) | copy-start | bytes 3145732
  23.2 117.2 %copy-start.10 = (bf16[512,1024]{0,1:T(8,128)(2,1)}, bf16[512,1024]{0,1:T(8,128)(2,1)S(1)}, u32[]{:S(2)}) copy-start(bf16[512,1024]{0,1:T(8,128)(2,1)S(1)} %get-tuple-element.18) | copy-start | bytes 3145732
  23.2 126.7 %copy-start.6 = (bf16[512,1024]{0,1:T(8,128)(2,1)}, bf16[512,1024]{0,1:T(8,128)(2,1)S(1)}, u32[]{:S(2)}) copy-start(bf16[512,1024]{0,1:T(8,128)(2,1)S(1)} %get-tuple-element.19) | copy-start | bytes 3145732
  24.0 106.4 %copy-start.21 = (bf16[1024,512]{0,1:T(8,128)(2,1)}, bf16[1024,512]{0,1:T(8,128)(2,1)S(1)}, u32[]{:S(2)}) copy-start(bf16[1024,512]{0,1:T(8,128)(2,1)S(1)} %get-tuple-element.50) | copy-start | bytes 3145732
  24.0 106.4 %copy-start.24 = (bf16[1024,512]{0,1:T(8,128)(2,1)}, bf16[1024,512]{0,1:T(8,128)(2,1)S(1)}, u32[]{:S(2)}) copy-start(bf16[1024,512]{0,1:T(8,128)(2,1)S(1)} %get-tuple-element.51) | copy-start | bytes 3145732
  25.0 109.6 %copy-start.39 = (bf16[512,1024]{1,0:T(8,128)(2,1)}, bf16[512,1024]{1,0:T(8,128)(2,1)S(1)}, u32[]{:S(2)}) copy-start(bf16[512,1024]{1,0:T(8,128)(2,1)S(1)} %get-tuple-element.105) | copy-start | bytes 3145732
  25.0 109.6 %copy-start.41 = (bf16[512,1024]{1,0:T(8,128)(2,1)}, bf16[512,1024]{1,0:T(8,128)(2,1)S(1)}, u32[]{:S(2)}) copy-start(bf16[512,1024]{1,0:T(8,128)(2,1)S(1)} %get-tuple-element.106) | copy-start | bytes 3145732
  25.0 111.5 %copy-start.35 = (bf16[512,1024]{1,0:T(8,128)(2,1)}, bf16[512,1024]{1,0:T(8,128)(2,1)S(1)}, u32[]{:S(2)}) copy-start(bf16[512,1024]{1,0:T(8,128)(2,1)S(1)} %get-tuple-element.42) | copy-start | bytes 3145732
  25.0 111.5 %copy-start.37 = (bf16[512,1024]{1,0:T(8,128)(2,1)}, bf16[512,1024]{1,0:T(8,128)(2,1)S(1)}, u32[]{:S(2)}) copy-start(bf16[512,1024]{1,0:T(8,128)(2,1)S(1)} %get-tuple-element.43) | copy-start | bytes 3145732
  25.0 34.1 %collective-permute-start.1 = (f32[128,1024]{1,0:T(8,128)S(1)}, f32[128,1024]{1,0:T(8,128)S(1)}, u32[]{:S(2)}, u32[]{:S(2)}) collective-permute-start(f32[128,1024]{1,0:T(8,128)S(1)} %bitcast_add_fusion.2), channel_id=1, source_target_pairs={{0,1},{3,5},{4,2},{7,6},{8,9},{11,13},{12,10},{15,14},{16,17},{19,... | collective-permute-start | bytes 1572872 | tf_op jit(solution)/shard_map/ppermute | solution.py:157
  26.4 63.6 %collective-permute-start.12 = (f32[256,1024]{1,0:T(8,128)S(1)}, f32[256,1024]{1,0:T(8,128)S(1)}, u32[]{:S(2)}, u32[]{:S(2)}) collective-permute-start(f32[256,1024]{1,0:T(8,128)S(1)} %bitcast.34), channel_id=1, source_target_pairs={{4,0},{8,4},{12,8},{16,12},{20,16},{24,20},{28,24},{5,1},{9,5},{13... | collective-permute-start | bytes 3145736 | tf_op jit(solution)/shard_map/ppermute | solution.py:202
  61.3 8.3 %collective-permute-start.6 = (f32[512,512]{1,0:T(8,128)S(1)}, f32[512,512]{1,0:T(8,128)S(1)}, u32[]{:S(2)}, u32[]{:S(2)}) collective-permute-start(f32[512,512]{1,0:T(8,128)S(1)} %fusion.58), channel_id=1, source_target_pairs={{0,4},{4,0},{8,12},{12,8},{16,20},{20,16},{24,28},{28,24},{1,5},{5... | collective-permute-start | bytes 3145736 | tf_op jit(solution)/shard_map/ppermute | solution.py:154
  65.9 66.5 %copy-start.27 = (bf16[1024,512]{0,1:T(8,128)(2,1)}, bf16[1024,512]{0,1:T(8,128)(2,1)S(1)}, u32[]{:S(2)}) copy-start(bf16[1024,512]{0,1:T(8,128)(2,1)S(1)} %get-tuple-element.48) | copy-start | bytes 3145732
  65.9 66.5 %copy-start.30 = (bf16[1024,512]{0,1:T(8,128)(2,1)}, bf16[1024,512]{0,1:T(8,128)(2,1)S(1)}, u32[]{:S(2)}) copy-start(bf16[1024,512]{0,1:T(8,128)(2,1)S(1)} %get-tuple-element.49) | copy-start | bytes 3145732
  73.7 4.2 %collective-permute-start.7 = (f32[512,512]{1,0:T(8,128)S(1)}, f32[512,512]{1,0:T(8,128)S(1)}, u32[]{:S(2)}, u32[]{:S(2)}) collective-permute-start(f32[512,512]{1,0:T(8,128)S(1)} %fusion.56), channel_id=1, source_target_pairs={{0,4},{4,0},{8,12},{12,8},{16,20},{20,16},{24,28},{28,24},{1,5},{5... | collective-permute-start | bytes 3145736 | tf_op jit(solution)/shard_map/ppermute | solution.py:154
  87.5 12.1 %collective-permute-start.10 = (f32[512,512]{1,0:T(8,128)S(1)}, f32[512,512]{1,0:T(8,128)S(1)}, u32[]{:S(2)}, u32[]{:S(2)}) collective-permute-start(f32[512,512]{1,0:T(8,128)S(1)} %fusion.54), channel_id=1, source_target_pairs={{0,4},{4,0},{8,12},{12,8},{16,20},{20,16},{24,28},{28,24},{1,5},{5... | collective-permute-start | bytes 3145736 | tf_op jit(solution)/shard_map/ppermute | solution.py:154
  88.1 34.1 %collective-permute-start.17 = (f32[256,1024]{1,0:T(8,128)S(1)}, f32[256,1024]{1,0:T(8,128)S(1)}, u32[]{:S(2)}, u32[]{:S(2)}) collective-permute-start(f32[256,1024]{1,0:T(8,128)S(1)} %bitcast.38), channel_id=1, source_target_pairs={{4,0},{8,4},{12,8},{16,12},{20,16},{24,20},{28,24},{5,1},{9,5},{13... | collective-permute-start | bytes 3145736 | tf_op jit(solution)/shard_map/ppermute | solution.py:203
  90.0 23.4 %copy-start.46 = (f32[256,1024]{1,0:T(8,128)}, f32[256,1024]{1,0:T(8,128)S(1)}, u32[]{:S(2)}) copy-start(f32[256,1024]{1,0:T(8,128)S(1)} %collective-permute-done.12) | copy-start | bytes 3145732
  90.1 27.5 %collective-permute-start.13 = (f32[256,1024]{1,0:T(8,128)S(1)}, f32[256,1024]{1,0:T(8,128)S(1)}, u32[]{:S(2)}, u32[]{:S(2)}) collective-permute-start(f32[256,1024]{1,0:T(8,128)S(1)} %collective-permute-done.12), channel_id=1, source_target_pairs={{0,1},{3,5},{4,2},{7,6},{8,9},{11,13},{12,10},{15,14},{16,17},{19,... | collective-permute-start | bytes 3145736 | tf_op jit(solution)/shard_map/ppermute | solution.py:157
  95.1 18.3 %collective-permute-start.14 = (f32[256,1024]{1,0:T(8,128)S(1)}, f32[256,1024]{1,0:T(8,128)S(1)}, u32[]{:S(2)}, u32[]{:S(2)}) collective-permute-start(f32[256,1024]{1,0:T(8,128)S(1)} %collective-permute-done.12), channel_id=1, source_target_pairs={{2,5},{5,2},{10,13},{13,10},{18,21},{21,18},{26,29},{29,26}} | collective-permute-start | bytes 3145736 | tf_op jit(solution)/shard_map/ppermute | solution.py:157
  102.9 61.5 %copy-start.2 = (f32[1024,512]{1,0:T(8,128)}, f32[1024,512]{1,0:T(8,128)S(1)}, u32[]{:S(2)}) copy-start(f32[1024,512]{1,0:T(8,128)S(1)} %get-tuple-element.100) | copy-start | bytes 6291460
  103.9 3.5 %copy-start.53 = (bf16[1024,512]{1,0:T(8,128)(2,1)S(1)}, bf16[1024,512]{1,0:T(8,128)(2,1)}, u32[]{:S(2)}) copy-start(bf16[1024,512]{1,0:T(8,128)(2,1)} %get-tuple-element.39) | copy-start | bytes 3145732
  110.4 2.7 collective-permute-start.11
  121.3 11.0 %collective-permute-start.15 = (f32[512,512]{1,0:T(8,128)S(1)}, f32[512,512]{1,0:T(8,128)S(1)}, u32[]{:S(2)}, u32[]{:S(2)}) collective-permute-start(f32[512,512]{1,0:T(8,128)S(1)} %fusion.50), channel_id=1, source_target_pairs={{0,4},{4,0},{8,12},{12,8},{16,20},{20,16},{24,28},{28,24},{1,5},{5... | collective-permute-start | bytes 3145736 | tf_op jit(solution)/shard_map/ppermute | solution.py:154
  122.2 27.5 %collective-permute-start.18 = (f32[256,1024]{1,0:T(8,128)S(1)}, f32[256,1024]{1,0:T(8,128)S(1)}, u32[]{:S(2)}, u32[]{:S(2)}) collective-permute-start(f32[256,1024]{1,0:T(8,128)S(1)} %collective-permute-done.17), channel_id=1, source_target_pairs={{0,1},{3,5},{4,2},{7,6},{8,9},{11,13},{12,10},{15,14},{16,17},{19,... | collective-permute-start | bytes 3145736 | tf_op jit(solution)/shard_map/ppermute | solution.py:157
  127.9 23.0 %collective-permute-start.19 = (f32[256,1024]{1,0:T(8,128)S(1)}, f32[256,1024]{1,0:T(8,128)S(1)}, u32[]{:S(2)}, u32[]{:S(2)}) collective-permute-start(f32[256,1024]{1,0:T(8,128)S(1)} %collective-permute-done.17), channel_id=1, source_target_pairs={{2,5},{5,2},{10,13},{13,10},{18,21},{21,18},{26,29},{29,26}} | collective-permute-start | bytes 3145736 | tf_op jit(solution)/shard_map/ppermute | solution.py:157
  138.2 3.2 collective-permute-start.16
  154.7 8.3 %collective-permute-start.20 = (f32[512,512]{1,0:T(8,128)}, f32[512,512]{1,0:T(8,128)}, u32[]{:S(2)}, u32[]{:S(2)}) collective-permute-start(f32[512,512]{1,0:T(8,128)} %fusion.46), channel_id=1, source_target_pairs={{0,4},{4,0},{8,12},{12,8},{16,20},{20,16},{24,28},{28,24},{1,5},{5... | collective-permute-start | bytes 3145736 | tf_op jit(solution)/shard_map/ppermute | solution.py:154
  156.2 4.9 %copy-start.22 = (bf16[1024,512]{0,1:T(8,128)(2,1)S(1)}, bf16[1024,512]{0,1:T(8,128)(2,1)}, u32[]{:S(2)}) copy-start(bf16[1024,512]{0,1:T(8,128)(2,1)} %copy-done.21) | copy-start | bytes 3145732
  156.2 4.9 %copy-start.25 = (bf16[1024,512]{0,1:T(8,128)(2,1)S(1)}, bf16[1024,512]{0,1:T(8,128)(2,1)}, u32[]{:S(2)}) copy-start(bf16[1024,512]{0,1:T(8,128)(2,1)} %copy-done.24) | copy-start | bytes 3145732
  161.1 3.2 copy-start.28
  161.1 3.2 copy-start.31
  168.0 27.6 %all-to-all-start = ((f32[8,128,512]{2,1,0:T(8,128)}), f32[8,128,512]{2,1,0:T(8,128)S(1)}, u32[]{:S(2)}, u32[]{:S(2)}) async-start(f32[8,128,512]{2,1,0:T(8,128)} %bitcast.33), calls=%async_computation | async-start | bytes 4194304 | tf_op jit(solution)/shard_map/all_to_all | solution.py:222
  200.8 32.4 %copy-start.3 = (f32[1024,512]{1,0:T(8,128)S(1)}, f32[1024,512]{1,0:T(8,128)}, u32[]{:S(2)}) copy-start(f32[1024,512]{1,0:T(8,128)} %copy-done.2) | copy-start | bytes 6291460
  236.6 3.2 copy-start.9
  236.6 3.2 copy-start.11
  238.4 3.6 %collective-permute-start.21 = (f32[512,512]{1,0:T(8,128)S(1)}, f32[512,512]{1,0:T(8,128)S(1)}, u32[]{:S(2)}, u32[]{:S(2)}) collective-permute-start(f32[512,512]{1,0:T(8,128)S(1)} %fusion.44), channel_id=1, source_target_pairs={{0,4},{4,0},{8,12},{12,8},{16,20},{20,16},{24,28},{28,24},{1,5},{5... | collective-permute-start | bytes 3145736 | tf_op jit(solution)/shard_map/ppermute | solution.py:154
  248.6 3.5 %copy-start.20 = (f32[256,1024]{1,0:T(8,128)S(1)}, f32[256,1024]{1,0:T(8,128)}, u32[]{:S(2)}) copy-start(f32[256,1024]{1,0:T(8,128)} %get-tuple-element.11) | copy-start | bytes 3145732
  248.6 8.4 %copy-start.13 = (bf16[1024,512]{1,0:T(8,128)(2,1)S(1)}, bf16[1024,512]{1,0:T(8,128)(2,1)}, u32[]{:S(2)}) copy-start(bf16[1024,512]{1,0:T(8,128)(2,1)} %copy-done.12) | copy-start | bytes 3145732
  248.6 8.4 %copy-start.15 = (bf16[1024,512]{1,0:T(8,128)(2,1)S(1)}, bf16[1024,512]{1,0:T(8,128)(2,1)}, u32[]{:S(2)}) copy-start(bf16[1024,512]{1,0:T(8,128)(2,1)} %copy-done.14) | copy-start | bytes 3145732
  250.4 10.3 %collective-permute-start.22 = (f32[512,512]{1,0:T(8,128)S(1)}, f32[512,512]{1,0:T(8,128)S(1)}, u32[]{:S(2)}, u32[]{:S(2)}) collective-permute-start(f32[512,512]{1,0:T(8,128)S(1)} %fusion.42), channel_id=1, source_target_pairs={{0,4},{4,0},{8,12},{12,8},{16,20},{20,16},{24,28},{28,24},{1,5},{5... | collective-permute-start | bytes 3145736 | tf_op jit(solution)/shard_map/ppermute | solution.py:154
  250.5 24.8 %collective-permute-start.27 = (f32[256,1024]{1,0:T(8,128)S(1)}, f32[256,1024]{1,0:T(8,128)}, u32[]{:S(2)}, u32[]{:S(2)}) collective-permute-start(f32[256,1024]{1,0:T(8,128)S(1)} %copy-done.45), channel_id=1, source_target_pairs={{1,0},{5,3}} | collective-permute-start | bytes 3145736 | tf_op jit(solution)/shard_map/ppermute | solution.py:157
  252.2 24.5 %collective-permute-start.26 = (f32[256,1024]{1,0:T(8,128)S(1)}, f32[256,1024]{1,0:T(8,128)}, u32[]{:S(2)}, u32[]{:S(2)}) collective-permute-start(f32[256,1024]{1,0:T(8,128)S(1)} %copy-done.20), channel_id=1, source_target_pairs={{5,2}} | collective-permute-start | bytes 3145736 | tf_op jit(solution)/shard_map/ppermute | solution.py:157
  253.8 24.7 %collective-permute-start.24 = (f32[256,1024]{1,0:T(8,128)S(1)}, f32[256,1024]{1,0:T(8,128)}, u32[]{:S(2)}, u32[]{:S(2)}) collective-permute-start(f32[256,1024]{1,0:T(8,128)S(1)} %get-tuple-element.10), channel_id=1, source_target_pairs={{5,2},{2,5},{13,10},{10,13},{21,18},{18,21},{29,26},{26,29}} | collective-permute-start | bytes 3145736 | tf_op jit(solution)/shard_map/ppermute | solution.py:157
  255.4 3.5 %copy-start.23 = (bf16[1024,512]{0,1:T(8,128)(2,1)S(1)}, bf16[1024,512]{0,1:T(8,128)(2,1)}, u32[]{:S(2)}) copy-start(bf16[1024,512]{0,1:T(8,128)(2,1)} %copy-done.21) | copy-start | bytes 3145732
  255.4 3.5 %copy-start.26 = (bf16[1024,512]{0,1:T(8,128)(2,1)S(1)}, bf16[1024,512]{0,1:T(8,128)(2,1)}, u32[]{:S(2)}) copy-start(bf16[1024,512]{0,1:T(8,128)(2,1)} %copy-done.24) | copy-start | bytes 3145732
  255.4 26.7 %collective-permute-start.25 = (f32[256,1024]{1,0:T(8,128)}, f32[256,1024]{1,0:T(8,128)}, u32[]{:S(2)}, u32[]{:S(2)}) collective-permute-start(f32[256,1024]{1,0:T(8,128)} %get-tuple-element.104), channel_id=1, source_target_pairs={{1,0},{5,3},{2,4},{6,7},{9,8},{13,11},{10,12},{14,15},{17,16},{21,... | collective-permute-start | bytes 3145736 | tf_op jit(solution)/shard_map/ppermute | solution.py:157
  266.7 2.7 collective-permute-start.23
  271.7 13.3 %collective-permute-start.28 = (f32[256,1024]{1,0:T(8,128)}, f32[256,1024]{1,0:T(8,128)}, u32[]{:S(2)}, u32[]{:S(2)}) collective-permute-start(f32[256,1024]{1,0:T(8,128)} %convolution_add_fusion), channel_id=1, source_target_pairs={{1,5},{5,6},{2,9},{6,10},{9,13},{13,14},{10,17},{14,18},{17,21},{2... | collective-permute-start | bytes 3145736 | tf_op jit(solution)/shard_map/ppermute | solution.py:157
  275.3 51.9 %collective-permute-start.29 = (f32[256,1024]{1,0:T(8,128)}, f32[256,1024]{1,0:T(8,128)}, u32[]{:S(2)}, u32[]{:S(2)}) collective-permute-start(f32[256,1024]{1,0:T(8,128)} %convolution_add_fusion.1), channel_id=1, source_target_pairs={{1,4},{5,7},{2,8},{6,11},{9,12},{13,15},{10,16},{14,19},{17,20},{2... | collective-permute-start | bytes 3145736 | tf_op jit(solution)/shard_map/ppermute | solution.py:157
  (21 other events, 34.8 us)

commit v3 on v2

--- a/solution.py
+++ b/solution.py
@@ -2,6 +2,7 @@
 import jax.numpy as jnp
 from jax import lax
 from jax.experimental import pallas as pl
+from jax.experimental.pallas import tpu as pltpu
 from jax.sharding import PartitionSpec as P
 
 
@@ -69,24 +70,30 @@
 
 
 def scan_kernel(terms, decay, carried, out):
-    state = decay[...] * carried[...]
-    out[0] = state
-    for k in range(1, out.shape[0]):
-        state = decay[...] * state + terms[k - 1]
-        out[k] = state
+    count, rows, _ = out.shape
+    step = min(rows, 16)
+
+    def body(i, _):
+        at = pl.ds(i * step, step)
+        factor = decay[at]
+        state = factor * carried[at]
+        out[0, at] = state
+        for k in range(1, count):
+            state = factor * state + terms[k - 1, at]
+            out[k, at] = state
+        return 0
+
+    lax.fori_loop(0, rows // step, body, 0)
 
 
 def scan_along(terms, decay, carried):
-    chains, rows, columns = terms.shape
-    step = min(rows, 32)
-    deep = pl.BlockSpec((chains, step, columns), lambda i: (0, i, 0))
-    flat = pl.BlockSpec((step, columns), lambda i: (i, 0))
+    whole = pl.BlockSpec(memory_space=pltpu.VMEM)
     return pl.pallas_call(
         scan_kernel,
-        grid=(rows // step,),
-        in_specs=[deep, flat, flat],
-        out_specs=deep,
+        in_specs=[whole] * 3,
+        out_specs=whole,
         out_shape=jax.ShapeDtypeStruct(terms.shape, terms.dtype),
+        compiler_params=pltpu.CompilerParams(vmem_limit_bytes=4 * terms.size * 2 + (4 << 20)),
         name="scan_along",
     )(terms, decay, carried)
 
@@ -132,7 +139,9 @@
             before, _ = lax.optimization_barrier((before, started[-1]))
         before = jnp.where(t == 0, initial_state[rows], before)
         started.append(reaction(before) + source_fine[rows])
-    eigen_basis, _ = lax.optimization_barrier((eigen_basis, started[0]))
+    eigen_basis, eigen_rates, carried_correction, _ = lax.optimization_barrier(
+        (eigen_basis, eigen_rates, carried_correction, started[0])
+    )
     rows_mine = rows_of(eigen_basis, h)
     rows_other = rows_of(eigen_basis, 1 - h)
     cols_mine = lax.dynamic_slice_in_dim(eigen_basis, mine, half, 1)

time: 335 us -> 329 us (0.982)
  waiting for transfers between devices: 79.4 us -> 85.1 us
  Pallas kernels: 3.83 us -> 0.19 us
  local copies, waits for them, and re-layouts: 12.5 us -> 9 us
    pallas_call x1, Pallas kernels: 3.83 us -> 0.19 us  [scan_along(): pl.pallas_call(scan_kernel, in_specs=[whole] * 3, out_specs=whole, out_sh...]
    ppermute x16, waiting for transfers between devices: 55.9 us -> 59.4 us  [sent(): return lax.ppermute(x, both, [(a, b) for a, b in pairs if a != b])]
  transfers between devices with their start and end apart: 31 -> 31, of which waited for: 9 -> 9; matrix products, arithmetic and copies ran while one was open for 29% -> 28% of each run, Pallas kernels for 0% -> 0%
where the time goes in v3:
time: 329 us; the launch traced here: 325 us
  matrix products  92.6 us (28%)
  starting transfers between devices  85.2 us (26%)
  waiting for transfers between devices  85.1 us (26%)
  blocking collectives  31.3 us (10%)
  other arithmetic  19 us (6%)
  local copies, waits for them, and re-layouts  9 us (3%)
    dot_general x50, matrix products, dot(): return jnp.dot(left, right, preferred_element_type=jnp.float32)  92.6 us
    ppermute x16, waiting for transfers between devices, sent(): return lax.ppermute(x, both, [(a, b) for a, b in pairs if a != b])  59.4 us
    ppermute x1, starting transfers between devices, on_device(): lax.ppermute(source_fine, 'tm', [(g + 1, g) for g in range(groups - 1)])  32.6 us
    all_to_all x1, blocking collectives, on_device(): lax.all_to_all(states, both, 0, 0, axis_index_groups=rings, tiled=True)  31.3 us
    ppermute x16, starting transfers between devices, sent(): return lax.ppermute(x, both, [(a, b) for a, b in pairs if a != b])  30.4 us
    all_to_all x1, waiting for transfers between devices, on_device(): lax.all_to_all(term, both, 0, 0, axis_index_groups=rings, tiled=True)  22 us
    ppermute x10, starting transfers between devices, swap(): return lax.ppermute(x, 'tm', plan.partners())  10.1 us
    another operation x21, other arithmetic  8.69 us
  transfers between devices with their start and end apart: 31, of which 9 were waited for; matrix products, arithmetic and copies ran while one was open for 28% of the time, Pallas kernels for 0%

profile of v3, /device:TPU:25, one launch (start us, length us, event | category | flops | bytes accessed | tf_op | source)
XLA Modules:
  0.0 324.7 jit_solution(12400367265239078879)
XLA Ops:
  0.7 2.4 slice_bitcast_fusion.1
  3.1 3.7 %collective-permute-start = (f32[128,1024]{1,0:T(8,128)}, f32[128,1024]{1,0:T(8,128)S(1)}, u32[]{:S(2)}, u32[]{:S(2)}) collective-permute-start(f32[128,1024]{1,0:T(8,128)} %get-tuple-element.98), channel_id=1, source_target_pairs={{0,4},{4,8},{8,12},{12,16},{16,20},{20,24},{24,28},{1,5},{5,9},{9,... | collective-permute-start | bytes 1572872 | tf_op jit(solution)/shard_map/ppermute | solution.py:134
  6.8 1.9 collective-permute-start.2
  8.7 3.1 collective-permute-start.8
  11.8 1.6 collective-permute-start.9
  13.4 1.5 bitcast_add_fusion.2
  15.7 3.1 collective-permute-done.2
  19.6 2.1 collective-permute-start.3
  26.4 32.6 %collective-permute-start.12 = (f32[256,1024]{1,0:T(8,128)S(1)}, f32[256,1024]{1,0:T(8,128)S(1)}, u32[]{:S(2)}, u32[]{:S(2)}) collective-permute-start(f32[256,1024]{1,0:T(8,128)S(1)} %bitcast.34), channel_id=1, source_target_pairs={{4,0},{8,4},{12,8},{16,12},{20,16},{24,20},{28,24},{5,1},{9,5},{13... | collective-permute-start | bytes 3145736 | tf_op jit(solution)/shard_map/ppermute | solution.py:211
  59.5 1.8 fusion.58
  61.3 4.1 %collective-permute-start.6 = (f32[512,512]{1,0:T(8,128)S(1)}, f32[512,512]{1,0:T(8,128)S(1)}, u32[]{:S(2)}, u32[]{:S(2)}) collective-permute-start(f32[512,512]{1,0:T(8,128)S(1)} %fusion.58), channel_id=1, source_target_pairs={{0,4},{4,0},{8,12},{12,8},{16,20},{20,16},{24,28},{28,24},{1,5},{5... | collective-permute-start | bytes 3145736 | tf_op jit(solution)/shard_map/ppermute | solution.py:163
  66.0 1.8 fusion.129
  67.8 1.8 fusion.60
  69.9 2.1 fusion.17
  72.0 1.8 fusion.56
  73.9 1.8 fusion.133
  79.2 3.1 select_add_fusion.1
  82.4 3.1 add_add_fusion.6
  85.9 1.8 fusion.54
  88.2 2.0 collective-permute-start.17
  90.2 4.9 %collective-permute-start.13 = (f32[256,1024]{1,0:T(8,128)S(1)}, f32[256,1024]{1,0:T(8,128)S(1)}, u32[]{:S(2)}, u32[]{:S(2)}) collective-permute-start(f32[256,1024]{1,0:T(8,128)S(1)} %collective-permute-done.12), channel_id=1, source_target_pairs={{0,1},{3,5},{4,2},{7,6},{8,9},{11,13},{12,10},{15,14},{16,17},{19,... | collective-permute-start | bytes 3145736 | tf_op jit(solution)/shard_map/ppermute | solution.py:166
  96.0 1.8 fusion.137
  97.8 1.8 fusion.72
  99.9 3.1 fusion.27
  102.9 4.2 %fusion.141 = (bf16[512,512]{0,1:T(8,128)(2,1)S(1)}, bf16[512,512]{0,1:T(8,128)(2,1)S(1)}) fusion(bf16[1024,512]{1,0:T(8,128)(2,1)} %get-tuple-element.43, bf16[1024,512]{1,0:T(8,128)(2,1)S(1)} %get-tuple-element.42, bf16[512,1024]{1,0:T(8,128)(2,1)S(1)} %get-tuple-element.109, bf16[512,1024]{1,0:T(8,128)(2,1)S(1)} %get-tuple-element.110), kind=kOutput, calls=%fused_computation.262 | convolution fusion | flops 1630797824 | bytes 5242880 | tf_op jit(solution)/shard_map/dot_general | solution.py:65
  107.1 1.8 fusion.52
  113.1 4.5 %collective-permute-done.13 = f32[256,1024]{1,0:T(8,128)S(1)} collective-permute-done((f32[256,1024]{1,0:T(8,128)S(1)}, f32[256,1024]{1,0:T(8,128)S(1)}, u32[]{:S(2)}, u32[]{:S(2)}) %collective-permute-start.13) | collective-permute-done | bytes 1048608 | tf_op jit(solution)/shard_map/ppermute | solution.py:166
  119.1 2.2 fusion.50
  122.2 5.7 %collective-permute-start.18 = (f32[256,1024]{1,0:T(8,128)S(1)}, f32[256,1024]{1,0:T(8,128)S(1)}, u32[]{:S(2)}, u32[]{:S(2)}) collective-permute-start(f32[256,1024]{1,0:T(8,128)S(1)} %collective-permute-done.17), channel_id=1, source_target_pairs={{0,1},{3,5},{4,2},{7,6},{8,9},{11,13},{12,10},{15,14},{16,17},{19,... | collective-permute-start | bytes 3145736 | tf_op jit(solution)/shard_map/ppermute | solution.py:166
  128.6 1.8 fusion.145
  130.5 1.8 fusion.84
  132.5 2.1 fusion.31
  134.6 1.8 fusion.149
  136.5 1.8 fusion.48
  142.8 6.9 %collective-permute-done.18 = f32[256,1024]{1,0:T(8,128)S(1)} collective-permute-done((f32[256,1024]{1,0:T(8,128)S(1)}, f32[256,1024]{1,0:T(8,128)S(1)}, u32[]{:S(2)}, u32[]{:S(2)}) %collective-permute-start.18) | collective-permute-done | bytes 1048608 | tf_op jit(solution)/shard_map/ppermute | solution.py:166
  151.9 3.0 fusion.46
  154.8 1.5 collective-permute-start.20
  156.3 4.4 %fusion.153 = (bf16[512,512]{1,0:T(8,128)(2,1)S(1)}, bf16[512,512]{1,0:T(8,128)(2,1)S(1)}) fusion(bf16[1024,512]{1,0:T(8,128)(2,1)S(1)} %get-tuple-element.29, bf16[1024,512]{1,0:T(8,128)(2,1)} %copy-done.15, bf16[512,1024]{1,0:T(8,128)(2,1)} %copy-done.35, bf16[512,1024]{1,0:T(8,128)(2,1)} %copy-done.34), kind=kOutput, calls=%fused_computation.274 | convolution fusion | flops 1630797824 | bytes 5242880 | tf_op jit(solution)/shard_map/dot_general | solution.py:65
  160.8 1.8 fusion.96
  162.6 1.4 fusion.155
  164.1 3.6 %subtract_select_fusion = f32[1024,512]{1,0:T(8,128)} fusion(f32[1024,512]{1,0:T(8,128)S(1)} %get-tuple-element.104, f32[1024,512]{1,0:T(8,128)S(1)} %fusion.96, f32[512]{0:T(512)S(1)} %dynamic_slice.29, f32[1024]{0:T(1024)S(1)} %copy-done.44, pred[]{:T(512)S(6)} %eq.39, bf16[512,512]{1,0:T(8,128)(2,1)S(1)} %get-tuple-element.71, ...), kind=kOutput, calls=%fused_computation.18 | convolution fusion | flops 1630535680 | bytes 9443329 | tf_op jit(solution)/shard_map/dot_general | solution.py:65
  167.7 4.4 %all-to-all-start = ((f32[8,128,512]{2,1,0:T(8,128)}), f32[8,128,512]{2,1,0:T(8,128)S(1)}, u32[]{:S(2)}, u32[]{:S(2)}) async-start(f32[8,128,512]{2,1,0:T(8,128)} %bitcast.33), calls=%async_computation | async-start | bytes 4194304 | tf_op jit(solution)/shard_map/all_to_all | solution.py:231
  173.3 22.0 %all-to-all-done.terms = f32[8,128,512]{2,1,0:T(8,128)S(1)} async-done(((f32[8,128,512]{2,1,0:T(8,128)}), f32[8,128,512]{2,1,0:T(8,128)S(1)}, u32[]{:S(2)}, u32[]{:S(2)}) %all-to-all-start) | async-done | bytes 2097184 | tf_op jit(solution)/shard_map/all_to_all | solution.py:231
  195.5 31.3 %all_to_all.18 = f32[8,128,512]{2,1,0:T(8,128)S(1)} all-to-all(f32[8,128,512]{2,1,0:T(8,128)S(1)} %scan_along.1), channel_id=1, replica_groups={{1,2,9,10,17,18,25,26},{5,6,13,14,21,22,29,30},{0,4,8,12,16,20,24,28},{..., dimensions={0} | all-to-all | bytes 4194304 | tf_op jit(solution)/shard_map/all_to_all | solution.py:234
  228.4 1.8 fusion.157
  230.3 1.8 fusion.44
  239.0 2.1 add_add_fusion.2
  242.6 1.8 fusion.42
  244.5 1.6 collective-permute-start.27
  246.1 1.6 collective-permute-start.26
  248.5 1.6 collective-permute-start.25
  250.2 1.8 fusion.161
  252.0 1.8 fusion.108
  254.0 2.1 fusion.39
  256.1 1.8 fusion.165
  258.0 1.8 fusion.40
  262.8 2.0 convolution_add_fusion
  264.8 1.6 collective-permute-start.28
  266.4 2.0 convolution_add_fusion.1
  269.8 1.8 select_select_fusion
  271.6 5.4 %collective-permute-done.25 = f32[256,1024]{1,0:T(8,128)} collective-permute-done((f32[256,1024]{1,0:T(8,128)}, f32[256,1024]{1,0:T(8,128)}, u32[]{:S(2)}, u32[]{:S(2)}) %collective-permute-start.25) | collective-permute-done | bytes 1048608 | tf_op jit(solution)/shard_map/ppermute | solution.py:166
  277.0 2.5 select_select_fusion.1
  279.5 42.6 %collective-permute-done.29 = f32[256,1024]{1,0:T(8,128)} collective-permute-done((f32[256,1024]{1,0:T(8,128)}, f32[256,1024]{1,0:T(8,128)}, u32[]{:S(2)}, u32[]{:S(2)}) %collective-permute-start.29) | collective-permute-done | bytes 1048608 | tf_op jit(solution)/shard_map/ppermute | solution.py:166
  322.0 2.5 select_bitcast_fusion
  (204 shorter events, 43.3 us)
Async XLA Ops:
  0.6 18.2 %copy-start.3 = (f32[256,1024]{1,0:T(8,128)S(1)}, f32[256,1024]{1,0:T(8,128)}, u32[]{:S(2)}) copy-start(f32[256,1024]{1,0:T(8,128)} %param.7) | copy-start | bytes 3145732
  0.6 18.2 %copy-start.4 = (f32[1,256,1024]{2,1,0:T(8,128)S(1)}, f32[1,256,1024]{2,1,0:T(8,128)}, u32[]{:S(2)}) copy-start(f32[1,256,1024]{2,1,0:T(8,128)} %param.9) | copy-start | bytes 3145732
  3.1 10.3 %collective-permute-start = (f32[128,1024]{1,0:T(8,128)}, f32[128,1024]{1,0:T(8,128)S(1)}, u32[]{:S(2)}, u32[]{:S(2)}) collective-permute-start(f32[128,1024]{1,0:T(8,128)} %get-tuple-element.98), channel_id=1, source_target_pairs={{0,4},{4,8},{8,12},{12,16},{16,20},{20,24},{24,28},{1,5},{5,9},{9,... | collective-permute-start | bytes 1572872 | tf_op jit(solution)/shard_map/ppermute | solution.py:134
  6.8 12.0 %collective-permute-start.2 = (f32[128,1024]{1,0:T(8,128)}, f32[128,1024]{1,0:T(8,128)S(1)}, u32[]{:S(2)}, u32[]{:S(2)}) collective-permute-start(f32[128,1024]{1,0:T(8,128)} %get-tuple-element.99), channel_id=1, source_target_pairs={{0,4},{4,8},{8,12},{12,16},{16,20},{20,24},{24,28},{1,5},{5,9},{9,... | collective-permute-start | bytes 1572872 | tf_op jit(solution)/shard_map/ppermute | solution.py:134
  8.7 73.7 %collective-permute-start.8 = (f32[256,1024]{1,0:T(8,128)}, f32[256,1024]{1,0:T(8,128)}, u32[]{:S(2)}, u32[]{:S(2)}) collective-permute-start(f32[256,1024]{1,0:T(8,128)} %bitcast.36), channel_id=1, source_target_pairs={{0,1},{3,5},{4,2},{7,6},{8,9},{11,13},{12,10},{15,14},{16,17},{19,... | collective-permute-start | bytes 3145736 | tf_op jit(solution)/shard_map/ppermute | solution.py:166
  11.8 66.5 %collective-permute-start.9 = (f32[256,1024]{1,0:T(8,128)}, f32[256,1024]{1,0:T(8,128)}, u32[]{:S(2)}, u32[]{:S(2)}) collective-permute-start(f32[256,1024]{1,0:T(8,128)} %bitcast.37), channel_id=1, source_target_pairs={{2,5},{5,2},{10,13},{13,10},{18,21},{21,18},{26,29},{29,26}} | collective-permute-start | bytes 3145736 | tf_op jit(solution)/shard_map/ppermute | solution.py:166
  13.4 8.3 %copy-start = (f32[1024,1024]{1,0:T(8,128)S(1)}, f32[1024,1024]{1,0:T(8,128)}, u32[]{:S(2)}) copy-start(f32[1024,1024]{1,0:T(8,128)} %param.11) | copy-start | bytes 12582916
  14.9 11.6 %collective-permute-start.4 = (f32[128,1024]{1,0:T(8,128)S(1)}, f32[128,1024]{1,0:T(8,128)S(1)}, u32[]{:S(2)}, u32[]{:S(2)}) collective-permute-start(f32[128,1024]{1,0:T(8,128)S(1)} %bitcast_add_fusion.2), channel_id=1, source_target_pairs={{2,5},{5,2},{10,13},{13,10},{18,21},{21,18},{26,29},{29,26}} | collective-permute-start | bytes 1572872 | tf_op jit(solution)/shard_map/ppermute | solution.py:166
  18.9 6.1 %collective-permute-start.5 = (f32[128,1024]{1,0:T(8,128)S(1)}, f32[128,1024]{1,0:T(8,128)S(1)}, u32[]{:S(2)}, u32[]{:S(2)}) collective-permute-start(f32[128,1024]{1,0:T(8,128)S(1)} %bitcast_add_fusion.1), channel_id=1, source_target_pairs={{2,5},{5,2},{10,13},{13,10},{18,21},{21,18},{26,29},{29,26}} | collective-permute-start | bytes 1572872 | tf_op jit(solution)/shard_map/ppermute | solution.py:166
  19.6 39.5 %collective-permute-start.3 = (f32[128,1024]{1,0:T(8,128)S(1)}, f32[128,1024]{1,0:T(8,128)S(1)}, u32[]{:S(2)}, u32[]{:S(2)}) collective-permute-start(f32[128,1024]{1,0:T(8,128)S(1)} %bitcast_add_fusion.1), channel_id=1, source_target_pairs={{0,1},{3,5},{4,2},{7,6},{8,9},{11,13},{12,10},{15,14},{16,17},{19,... | collective-permute-start | bytes 1572872 | tf_op jit(solution)/shard_map/ppermute | solution.py:166
  22.4 106.2 %copy-start.15 = (bf16[1024,512]{1,0:T(8,128)(2,1)}, bf16[1024,512]{1,0:T(8,128)(2,1)S(1)}, u32[]{:S(2)}) copy-start(bf16[1024,512]{1,0:T(8,128)(2,1)S(1)} %get-tuple-element.31) | copy-start | bytes 3145732
  22.4 129.4 %copy-start.17 = (bf16[1024,512]{1,0:T(8,128)(2,1)}, bf16[1024,512]{1,0:T(8,128)(2,1)S(1)}, u32[]{:S(2)}) copy-start(bf16[1024,512]{1,0:T(8,128)(2,1)S(1)} %get-tuple-element.28) | copy-start | bytes 3145732
  22.4 129.4 %copy-start.19 = (bf16[1024,512]{1,0:T(8,128)(2,1)}, bf16[1024,512]{1,0:T(8,128)(2,1)S(1)}, u32[]{:S(2)}) copy-start(bf16[1024,512]{1,0:T(8,128)(2,1)S(1)} %get-tuple-element.30) | copy-start | bytes 3145732
  22.4 133.9 %copy-start.13 = (bf16[1024,512]{1,0:T(8,128)(2,1)}, bf16[1024,512]{1,0:T(8,128)(2,1)S(1)}, u32[]{:S(2)}) copy-start(bf16[1024,512]{1,0:T(8,128)(2,1)S(1)} %get-tuple-element.29) | copy-start | bytes 3145732
  23.2 117.2 %copy-start.9 = (bf16[512,1024]{0,1:T(8,128)(2,1)}, bf16[512,1024]{0,1:T(8,128)(2,1)S(1)}, u32[]{:S(2)}) copy-start(bf16[512,1024]{0,1:T(8,128)(2,1)S(1)} %get-tuple-element.21) | copy-start | bytes 3145732
  23.2 117.2 %copy-start.11 = (bf16[512,1024]{0,1:T(8,128)(2,1)}, bf16[512,1024]{0,1:T(8,128)(2,1)S(1)}, u32[]{:S(2)}) copy-start(bf16[512,1024]{0,1:T(8,128)(2,1)S(1)} %get-tuple-element.22) | copy-start | bytes 3145732
  23.2 126.8 %copy-start.5 = (bf16[512,1024]{0,1:T(8,128)(2,1)}, bf16[512,1024]{0,1:T(8,128)(2,1)S(1)}, u32[]{:S(2)}) copy-start(bf16[512,1024]{0,1:T(8,128)(2,1)S(1)} %get-tuple-element.20) | copy-start | bytes 3145732
  23.2 126.8 %copy-start.7 = (bf16[512,1024]{0,1:T(8,128)(2,1)}, bf16[512,1024]{0,1:T(8,128)(2,1)S(1)}, u32[]{:S(2)}) copy-start(bf16[512,1024]{0,1:T(8,128)(2,1)S(1)} %get-tuple-element.23) | copy-start | bytes 3145732
  24.0 106.4 %copy-start.22 = (bf16[1024,512]{0,1:T(8,128)(2,1)}, bf16[1024,512]{0,1:T(8,128)(2,1)S(1)}, u32[]{:S(2)}) copy-start(bf16[1024,512]{0,1:T(8,128)(2,1)S(1)} %get-tuple-element.54) | copy-start | bytes 3145732
  24.0 106.4 %copy-start.25 = (bf16[1024,512]{0,1:T(8,128)(2,1)}, bf16[1024,512]{0,1:T(8,128)(2,1)S(1)}, u32[]{:S(2)}) copy-start(bf16[1024,512]{0,1:T(8,128)(2,1)S(1)} %get-tuple-element.55) | copy-start | bytes 3145732
  25.0 109.6 %copy-start.40 = (bf16[512,1024]{1,0:T(8,128)(2,1)}, bf16[512,1024]{1,0:T(8,128)(2,1)S(1)}, u32[]{:S(2)}) copy-start(bf16[512,1024]{1,0:T(8,128)(2,1)S(1)} %get-tuple-element.109) | copy-start | bytes 3145732
  25.0 109.6 %copy-start.42 = (bf16[512,1024]{1,0:T(8,128)(2,1)}, bf16[512,1024]{1,0:T(8,128)(2,1)S(1)}, u32[]{:S(2)}) copy-start(bf16[512,1024]{1,0:T(8,128)(2,1)S(1)} %get-tuple-element.110) | copy-start | bytes 3145732
  25.0 111.5 %copy-start.36 = (bf16[512,1024]{1,0:T(8,128)(2,1)}, bf16[512,1024]{1,0:T(8,128)(2,1)S(1)}, u32[]{:S(2)}) copy-start(bf16[512,1024]{1,0:T(8,128)(2,1)S(1)} %get-tuple-element.46) | copy-start | bytes 3145732
  25.0 111.5 %copy-start.38 = (bf16[512,1024]{1,0:T(8,128)(2,1)}, bf16[512,1024]{1,0:T(8,128)(2,1)S(1)}, u32[]{:S(2)}) copy-start(bf16[512,1024]{1,0:T(8,128)(2,1)S(1)} %get-tuple-element.47) | copy-start | bytes 3145732
  25.0 34.1 %collective-permute-start.1 = (f32[128,1024]{1,0:T(8,128)S(1)}, f32[128,1024]{1,0:T(8,128)S(1)}, u32[]{:S(2)}, u32[]{:S(2)}) collective-permute-start(f32[128,1024]{1,0:T(8,128)S(1)} %bitcast_add_fusion.2), channel_id=1, source_target_pairs={{0,1},{3,5},{4,2},{7,6},{8,9},{11,13},{12,10},{15,14},{16,17},{19,... | collective-permute-start | bytes 1572872 | tf_op jit(solution)/shard_map/ppermute | solution.py:166
  26.4 63.8 %collective-permute-start.12 = (f32[256,1024]{1,0:T(8,128)S(1)}, f32[256,1024]{1,0:T(8,128)S(1)}, u32[]{:S(2)}, u32[]{:S(2)}) collective-permute-start(f32[256,1024]{1,0:T(8,128)S(1)} %bitcast.34), channel_id=1, source_target_pairs={{4,0},{8,4},{12,8},{16,12},{20,16},{24,20},{28,24},{5,1},{9,5},{13... | collective-permute-start | bytes 3145736 | tf_op jit(solution)/shard_map/ppermute | solution.py:211
  61.3 4.6 %copy-start.44 = (f32[1024]{0:T(1024)S(1)}, f32[1024]{0:T(1024)}, u32[]{:S(2)}) copy-start(f32[1024]{0:T(1024)} %param.12) | copy-start | bytes 12292
  61.3 8.4 %collective-permute-start.6 = (f32[512,512]{1,0:T(8,128)S(1)}, f32[512,512]{1,0:T(8,128)S(1)}, u32[]{:S(2)}, u32[]{:S(2)}) collective-permute-start(f32[512,512]{1,0:T(8,128)S(1)} %fusion.58), channel_id=1, source_target_pairs={{0,4},{4,0},{8,12},{12,8},{16,20},{20,16},{24,28},{28,24},{1,5},{5... | collective-permute-start | bytes 3145736 | tf_op jit(solution)/shard_map/ppermute | solution.py:163
  65.9 66.5 %copy-start.28 = (bf16[1024,512]{0,1:T(8,128)(2,1)}, bf16[1024,512]{0,1:T(8,128)(2,1)S(1)}, u32[]{:S(2)}) copy-start(bf16[1024,512]{0,1:T(8,128)(2,1)S(1)} %get-tuple-element.52) | copy-start | bytes 3145732
  65.9 66.5 %copy-start.31 = (bf16[1024,512]{0,1:T(8,128)(2,1)}, bf16[1024,512]{0,1:T(8,128)(2,1)S(1)}, u32[]{:S(2)}) copy-start(bf16[1024,512]{0,1:T(8,128)(2,1)S(1)} %get-tuple-element.53) | copy-start | bytes 3145732
  73.7 4.3 %collective-permute-start.7 = (f32[512,512]{1,0:T(8,128)S(1)}, f32[512,512]{1,0:T(8,128)S(1)}, u32[]{:S(2)}, u32[]{:S(2)}) collective-permute-start(f32[512,512]{1,0:T(8,128)S(1)} %fusion.56), channel_id=1, source_target_pairs={{0,4},{4,0},{8,12},{12,8},{16,20},{20,16},{24,28},{28,24},{1,5},{5... | collective-permute-start | bytes 3145736 | tf_op jit(solution)/shard_map/ppermute | solution.py:163
  87.7 12.0 %collective-permute-start.10 = (f32[512,512]{1,0:T(8,128)S(1)}, f32[512,512]{1,0:T(8,128)S(1)}, u32[]{:S(2)}, u32[]{:S(2)}) collective-permute-start(f32[512,512]{1,0:T(8,128)S(1)} %fusion.54), channel_id=1, source_target_pairs={{0,4},{4,0},{8,12},{12,8},{16,20},{20,16},{24,28},{28,24},{1,5},{5... | collective-permute-start | bytes 3145736 | tf_op jit(solution)/shard_map/ppermute | solution.py:163
  88.2 34.0 %collective-permute-start.17 = (f32[256,1024]{1,0:T(8,128)S(1)}, f32[256,1024]{1,0:T(8,128)S(1)}, u32[]{:S(2)}, u32[]{:S(2)}) collective-permute-start(f32[256,1024]{1,0:T(8,128)S(1)} %bitcast.38), channel_id=1, source_target_pairs={{4,0},{8,4},{12,8},{16,12},{20,16},{24,20},{28,24},{5,1},{9,5},{13... | collective-permute-start | bytes 3145736 | tf_op jit(solution)/shard_map/ppermute | solution.py:212
  90.2 21.7 %copy-start.47 = (f32[256,1024]{1,0:T(8,128)}, f32[256,1024]{1,0:T(8,128)S(1)}, u32[]{:S(2)}) copy-start(f32[256,1024]{1,0:T(8,128)S(1)} %collective-permute-done.12) | copy-start | bytes 3145732
  90.2 27.4 %collective-permute-start.13 = (f32[256,1024]{1,0:T(8,128)S(1)}, f32[256,1024]{1,0:T(8,128)S(1)}, u32[]{:S(2)}, u32[]{:S(2)}) collective-permute-start(f32[256,1024]{1,0:T(8,128)S(1)} %collective-permute-done.12), channel_id=1, source_target_pairs={{0,1},{3,5},{4,2},{7,6},{8,9},{11,13},{12,10},{15,14},{16,17},{19,... | collective-permute-start | bytes 3145736 | tf_op jit(solution)/shard_map/ppermute | solution.py:166
  95.1 16.8 %collective-permute-start.14 = (f32[256,1024]{1,0:T(8,128)S(1)}, f32[256,1024]{1,0:T(8,128)S(1)}, u32[]{:S(2)}, u32[]{:S(2)}) collective-permute-start(f32[256,1024]{1,0:T(8,128)S(1)} %collective-permute-done.12), channel_id=1, source_target_pairs={{2,5},{5,2},{10,13},{13,10},{18,21},{21,18},{26,29},{29,26}} | collective-permute-start | bytes 3145736 | tf_op jit(solution)/shard_map/ppermute | solution.py:166
  102.9 61.1 %copy-start.1 = (f32[1024,512]{1,0:T(8,128)}, f32[1024,512]{1,0:T(8,128)S(1)}, u32[]{:S(2)}) copy-start(f32[1024,512]{1,0:T(8,128)S(1)} %get-tuple-element.104) | copy-start | bytes 6291460
  102.9 4.2 %copy-start.53 = (bf16[1024,512]{1,0:T(8,128)(2,1)S(1)}, bf16[1024,512]{1,0:T(8,128)(2,1)}, u32[]{:S(2)}) copy-start(bf16[1024,512]{1,0:T(8,128)(2,1)} %get-tuple-element.43) | copy-start | bytes 3145732
  108.9 2.7 collective-permute-start.11
  121.3 11.0 %collective-permute-start.15 = (f32[512,512]{1,0:T(8,128)S(1)}, f32[512,512]{1,0:T(8,128)S(1)}, u32[]{:S(2)}, u32[]{:S(2)}) collective-permute-start(f32[512,512]{1,0:T(8,128)S(1)} %fusion.50), channel_id=1, source_target_pairs={{0,4},{4,0},{8,12},{12,8},{16,20},{20,16},{24,28},{28,24},{1,5},{5... | collective-permute-start | bytes 3145736 | tf_op jit(solution)/shard_map/ppermute | solution.py:163
  122.2 27.5 %collective-permute-start.18 = (f32[256,1024]{1,0:T(8,128)S(1)}, f32[256,1024]{1,0:T(8,128)S(1)}, u32[]{:S(2)}, u32[]{:S(2)}) collective-permute-start(f32[256,1024]{1,0:T(8,128)S(1)} %collective-permute-done.17), channel_id=1, source_target_pairs={{0,1},{3,5},{4,2},{7,6},{8,9},{11,13},{12,10},{15,14},{16,17},{19,... | collective-permute-start | bytes 3145736 | tf_op jit(solution)/shard_map/ppermute | solution.py:166
  127.9 23.1 %collective-permute-start.19 = (f32[256,1024]{1,0:T(8,128)S(1)}, f32[256,1024]{1,0:T(8,128)S(1)}, u32[]{:S(2)}, u32[]{:S(2)}) collective-permute-start(f32[256,1024]{1,0:T(8,128)S(1)} %collective-permute-done.17), channel_id=1, source_target_pairs={{2,5},{5,2},{10,13},{13,10},{18,21},{21,18},{26,29},{29,26}} | collective-permute-start | bytes 3145736 | tf_op jit(solution)/shard_map/ppermute | solution.py:166
  138.3 3.2 collective-permute-start.16
  154.8 7.8 %collective-permute-start.20 = (f32[512,512]{1,0:T(8,128)}, f32[512,512]{1,0:T(8,128)}, u32[]{:S(2)}, u32[]{:S(2)}) collective-permute-start(f32[512,512]{1,0:T(8,128)} %fusion.46), channel_id=1, source_target_pairs={{0,4},{4,0},{8,12},{12,8},{16,20},{20,16},{24,28},{28,24},{1,5},{5... | collective-permute-start | bytes 3145736 | tf_op jit(solution)/shard_map/ppermute | solution.py:163
  156.3 4.4 %copy-start.23 = (bf16[1024,512]{0,1:T(8,128)(2,1)S(1)}, bf16[1024,512]{0,1:T(8,128)(2,1)}, u32[]{:S(2)}) copy-start(bf16[1024,512]{0,1:T(8,128)(2,1)} %copy-done.22) | copy-start | bytes 3145732
  156.3 4.4 %copy-start.26 = (bf16[1024,512]{0,1:T(8,128)(2,1)S(1)}, bf16[1024,512]{0,1:T(8,128)(2,1)}, u32[]{:S(2)}) copy-start(bf16[1024,512]{0,1:T(8,128)(2,1)} %copy-done.25) | copy-start | bytes 3145732
  160.8 3.2 %copy-start.29 = (bf16[1024,512]{0,1:T(8,128)(2,1)S(1)}, bf16[1024,512]{0,1:T(8,128)(2,1)}, u32[]{:S(2)}) copy-start(bf16[1024,512]{0,1:T(8,128)(2,1)} %copy-done.28) | copy-start | bytes 3145732
  160.8 3.2 %copy-start.32 = (bf16[1024,512]{0,1:T(8,128)(2,1)S(1)}, bf16[1024,512]{0,1:T(8,128)(2,1)}, u32[]{:S(2)}) copy-start(bf16[1024,512]{0,1:T(8,128)(2,1)} %copy-done.31) | copy-start | bytes 3145732
  167.7 27.6 %all-to-all-start = ((f32[8,128,512]{2,1,0:T(8,128)}), f32[8,128,512]{2,1,0:T(8,128)S(1)}, u32[]{:S(2)}, u32[]{:S(2)}) async-start(f32[8,128,512]{2,1,0:T(8,128)} %bitcast.33), calls=%async_computation | async-start | bytes 4194304 | tf_op jit(solution)/shard_map/all_to_all | solution.py:231
  195.5 31.3 %copy-start.2 = (f32[1024,512]{1,0:T(8,128)S(1)}, f32[1024,512]{1,0:T(8,128)}, u32[]{:S(2)}) copy-start(f32[1024,512]{1,0:T(8,128)} %copy-done.1) | copy-start | bytes 6291460
  232.1 3.6 %collective-permute-start.21 = (f32[512,512]{1,0:T(8,128)S(1)}, f32[512,512]{1,0:T(8,128)S(1)}, u32[]{:S(2)}, u32[]{:S(2)}) collective-permute-start(f32[512,512]{1,0:T(8,128)S(1)} %fusion.44), channel_id=1, source_target_pairs={{0,4},{4,0},{8,12},{12,8},{16,20},{20,16},{24,28},{28,24},{1,5},{5... | collective-permute-start | bytes 3145736 | tf_op jit(solution)/shard_map/ppermute | solution.py:163
  242.6 3.5 %copy-start.21 = (f32[256,1024]{1,0:T(8,128)S(1)}, f32[256,1024]{1,0:T(8,128)}, u32[]{:S(2)}) copy-start(f32[256,1024]{1,0:T(8,128)} %get-tuple-element.15) | copy-start | bytes 3145732
  242.6 7.6 %copy-start.14 = (bf16[1024,512]{1,0:T(8,128)(2,1)S(1)}, bf16[1024,512]{1,0:T(8,128)(2,1)}, u32[]{:S(2)}) copy-start(bf16[1024,512]{1,0:T(8,128)(2,1)} %copy-done.13) | copy-start | bytes 3145732
  242.6 7.6 %copy-start.16 = (bf16[1024,512]{1,0:T(8,128)(2,1)S(1)}, bf16[1024,512]{1,0:T(8,128)(2,1)}, u32[]{:S(2)}) copy-start(bf16[1024,512]{1,0:T(8,128)(2,1)} %copy-done.15) | copy-start | bytes 3145732
  244.4 9.4 %collective-permute-start.22 = (f32[512,512]{1,0:T(8,128)S(1)}, f32[512,512]{1,0:T(8,128)S(1)}, u32[]{:S(2)}, u32[]{:S(2)}) collective-permute-start(f32[512,512]{1,0:T(8,128)S(1)} %fusion.42), channel_id=1, source_target_pairs={{0,4},{4,0},{8,12},{12,8},{16,20},{20,16},{24,28},{28,24},{1,5},{5... | collective-permute-start | bytes 3145736 | tf_op jit(solution)/shard_map/ppermute | solution.py:163
  244.5 24.0 %collective-permute-start.27 = (f32[256,1024]{1,0:T(8,128)S(1)}, f32[256,1024]{1,0:T(8,128)}, u32[]{:S(2)}, u32[]{:S(2)}) collective-permute-start(f32[256,1024]{1,0:T(8,128)S(1)} %copy-done.46), channel_id=1, source_target_pairs={{1,0},{5,3}} | collective-permute-start | bytes 3145736 | tf_op jit(solution)/shard_map/ppermute | solution.py:166
  246.1 23.6 %collective-permute-start.26 = (f32[256,1024]{1,0:T(8,128)S(1)}, f32[256,1024]{1,0:T(8,128)}, u32[]{:S(2)}, u32[]{:S(2)}) collective-permute-start(f32[256,1024]{1,0:T(8,128)S(1)} %copy-done.21), channel_id=1, source_target_pairs={{5,2}} | collective-permute-start | bytes 3145736 | tf_op jit(solution)/shard_map/ppermute | solution.py:166
  247.8 23.8 %collective-permute-start.24 = (f32[256,1024]{1,0:T(8,128)S(1)}, f32[256,1024]{1,0:T(8,128)S(1)}, u32[]{:S(2)}, u32[]{:S(2)}) collective-permute-start(f32[256,1024]{1,0:T(8,128)S(1)} %get-tuple-element.14), channel_id=1, source_target_pairs={{5,2},{2,5},{13,10},{10,13},{21,18},{18,21},{29,26},{26,29}} | collective-permute-start | bytes 3145736 | tf_op jit(solution)/shard_map/ppermute | solution.py:166
  248.5 3.5 %copy-start.24 = (bf16[1024,512]{0,1:T(8,128)(2,1)S(1)}, bf16[1024,512]{0,1:T(8,128)(2,1)}, u32[]{:S(2)}) copy-start(bf16[1024,512]{0,1:T(8,128)(2,1)} %copy-done.22) | copy-start | bytes 3145732
  248.5 3.5 %copy-start.27 = (bf16[1024,512]{0,1:T(8,128)(2,1)S(1)}, bf16[1024,512]{0,1:T(8,128)(2,1)}, u32[]{:S(2)}) copy-start(bf16[1024,512]{0,1:T(8,128)(2,1)} %copy-done.25) | copy-start | bytes 3145732
  248.5 28.5 %collective-permute-start.25 = (f32[256,1024]{1,0:T(8,128)}, f32[256,1024]{1,0:T(8,128)}, u32[]{:S(2)}, u32[]{:S(2)}) collective-permute-start(f32[256,1024]{1,0:T(8,128)} %get-tuple-element.108), channel_id=1, source_target_pairs={{1,0},{5,3},{2,4},{6,7},{9,8},{13,11},{10,12},{14,15},{17,16},{21,... | collective-permute-start | bytes 3145736 | tf_op jit(solution)/shard_map/ppermute | solution.py:166
  259.8 2.7 collective-permute-start.23
  264.8 14.7 %collective-permute-start.28 = (f32[256,1024]{1,0:T(8,128)}, f32[256,1024]{1,0:T(8,128)}, u32[]{:S(2)}, u32[]{:S(2)}) collective-permute-start(f32[256,1024]{1,0:T(8,128)} %convolution_add_fusion), channel_id=1, source_target_pairs={{1,5},{5,6},{2,9},{6,10},{9,13},{13,14},{10,17},{14,18},{17,21},{2... | collective-permute-start | bytes 3145736 | tf_op jit(solution)/shard_map/ppermute | solution.py:166
  268.5 53.6 %collective-permute-start.29 = (f32[256,1024]{1,0:T(8,128)}, f32[256,1024]{1,0:T(8,128)}, u32[]{:S(2)}, u32[]{:S(2)}) collective-permute-start(f32[256,1024]{1,0:T(8,128)} %convolution_add_fusion.1), channel_id=1, source_target_pairs={{1,4},{5,7},{2,8},{6,11},{9,12},{13,15},{10,16},{14,19},{17,20},{2... | collective-permute-start | bytes 3145736 | tf_op jit(solution)/shard_map/ppermute | solution.py:166
  (21 other events, 39.1 us)

commit v4 on v3

--- a/solution.py
+++ b/solution.py
@@ -194,10 +194,12 @@
         kept = dot(down_mine, operand(dot(field, right_mine), 0))
         return kept + dot(down_other, operand(arrived, 0))
 
-    def from_eigen(coeffs):
+    def from_eigen(coeffs, whole=False):
         coeffs = operand(coeffs, 0)
         arrived = operand(swap(dot(up_other, coeffs)), 1)
         kept = operand(dot(up_mine, coeffs), 1)
+        if whole:
+            return [dot(kept, back_mine) + dot(arrived, back_other)]
         out = []
         for r in range(plan.rounds):
             rows = slice(r * block, (r + 1) * block)
@@ -220,11 +222,11 @@
 
     relaxed_fine = from_eigen(fine_decay * to_eigen(start))
     coeffs = fine_decay * to_eigen(forced(relaxed_fine, coarse_now))
-    relaxed_coarse = from_eigen(coeffs)
+    relaxed_coarse = from_eigen(coeffs, True)
     first = chain == 0
-    second = to_eigen(forced(relaxed_coarse, fine_next))
-    second = from_eigen(fine_decay * second)
-    ahead = fine_decay * to_eigen(forced(second, coarse_next))
+    second = to_eigen(forced(relaxed_coarse, [jnp.concatenate(fine_next, 0)]))
+    second = from_eigen(fine_decay * second, True)
+    ahead = fine_decay * to_eigen(forced(second, [jnp.concatenate(coarse_next, 0)]))
     term = jnp.where(first, ahead, ahead - coarse_decay * coeffs)
 
     rings = plan.rings()

time: 329 us -> 339 us (1.030)
  starting transfers between devices: 85.2 us -> 98.2 us
  waiting for transfers between devices: 85.1 us -> 81.5 us
    ppermute x16, starting transfers between devices: 30.4 us -> 38.7 us  [sent(): return lax.ppermute(x, both, [(a, b) for a, b in pairs if a != b])]
    ppermute x10, starting transfers between devices: 10.1 us -> 15.1 us  [swap(): return lax.ppermute(x, 'tm', plan.partners())]
    dot_general x50 -> x46, matrix products: 92.6 us -> 94.8 us  [dot(): return jnp.dot(left, right, preferred_element_type=jnp.float32)]
    another operation x21 -> x19, other arithmetic: 8.69 us -> 7.79 us
  transfers between devices with their start and end apart: 31 -> 31, of which waited for: 9 -> 7; matrix products, arithmetic and copies ran while one was open for 28% -> 28% of each run, Pallas kernels for 0% -> 0%
where the time goes in v4:
time: 339 us; the launch traced here: 334 us
  starting transfers between devices  98.2 us (29%)
  matrix products  94.8 us (28%)
  waiting for transfers between devices  81.5 us (24%)
  blocking collectives  31.3 us (9%)
  other arithmetic  17.3 us (5%)
  local copies, waits for them, and re-layouts  8.66 us (3%)
    dot_general x46, matrix products, dot(): return jnp.dot(left, right, preferred_element_type=jnp.float32)  94.8 us
    ppermute x16, waiting for transfers between devices, sent(): return lax.ppermute(x, both, [(a, b) for a, b in pairs if a != b])  56.2 us
    ppermute x16, starting transfers between devices, sent(): return lax.ppermute(x, both, [(a, b) for a, b in pairs if a != b])  38.7 us
    ppermute x1, starting transfers between devices, on_device(): lax.ppermute(source_fine, 'tm', [(g + 1, g) for g in range(groups - 1)])  31.8 us
    all_to_all x1, blocking collectives, on_device(): lax.all_to_all(states, both, 0, 0, axis_index_groups=rings, tiled=True)  31.3 us
    all_to_all x1, waiting for transfers between devices, on_device(): lax.all_to_all(term, both, 0, 0, axis_index_groups=rings, tiled=True)  22 us
    ppermute x10, starting transfers between devices, swap(): return lax.ppermute(x, 'tm', plan.partners())  15.1 us
    another operation x19, other arithmetic  7.79 us
  transfers between devices with their start and end apart: 31, of which 7 were waited for; matrix products, arithmetic and copies ran while one was open for 28% of the time, Pallas kernels for 0%

profile of v4, /device:TPU:25, one launch (start us, length us, event | category | flops | bytes accessed | tf_op | source)
XLA Modules:
  0.0 334.1 jit_solution(5871043594973338201)
XLA Ops:
  0.7 2.4 slice_bitcast_fusion.1
  3.1 3.7 %collective-permute-start = (f32[128,1024]{1,0:T(8,128)}, f32[128,1024]{1,0:T(8,128)S(1)}, u32[]{:S(2)}, u32[]{:S(2)}) collective-permute-start(f32[128,1024]{1,0:T(8,128)} %get-tuple-element.98), channel_id=1, source_target_pairs={{0,4},{4,8},{8,12},{12,16},{16,20},{20,24},{24,28},{1,5},{5,9},{9,... | collective-permute-start | bytes 1572872 | tf_op jit(solution)/shard_map/ppermute | solution.py:134
  6.8 1.9 collective-permute-start.2
  8.7 1.7 collective-permute-start.9
  10.3 3.0 collective-permute-start.8
  15.7 3.1 collective-permute-done.2
  19.6 2.1 collective-permute-start.3
  26.4 31.8 %collective-permute-start.12 = (f32[256,1024]{1,0:T(8,128)S(1)}, f32[256,1024]{1,0:T(8,128)S(1)}, u32[]{:S(2)}, u32[]{:S(2)}) collective-permute-start(f32[256,1024]{1,0:T(8,128)S(1)} %bitcast.34), channel_id=1, source_target_pairs={{4,0},{8,4},{12,8},{16,12},{20,16},{24,20},{28,24},{5,1},{9,5},{13... | collective-permute-start | bytes 3145736 | tf_op jit(solution)/shard_map/ppermute | solution.py:213
  58.7 1.8 fusion.58
  60.5 4.2 %collective-permute-start.6 = (f32[512,512]{1,0:T(8,128)S(1)}, f32[512,512]{1,0:T(8,128)S(1)}, u32[]{:S(2)}, u32[]{:S(2)}) collective-permute-start(f32[512,512]{1,0:T(8,128)S(1)} %fusion.58), channel_id=1, source_target_pairs={{0,4},{4,0},{8,12},{12,8},{16,20},{20,16},{24,28},{28,24},{1,5},{5... | collective-permute-start | bytes 3145736 | tf_op jit(solution)/shard_map/ppermute | solution.py:163
  65.2 1.8 fusion.157
  67.0 1.8 fusion.60
  69.0 2.1 fusion.17
  71.1 1.8 fusion.56
  73.1 1.8 fusion.161
  78.4 3.2 select_add_fusion
  81.6 3.1 add_add_fusion.3
  85.1 1.8 fusion.54
  87.3 2.0 collective-permute-start.17
  89.4 4.6 %collective-permute-start.13 = (f32[256,1024]{1,0:T(8,128)S(1)}, f32[256,1024]{1,0:T(8,128)S(1)}, u32[]{:S(2)}, u32[]{:S(2)}) collective-permute-start(f32[256,1024]{1,0:T(8,128)S(1)} %collective-permute-done.12), channel_id=1, source_target_pairs={{0,1},{3,5},{4,2},{7,6},{8,9},{11,13},{12,10},{15,14},{16,17},{19,... | collective-permute-start | bytes 3145736 | tf_op jit(solution)/shard_map/ppermute | solution.py:166
  94.9 1.8 fusion.165
  96.7 1.8 fusion.72
  98.7 2.1 fusion.27
  100.9 1.8 fusion.52
  103.4 4.6 %fusion.169 = (bf16[512,512]{0,1:T(8,128)(2,1)S(1)}, bf16[512,512]{0,1:T(8,128)(2,1)}) fusion(bf16[1024,512]{1,0:T(8,128)(2,1)} %copy-done.50, bf16[1024,512]{1,0:T(8,128)(2,1)S(1)} %get-tuple-element.42, bf16[512,1024]{1,0:T(8,128)(2,1)S(1)} %get-tuple-element.109, bf16[512,1024]{1,0:T(8,128)(2,1)S(1)} %get-tuple-element.110), kind=kOutput, calls=%fused_computation.278 | convolution fusion | flops 1630797824 | bytes 5242880 | tf_op jit(solution)/shard_map/dot_general | solution.py:65
  108.0 4.4 %fusion.84 = f32[512,1024]{1,0:T(8,128)} fusion(bf16[512,512]{0,1:T(8,128)(2,1)} %get-tuple-element.85, bf16[512,512]{0,1:T(8,128)(2,1)S(1)} %get-tuple-element.84, bf16[512,1024]{0,1:T(8,128)(2,1)S(1)} %get-tuple-element.22, bf16[512,1024]{0,1:T(8,128)(2,1)S(1)} %get-tuple-element.21), kind=kOutput, calls=%fused_computation.155 | convolution fusion | flops 1624768512 | bytes 5242880 | tf_op jit(solution)/shard_map/dot_general | solution.py:65
  112.6 3.6 %collective-permute-done.13 = f32[256,1024]{1,0:T(8,128)S(1)} collective-permute-done((f32[256,1024]{1,0:T(8,128)S(1)}, f32[256,1024]{1,0:T(8,128)S(1)}, u32[]{:S(2)}, u32[]{:S(2)}) %collective-permute-start.13) | collective-permute-done | bytes 1048608 | tf_op jit(solution)/shard_map/ppermute | solution.py:166
  116.2 4.1 %fusion.29 = (bf16[512,1024]{1,0:T(8,128)(2,1)S(1)}, bf16[512,1024]{1,0:T(8,128)(2,1)S(1)}) fusion(f32[256,1024]{1,0:T(8,128)S(1)} %broadcast_select_fusion.1, f32[256,1024]{1,0:T(8,128)S(1)} %collective-permute-done.13, f32[512,1024]{1,0:T(8,128)} %fusion.84, bf16[512,1024]{0,1:T(8,128)(2,1)S(1)} %get-tuple-element.23, ...), kind=kOutput, calls=%fused_computation.86 | convolution fusion | flops 1630011392 | bytes 9437184 | tf_op jit(solution)/shard_map/dot_general | solution.py:65
  120.3 1.8 fusion.50
  124.0 14.3 %collective-permute-start.18 = (f32[256,1024]{1,0:T(8,128)S(1)}, f32[256,1024]{1,0:T(8,128)S(1)}, u32[]{:S(2)}, u32[]{:S(2)}) collective-permute-start(f32[256,1024]{1,0:T(8,128)S(1)} %collective-permute-done.17), channel_id=1, source_target_pairs={{0,1},{3,5},{4,2},{7,6},{8,9},{11,13},{12,10},{15,14},{16,17},{19,... | collective-permute-start | bytes 3145736 | tf_op jit(solution)/shard_map/ppermute | solution.py:166
  138.2 1.8 fusion.173
  140.1 1.8 fusion.96
  142.1 2.1 fusion.31
  144.2 1.8 fusion.48
  146.0 2.7 collective-permute-start.16
  149.0 1.8 fusion.177
  150.8 1.8 fusion.108
  152.9 5.0 %collective-permute-done.18 = f32[256,1024]{1,0:T(8,128)S(1)} collective-permute-done((f32[256,1024]{1,0:T(8,128)S(1)}, f32[256,1024]{1,0:T(8,128)S(1)}, u32[]{:S(2)}, u32[]{:S(2)}) %collective-permute-start.18) | collective-permute-done | bytes 1048608 | tf_op jit(solution)/shard_map/ppermute | solution.py:166
  157.9 2.1 fusion.33
  160.0 2.9 fusion.46
  162.9 3.3 collective-permute-start.20
  166.2 4.4 %fusion.181 = (bf16[512,512]{1,0:T(8,128)(2,1)S(1)}, bf16[512,512]{1,0:T(8,128)(2,1)S(1)}) fusion(bf16[1024,512]{1,0:T(8,128)(2,1)S(1)} %get-tuple-element.29, bf16[1024,512]{1,0:T(8,128)(2,1)} %copy-done.15, bf16[512,1024]{1,0:T(8,128)(2,1)} %copy-done.49, bf16[512,1024]{1,0:T(8,128)(2,1)} %copy-done.48), kind=kOutput, calls=%fused_computation.290 | convolution fusion | flops 1630797824 | bytes 5242880 | tf_op jit(solution)/shard_map/dot_general | solution.py:65
  170.7 1.8 fusion.120
  173.9 3.6 %subtract_select_fusion = f32[1024,512]{1,0:T(8,128)} fusion(f32[1024,512]{1,0:T(8,128)S(1)} %get-tuple-element.104, f32[1024,512]{1,0:T(8,128)S(1)} %fusion.120, f32[512]{0:T(512)S(1)} %dynamic_slice.29, f32[1024]{0:T(1024)S(1)} %copy-done.44, pred[]{:T(512)S(6)} %eq.39, bf16[512,512]{1,0:T(8,128)(2,1)S(1)} %get-tuple-element.71, ...), kind=kOutput, calls=%fused_computation.18 | convolution fusion | flops 1630535680 | bytes 9443329 | tf_op jit(solution)/shard_map/dot_general | solution.py:65
  177.5 5.0 %all-to-all-start = ((f32[8,128,512]{2,1,0:T(8,128)}), f32[8,128,512]{2,1,0:T(8,128)S(1)}, u32[]{:S(2)}, u32[]{:S(2)}) async-start(f32[8,128,512]{2,1,0:T(8,128)} %bitcast.33), calls=%async_computation | async-start | bytes 4194304 | tf_op jit(solution)/shard_map/all_to_all | solution.py:233
  183.7 22.0 %all-to-all-done.terms = f32[8,128,512]{2,1,0:T(8,128)S(1)} async-done(((f32[8,128,512]{2,1,0:T(8,128)}), f32[8,128,512]{2,1,0:T(8,128)S(1)}, u32[]{:S(2)}, u32[]{:S(2)}) %all-to-all-start) | async-done | bytes 2097184 | tf_op jit(solution)/shard_map/all_to_all | solution.py:233
  206.0 31.3 %all_to_all.18 = f32[8,128,512]{2,1,0:T(8,128)S(1)} all-to-all(f32[8,128,512]{2,1,0:T(8,128)S(1)} %scan_along.1), channel_id=1, replica_groups={{1,2,9,10,17,18,25,26},{5,6,13,14,21,22,29,30},{0,4,8,12,16,20,24,28},{..., dimensions={0} | all-to-all | bytes 4194304 | tf_op jit(solution)/shard_map/all_to_all | solution.py:236
  238.9 1.8 fusion.185
  240.7 1.8 fusion.44
  251.8 1.8 fusion.42
  254.4 1.6 collective-permute-start.26
  257.4 2.0 collective-permute-start.24
  259.4 1.8 fusion.189
  261.2 1.8 fusion.132
  263.2 2.1 fusion.39
  265.3 1.8 fusion.193
  267.1 1.8 fusion.40
  272.6 2.0 convolution_add_fusion
  274.6 1.6 collective-permute-start.28
  276.3 2.0 convolution_add_fusion.1
  278.3 8.1 %collective-permute-done.25 = f32[256,1024]{1,0:T(8,128)} collective-permute-done((f32[256,1024]{1,0:T(8,128)S(1)}, f32[256,1024]{1,0:T(8,128)}, u32[]{:S(2)}, u32[]{:S(2)}) %collective-permute-start.25) | collective-permute-done | bytes 1048608 | tf_op jit(solution)/shard_map/ppermute | solution.py:166
  287.7 2.8 select_select_fusion.1
  292.0 39.4 %collective-permute-done.29 = f32[256,1024]{1,0:T(8,128)} collective-permute-done((f32[256,1024]{1,0:T(8,128)}, f32[256,1024]{1,0:T(8,128)}, u32[]{:S(2)}, u32[]{:S(2)}) %collective-permute-start.29) | collective-permute-done | bytes 1048608 | tf_op jit(solution)/shard_map/ppermute | solution.py:166
  331.4 2.5 select_bitcast_fusion
  (188 shorter events, 39.8 us)
Async XLA Ops:
  0.6 18.2 %copy-start.4 = (f32[1,256,1024]{2,1,0:T(8,128)S(1)}, f32[1,256,1024]{2,1,0:T(8,128)}, u32[]{:S(2)}) copy-start(f32[1,256,1024]{2,1,0:T(8,128)} %param.9) | copy-start | bytes 3145732
  0.6 18.2 %copy-start.3 = (f32[256,1024]{1,0:T(8,128)S(1)}, f32[256,1024]{1,0:T(8,128)}, u32[]{:S(2)}) copy-start(f32[256,1024]{1,0:T(8,128)} %param.7) | copy-start | bytes 3145732
  3.1 10.3 %collective-permute-start = (f32[128,1024]{1,0:T(8,128)}, f32[128,1024]{1,0:T(8,128)S(1)}, u32[]{:S(2)}, u32[]{:S(2)}) collective-permute-start(f32[128,1024]{1,0:T(8,128)} %get-tuple-element.98), channel_id=1, source_target_pairs={{0,4},{4,8},{8,12},{12,16},{16,20},{20,24},{24,28},{1,5},{5,9},{9,... | collective-permute-start | bytes 1572872 | tf_op jit(solution)/shard_map/ppermute | solution.py:134
  6.8 12.0 %collective-permute-start.2 = (f32[128,1024]{1,0:T(8,128)}, f32[128,1024]{1,0:T(8,128)S(1)}, u32[]{:S(2)}, u32[]{:S(2)}) collective-permute-start(f32[128,1024]{1,0:T(8,128)} %get-tuple-element.99), channel_id=1, source_target_pairs={{0,4},{4,8},{8,12},{12,16},{16,20},{20,24},{24,28},{1,5},{5,9},{9,... | collective-permute-start | bytes 1572872 | tf_op jit(solution)/shard_map/ppermute | solution.py:134
  8.7 68.8 %collective-permute-start.9 = (f32[256,1024]{1,0:T(8,128)}, f32[256,1024]{1,0:T(8,128)}, u32[]{:S(2)}, u32[]{:S(2)}) collective-permute-start(f32[256,1024]{1,0:T(8,128)} %bitcast.36), channel_id=1, source_target_pairs={{2,5},{5,2},{10,13},{13,10},{18,21},{21,18},{26,29},{29,26}} | collective-permute-start | bytes 3145736 | tf_op jit(solution)/shard_map/ppermute | solution.py:166
  10.3 71.3 %collective-permute-start.8 = (f32[256,1024]{1,0:T(8,128)}, f32[256,1024]{1,0:T(8,128)}, u32[]{:S(2)}, u32[]{:S(2)}) collective-permute-start(f32[256,1024]{1,0:T(8,128)} %bitcast.37), channel_id=1, source_target_pairs={{0,1},{3,5},{4,2},{7,6},{8,9},{11,13},{12,10},{15,14},{16,17},{19,... | collective-permute-start | bytes 3145736 | tf_op jit(solution)/shard_map/ppermute | solution.py:166
  13.4 8.4 %copy-start = (f32[1024,1024]{1,0:T(8,128)S(1)}, f32[1024,1024]{1,0:T(8,128)}, u32[]{:S(2)}) copy-start(f32[1024,1024]{1,0:T(8,128)} %param.11) | copy-start | bytes 12582916
  14.8 11.6 %collective-permute-start.4 = (f32[128,1024]{1,0:T(8,128)S(1)}, f32[128,1024]{1,0:T(8,128)S(1)}, u32[]{:S(2)}, u32[]{:S(2)}) collective-permute-start(f32[128,1024]{1,0:T(8,128)S(1)} %bitcast_add_fusion.2), channel_id=1, source_target_pairs={{2,5},{5,2},{10,13},{13,10},{18,21},{21,18},{26,29},{29,26}} | collective-permute-start | bytes 1572872 | tf_op jit(solution)/shard_map/ppermute | solution.py:166
  18.9 6.1 %collective-permute-start.5 = (f32[128,1024]{1,0:T(8,128)S(1)}, f32[128,1024]{1,0:T(8,128)S(1)}, u32[]{:S(2)}, u32[]{:S(2)}) collective-permute-start(f32[128,1024]{1,0:T(8,128)S(1)} %bitcast_add_fusion.1), channel_id=1, source_target_pairs={{2,5},{5,2},{10,13},{13,10},{18,21},{21,18},{26,29},{29,26}} | collective-permute-start | bytes 1572872 | tf_op jit(solution)/shard_map/ppermute | solution.py:166
  19.6 38.7 %collective-permute-start.3 = (f32[128,1024]{1,0:T(8,128)S(1)}, f32[128,1024]{1,0:T(8,128)S(1)}, u32[]{:S(2)}, u32[]{:S(2)}) collective-permute-start(f32[128,1024]{1,0:T(8,128)S(1)} %bitcast_add_fusion.1), channel_id=1, source_target_pairs={{0,1},{3,5},{4,2},{7,6},{8,9},{11,13},{12,10},{15,14},{16,17},{19,... | collective-permute-start | bytes 1572872 | tf_op jit(solution)/shard_map/ppermute | solution.py:166
  22.4 115.8 %copy-start.15 = (bf16[1024,512]{1,0:T(8,128)(2,1)}, bf16[1024,512]{1,0:T(8,128)(2,1)S(1)}, u32[]{:S(2)}) copy-start(bf16[1024,512]{1,0:T(8,128)(2,1)S(1)} %get-tuple-element.31) | copy-start | bytes 3145732
  22.4 137.6 %copy-start.17 = (bf16[1024,512]{1,0:T(8,128)(2,1)}, bf16[1024,512]{1,0:T(8,128)(2,1)S(1)}, u32[]{:S(2)}) copy-start(bf16[1024,512]{1,0:T(8,128)(2,1)S(1)} %get-tuple-element.28) | copy-start | bytes 3145732
  22.4 137.6 %copy-start.19 = (bf16[1024,512]{1,0:T(8,128)(2,1)}, bf16[1024,512]{1,0:T(8,128)(2,1)S(1)}, u32[]{:S(2)}) copy-start(bf16[1024,512]{1,0:T(8,128)(2,1)S(1)} %get-tuple-element.30) | copy-start | bytes 3145732
  22.5 143.7 %copy-start.13 = (bf16[1024,512]{1,0:T(8,128)(2,1)}, bf16[1024,512]{1,0:T(8,128)(2,1)S(1)}, u32[]{:S(2)}) copy-start(bf16[1024,512]{1,0:T(8,128)(2,1)S(1)} %get-tuple-element.29) | copy-start | bytes 3145732
  23.2 127.6 %copy-start.9 = (bf16[512,1024]{0,1:T(8,128)(2,1)}, bf16[512,1024]{0,1:T(8,128)(2,1)S(1)}, u32[]{:S(2)}) copy-start(bf16[512,1024]{0,1:T(8,128)(2,1)S(1)} %get-tuple-element.21) | copy-start | bytes 3145732
  23.2 127.6 %copy-start.11 = (bf16[512,1024]{0,1:T(8,128)(2,1)}, bf16[512,1024]{0,1:T(8,128)(2,1)S(1)}, u32[]{:S(2)}) copy-start(bf16[512,1024]{0,1:T(8,128)(2,1)S(1)} %get-tuple-element.22) | copy-start | bytes 3145732
  23.2 134.7 %copy-start.5 = (bf16[512,1024]{0,1:T(8,128)(2,1)}, bf16[512,1024]{0,1:T(8,128)(2,1)S(1)}, u32[]{:S(2)}) copy-start(bf16[512,1024]{0,1:T(8,128)(2,1)S(1)} %get-tuple-element.20) | copy-start | bytes 3145732
  23.2 134.7 %copy-start.7 = (bf16[512,1024]{0,1:T(8,128)(2,1)}, bf16[512,1024]{0,1:T(8,128)(2,1)S(1)}, u32[]{:S(2)}) copy-start(bf16[512,1024]{0,1:T(8,128)(2,1)S(1)} %get-tuple-element.23) | copy-start | bytes 3145732
  24.0 116.1 %copy-start.24 = (bf16[1024,512]{0,1:T(8,128)(2,1)}, bf16[1024,512]{0,1:T(8,128)(2,1)S(1)}, u32[]{:S(2)}) copy-start(bf16[1024,512]{0,1:T(8,128)(2,1)S(1)} %get-tuple-element.54) | copy-start | bytes 3145732
  24.0 116.1 %copy-start.27 = (bf16[1024,512]{0,1:T(8,128)(2,1)}, bf16[1024,512]{0,1:T(8,128)(2,1)S(1)}, u32[]{:S(2)}) copy-start(bf16[1024,512]{0,1:T(8,128)(2,1)S(1)} %get-tuple-element.55) | copy-start | bytes 3145732
  25.0 119.2 %copy-start.36 = (bf16[512,1024]{1,0:T(8,128)(2,1)}, bf16[512,1024]{1,0:T(8,128)(2,1)S(1)}, u32[]{:S(2)}) copy-start(bf16[512,1024]{1,0:T(8,128)(2,1)S(1)} %get-tuple-element.46) | copy-start | bytes 3145732
  25.0 119.2 %copy-start.38 = (bf16[512,1024]{1,0:T(8,128)(2,1)}, bf16[512,1024]{1,0:T(8,128)(2,1)S(1)}, u32[]{:S(2)}) copy-start(bf16[512,1024]{1,0:T(8,128)(2,1)S(1)} %get-tuple-element.47) | copy-start | bytes 3145732
  25.0 124.0 %copy-start.40 = (bf16[512,1024]{1,0:T(8,128)(2,1)}, bf16[512,1024]{1,0:T(8,128)(2,1)S(1)}, u32[]{:S(2)}) copy-start(bf16[512,1024]{1,0:T(8,128)(2,1)S(1)} %get-tuple-element.109) | copy-start | bytes 3145732
  25.0 124.0 %copy-start.42 = (bf16[512,1024]{1,0:T(8,128)(2,1)}, bf16[512,1024]{1,0:T(8,128)(2,1)S(1)}, u32[]{:S(2)}) copy-start(bf16[512,1024]{1,0:T(8,128)(2,1)S(1)} %get-tuple-element.110) | copy-start | bytes 3145732
  25.0 33.3 %collective-permute-start.1 = (f32[128,1024]{1,0:T(8,128)S(1)}, f32[128,1024]{1,0:T(8,128)S(1)}, u32[]{:S(2)}, u32[]{:S(2)}) collective-permute-start(f32[128,1024]{1,0:T(8,128)S(1)} %bitcast_add_fusion.2), channel_id=1, source_target_pairs={{0,1},{3,5},{4,2},{7,6},{8,9},{11,13},{12,10},{15,14},{16,17},{19,... | collective-permute-start | bytes 1572872 | tf_op jit(solution)/shard_map/ppermute | solution.py:166
  26.4 62.9 %collective-permute-start.12 = (f32[256,1024]{1,0:T(8,128)S(1)}, f32[256,1024]{1,0:T(8,128)S(1)}, u32[]{:S(2)}, u32[]{:S(2)}) collective-permute-start(f32[256,1024]{1,0:T(8,128)S(1)} %bitcast.34), channel_id=1, source_target_pairs={{4,0},{8,4},{12,8},{16,12},{20,16},{24,20},{28,24},{5,1},{9,5},{13... | collective-permute-start | bytes 3145736 | tf_op jit(solution)/shard_map/ppermute | solution.py:213
  60.5 4.6 %copy-start.44 = (f32[1024]{0:T(1024)S(1)}, f32[1024]{0:T(1024)}, u32[]{:S(2)}) copy-start(f32[1024]{0:T(1024)} %param.12) | copy-start | bytes 12292
  60.5 8.3 %collective-permute-start.6 = (f32[512,512]{1,0:T(8,128)S(1)}, f32[512,512]{1,0:T(8,128)S(1)}, u32[]{:S(2)}, u32[]{:S(2)}) collective-permute-start(f32[512,512]{1,0:T(8,128)S(1)} %fusion.58), channel_id=1, source_target_pairs={{0,4},{4,0},{8,12},{12,8},{16,20},{20,16},{24,28},{28,24},{1,5},{5... | collective-permute-start | bytes 3145736 | tf_op jit(solution)/shard_map/ppermute | solution.py:163
  65.1 77.0 %copy-start.30 = (bf16[1024,512]{0,1:T(8,128)(2,1)}, bf16[1024,512]{0,1:T(8,128)(2,1)S(1)}, u32[]{:S(2)}) copy-start(bf16[1024,512]{0,1:T(8,128)(2,1)S(1)} %get-tuple-element.52) | copy-start | bytes 3145732
  65.1 77.0 %copy-start.33 = (bf16[1024,512]{0,1:T(8,128)(2,1)}, bf16[1024,512]{0,1:T(8,128)(2,1)S(1)}, u32[]{:S(2)}) copy-start(bf16[1024,512]{0,1:T(8,128)(2,1)S(1)} %get-tuple-element.53) | copy-start | bytes 3145732
  72.9 4.3 %collective-permute-start.7 = (f32[512,512]{1,0:T(8,128)S(1)}, f32[512,512]{1,0:T(8,128)S(1)}, u32[]{:S(2)}, u32[]{:S(2)}) collective-permute-start(f32[512,512]{1,0:T(8,128)S(1)} %fusion.56), channel_id=1, source_target_pairs={{0,4},{4,0},{8,12},{12,8},{16,20},{20,16},{24,28},{28,24},{1,5},{5... | collective-permute-start | bytes 3145736 | tf_op jit(solution)/shard_map/ppermute | solution.py:163
  86.9 11.7 %collective-permute-start.10 = (f32[512,512]{1,0:T(8,128)S(1)}, f32[512,512]{1,0:T(8,128)S(1)}, u32[]{:S(2)}, u32[]{:S(2)}) collective-permute-start(f32[512,512]{1,0:T(8,128)S(1)} %fusion.54), channel_id=1, source_target_pairs={{0,4},{4,0},{8,12},{12,8},{16,20},{20,16},{24,28},{28,24},{1,5},{5... | collective-permute-start | bytes 3145736 | tf_op jit(solution)/shard_map/ppermute | solution.py:163
  87.3 35.9 %collective-permute-start.17 = (f32[256,1024]{1,0:T(8,128)S(1)}, f32[256,1024]{1,0:T(8,128)S(1)}, u32[]{:S(2)}, u32[]{:S(2)}) collective-permute-start(f32[256,1024]{1,0:T(8,128)S(1)} %bitcast.38), channel_id=1, source_target_pairs={{4,0},{8,4},{12,8},{16,12},{20,16},{24,20},{28,24},{5,1},{9,5},{13... | collective-permute-start | bytes 3145736 | tf_op jit(solution)/shard_map/ppermute | solution.py:214
  89.4 26.8 %collective-permute-start.13 = (f32[256,1024]{1,0:T(8,128)S(1)}, f32[256,1024]{1,0:T(8,128)S(1)}, u32[]{:S(2)}, u32[]{:S(2)}) collective-permute-start(f32[256,1024]{1,0:T(8,128)S(1)} %collective-permute-done.12), channel_id=1, source_target_pairs={{0,1},{3,5},{4,2},{7,6},{8,9},{11,13},{12,10},{15,14},{16,17},{19,... | collective-permute-start | bytes 3145736 | tf_op jit(solution)/shard_map/ppermute | solution.py:166
  94.0 9.3 %collective-permute-start.14 = (f32[256,1024]{1,0:T(8,128)S(1)}, f32[256,1024]{1,0:T(8,128)S(1)}, u32[]{:S(2)}, u32[]{:S(2)}) collective-permute-start(f32[256,1024]{1,0:T(8,128)S(1)} %collective-permute-done.12), channel_id=1, source_target_pairs={{2,5},{5,2},{10,13},{13,10},{18,21},{21,18},{26,29},{29,26}} | collective-permute-start | bytes 3145736 | tf_op jit(solution)/shard_map/ppermute | solution.py:166
  100.9 73.0 %copy-start.1 = (f32[1024,512]{1,0:T(8,128)}, f32[1024,512]{1,0:T(8,128)S(1)}, u32[]{:S(2)}) copy-start(f32[1024,512]{1,0:T(8,128)S(1)} %get-tuple-element.104) | copy-start | bytes 6291460
  102.7 9.7 %collective-permute-start.11 = (f32[512,512]{1,0:T(8,128)S(1)}, f32[512,512]{1,0:T(8,128)S(1)}, u32[]{:S(2)}, u32[]{:S(2)}) collective-permute-start(f32[512,512]{1,0:T(8,128)S(1)} %fusion.52), channel_id=1, source_target_pairs={{0,4},{4,0},{8,12},{12,8},{16,20},{20,16},{24,28},{28,24},{1,5},{5... | collective-permute-start | bytes 3145736 | tf_op jit(solution)/shard_map/ppermute | solution.py:163
  103.4 12.7 %copy-start.22 = (f32[256,1024]{1,0:T(8,128)}, f32[256,1024]{1,0:T(8,128)S(1)}, u32[]{:S(2)}) copy-start(f32[256,1024]{1,0:T(8,128)S(1)} %broadcast_select_fusion.1) | copy-start | bytes 3145732
  116.2 4.1 %copy-start.46 = (f32[256,1024]{1,0:T(8,128)}, f32[256,1024]{1,0:T(8,128)S(1)}, u32[]{:S(2)}) copy-start(f32[256,1024]{1,0:T(8,128)S(1)} %collective-permute-done.13) | copy-start | bytes 3145732
  122.1 19.8 %collective-permute-start.15 = (f32[512,512]{1,0:T(8,128)S(1)}, f32[512,512]{1,0:T(8,128)S(1)}, u32[]{:S(2)}, u32[]{:S(2)}) collective-permute-start(f32[512,512]{1,0:T(8,128)S(1)} %fusion.50), channel_id=1, source_target_pairs={{0,4},{4,0},{8,12},{12,8},{16,20},{20,16},{24,28},{28,24},{1,5},{5... | collective-permute-start | bytes 3145736 | tf_op jit(solution)/shard_map/ppermute | solution.py:163
  123.2 25.5 %collective-permute-start.19 = (f32[256,1024]{1,0:T(8,128)S(1)}, f32[256,1024]{1,0:T(8,128)S(1)}, u32[]{:S(2)}, u32[]{:S(2)}) collective-permute-start(f32[256,1024]{1,0:T(8,128)S(1)} %collective-permute-done.17), channel_id=1, source_target_pairs={{2,5},{5,2},{10,13},{13,10},{18,21},{21,18},{26,29},{29,26}} | collective-permute-start | bytes 3145736 | tf_op jit(solution)/shard_map/ppermute | solution.py:166
  124.0 33.9 %collective-permute-start.18 = (f32[256,1024]{1,0:T(8,128)S(1)}, f32[256,1024]{1,0:T(8,128)S(1)}, u32[]{:S(2)}, u32[]{:S(2)}) collective-permute-start(f32[256,1024]{1,0:T(8,128)S(1)} %collective-permute-done.17), channel_id=1, source_target_pairs={{0,1},{3,5},{4,2},{7,6},{8,9},{11,13},{12,10},{15,14},{16,17},{19,... | collective-permute-start | bytes 3145736 | tf_op jit(solution)/shard_map/ppermute | solution.py:166
  146.0 6.7 %collective-permute-start.16 = (f32[512,512]{1,0:T(8,128)S(1)}, f32[512,512]{1,0:T(8,128)S(1)}, u32[]{:S(2)}, u32[]{:S(2)}) collective-permute-start(f32[512,512]{1,0:T(8,128)S(1)} %fusion.48), channel_id=1, source_target_pairs={{0,4},{4,0},{8,12},{12,8},{16,20},{20,16},{24,28},{28,24},{1,5},{5... | collective-permute-start | bytes 3145736 | tf_op jit(solution)/shard_map/ppermute | solution.py:163
  162.9 9.6 %collective-permute-start.20 = (f32[512,512]{1,0:T(8,128)}, f32[512,512]{1,0:T(8,128)}, u32[]{:S(2)}, u32[]{:S(2)}) collective-permute-start(f32[512,512]{1,0:T(8,128)} %fusion.46), channel_id=1, source_target_pairs={{0,4},{4,0},{8,12},{12,8},{16,20},{20,16},{24,28},{28,24},{1,5},{5... | collective-permute-start | bytes 3145736 | tf_op jit(solution)/shard_map/ppermute | solution.py:163
  166.2 4.4 %copy-start.25 = (bf16[1024,512]{0,1:T(8,128)(2,1)S(1)}, bf16[1024,512]{0,1:T(8,128)(2,1)}, u32[]{:S(2)}) copy-start(bf16[1024,512]{0,1:T(8,128)(2,1)} %copy-done.24) | copy-start | bytes 3145732
  166.2 4.5 %copy-start.28 = (bf16[1024,512]{0,1:T(8,128)(2,1)S(1)}, bf16[1024,512]{0,1:T(8,128)(2,1)}, u32[]{:S(2)}) copy-start(bf16[1024,512]{0,1:T(8,128)(2,1)} %copy-done.27) | copy-start | bytes 3145732
  170.6 3.2 copy-start.31
  170.6 3.2 copy-start.34
  177.5 28.2 %all-to-all-start = ((f32[8,128,512]{2,1,0:T(8,128)}), f32[8,128,512]{2,1,0:T(8,128)S(1)}, u32[]{:S(2)}, u32[]{:S(2)}) async-start(f32[8,128,512]{2,1,0:T(8,128)} %bitcast.33), calls=%async_computation | async-start | bytes 4194304 | tf_op jit(solution)/shard_map/all_to_all | solution.py:233
  206.0 31.3 %copy-start.2 = (f32[1024,512]{1,0:T(8,128)S(1)}, f32[1024,512]{1,0:T(8,128)}, u32[]{:S(2)}) copy-start(f32[1024,512]{1,0:T(8,128)} %copy-done.1) | copy-start | bytes 6291460
  240.7 3.2 copy-start.10
  242.5 3.6 %collective-permute-start.21 = (f32[512,512]{1,0:T(8,128)S(1)}, f32[512,512]{1,0:T(8,128)S(1)}, u32[]{:S(2)}, u32[]{:S(2)}) collective-permute-start(f32[512,512]{1,0:T(8,128)S(1)} %fusion.44), channel_id=1, source_target_pairs={{0,4},{4,0},{8,12},{12,8},{16,20},{20,16},{24,28},{28,24},{1,5},{5... | collective-permute-start | bytes 3145736 | tf_op jit(solution)/shard_map/ppermute | solution.py:163
  251.8 7.5 %copy-start.14 = (bf16[1024,512]{1,0:T(8,128)(2,1)S(1)}, bf16[1024,512]{1,0:T(8,128)(2,1)}, u32[]{:S(2)}) copy-start(bf16[1024,512]{1,0:T(8,128)(2,1)} %copy-done.13) | copy-start | bytes 3145732
  251.8 7.6 %copy-start.16 = (bf16[1024,512]{1,0:T(8,128)(2,1)S(1)}, bf16[1024,512]{1,0:T(8,128)(2,1)}, u32[]{:S(2)}) copy-start(bf16[1024,512]{1,0:T(8,128)(2,1)} %copy-done.15) | copy-start | bytes 3145732
  253.6 9.4 %collective-permute-start.22 = (f32[512,512]{1,0:T(8,128)S(1)}, f32[512,512]{1,0:T(8,128)S(1)}, u32[]{:S(2)}, u32[]{:S(2)}) collective-permute-start(f32[512,512]{1,0:T(8,128)S(1)} %fusion.42), channel_id=1, source_target_pairs={{0,4},{4,0},{8,12},{12,8},{16,20},{20,16},{24,28},{28,24},{1,5},{5... | collective-permute-start | bytes 3145736 | tf_op jit(solution)/shard_map/ppermute | solution.py:163
  253.7 36.9 %collective-permute-start.27 = (f32[256,1024]{1,0:T(8,128)}, f32[256,1024]{1,0:T(8,128)S(1)}, u32[]{:S(2)}, u32[]{:S(2)}) collective-permute-start(f32[256,1024]{1,0:T(8,128)} %get-tuple-element.103), channel_id=1, source_target_pairs={{1,0},{5,3}} | collective-permute-start | bytes 3145736 | tf_op jit(solution)/shard_map/ppermute | solution.py:166
  254.4 36.1 %collective-permute-start.26 = (f32[256,1024]{1,0:T(8,128)S(1)}, f32[256,1024]{1,0:T(8,128)}, u32[]{:S(2)}, u32[]{:S(2)}) collective-permute-start(f32[256,1024]{1,0:T(8,128)S(1)} %copy-done.21), channel_id=1, source_target_pairs={{5,2}} | collective-permute-start | bytes 3145736 | tf_op jit(solution)/shard_map/ppermute | solution.py:166
  256.0 30.4 %collective-permute-start.25 = (f32[256,1024]{1,0:T(8,128)S(1)}, f32[256,1024]{1,0:T(8,128)}, u32[]{:S(2)}, u32[]{:S(2)}) collective-permute-start(f32[256,1024]{1,0:T(8,128)S(1)} %get-tuple-element.108), channel_id=1, source_target_pairs={{1,0},{5,3},{2,4},{6,7},{9,8},{13,11},{10,12},{14,15},{17,16},{21,... | collective-permute-start | bytes 3145736 | tf_op jit(solution)/shard_map/ppermute | solution.py:166
  257.3 3.8 %copy-start.26 = (bf16[1024,512]{0,1:T(8,128)(2,1)S(1)}, bf16[1024,512]{0,1:T(8,128)(2,1)}, u32[]{:S(2)}) copy-start(bf16[1024,512]{0,1:T(8,128)(2,1)} %copy-done.24) | copy-start | bytes 3145732
  257.3 3.8 %copy-start.29 = (bf16[1024,512]{0,1:T(8,128)(2,1)S(1)}, bf16[1024,512]{0,1:T(8,128)(2,1)}, u32[]{:S(2)}) copy-start(bf16[1024,512]{0,1:T(8,128)(2,1)} %copy-done.27) | copy-start | bytes 3145732
  257.4 30.4 %collective-permute-start.24 = (f32[256,1024]{1,0:T(8,128)S(1)}, f32[256,1024]{1,0:T(8,128)}, u32[]{:S(2)}, u32[]{:S(2)}) collective-permute-start(f32[256,1024]{1,0:T(8,128)S(1)} %get-tuple-element.14), channel_id=1, source_target_pairs={{5,2},{2,5},{13,10},{10,13},{21,18},{18,21},{29,26},{26,29}} | collective-permute-start | bytes 3145736 | tf_op jit(solution)/shard_map/ppermute | solution.py:166
  268.9 3.4 %collective-permute-start.23 = (f32[512,512]{1,0:T(8,128)S(1)}, f32[512,512]{1,0:T(8,128)S(1)}, u32[]{:S(2)}, u32[]{:S(2)}) collective-permute-start(f32[512,512]{1,0:T(8,128)S(1)} %fusion.40), channel_id=1, source_target_pairs={{0,4},{4,0},{8,12},{12,8},{16,20},{20,16},{24,28},{28,24},{1,5},{5... | collective-permute-start | bytes 3145736 | tf_op jit(solution)/shard_map/ppermute | solution.py:163
  274.6 17.4 %collective-permute-start.28 = (f32[256,1024]{1,0:T(8,128)}, f32[256,1024]{1,0:T(8,128)}, u32[]{:S(2)}, u32[]{:S(2)}) collective-permute-start(f32[256,1024]{1,0:T(8,128)} %convolution_add_fusion), channel_id=1, source_target_pairs={{1,5},{5,6},{2,9},{6,10},{9,13},{13,14},{10,17},{14,18},{17,21},{2... | collective-permute-start | bytes 3145736 | tf_op jit(solution)/shard_map/ppermute | solution.py:166
  286.4 45.0 %collective-permute-start.29 = (f32[256,1024]{1,0:T(8,128)}, f32[256,1024]{1,0:T(8,128)}, u32[]{:S(2)}, u32[]{:S(2)}) collective-permute-start(f32[256,1024]{1,0:T(8,128)} %convolution_add_fusion.1), channel_id=1, source_target_pairs={{1,4},{5,7},{2,8},{6,11},{9,12},{13,15},{10,16},{14,19},{17,20},{2... | collective-permute-start | bytes 3145736 | tf_op jit(solution)/shard_map/ppermute | solution.py:166
  (18 other events, 33.8 us)
